TPU v7x, 16 devices: a whole 2x2x2 slice. The times are simulated.
16 devices in a mesh: dp: 2 (over z), sp: 8 (over y, x, core).
Axes of the slice: x: 2, y: 2, z: 2, core: 2. Of those that a mesh axis runs over, the one named last changes fastest.
Arguments:
- hidden: bfloat16 [2, 4096, 1024], P('dp', 'sp')
- positions: int32 [2, 4096], P('dp', 'sp')
- grad_out: bfloat16 [2, 4096, 1024], P('dp', 'sp')
- gain_attn: bfloat16 [1024], P(('dp', 'sp'))
- gain_mlp: bfloat16 [1024], P(('dp', 'sp'))
- w_query: bfloat16 [1024, 2048], P(('dp', 'sp'))
- w_key: bfloat16 [1024, 1024], P(('dp', 'sp'))
- w_value: bfloat16 [1024, 1024], P(('dp', 'sp'))
- w_out: bfloat16 [2048, 1024], P(('dp', 'sp'))
- w_gate: bfloat16 [1024, 3072], P(('dp', 'sp'))
- w_up: bfloat16 [1024, 3072], P(('dp', 'sp'))
- w_down: bfloat16 [3072, 1024], P(('dp', 'sp'))
Outputs:
- output 1: bfloat16 [2, 4096, 1024], P('dp', 'sp')
- output 2: bfloat16 [2, 4096, 1024], P('dp', 'sp')
- output 3: float32 [1024], P(('dp', 'sp'))
- output 4: float32 [1024], P(('dp', 'sp'))
- output 5: float32 [1024, 2048], P(('dp', 'sp'))
- output 6: float32 [1024, 1024], P(('dp', 'sp'))
- output 7: float32 [1024, 1024], P(('dp', 'sp'))
- output 8: float32 [2048, 1024], P(('dp', 'sp'))
- output 9: float32 [1024, 3072], P(('dp', 'sp'))
- output 10: float32 [1024, 3072], P(('dp', 'sp'))
- output 11: float32 [3072, 1024], P(('dp', 'sp'))
All inputs are finite; a program needn't handle non-finite values.
Results may differ from a plain program's by a relative error of at most 0.0153369.
Values are sent between devices in bfloat16 or wider.
A program may use at most 1 GiB of HBM per device.

v0:
```python
import jax
import jax.numpy as jnp
from jax import lax
from jax.sharding import PartitionSpec as P

HEAD_DIM = 128
ROPE_BASE = 10000.0
NORM_EPS = 1e-5
ATTN_SCALE = HEAD_DIM ** -0.5
ALL_AXES = ('dp', 'sp')


def rope_tables(pos_ids):
    inv_freq = ROPE_BASE ** (-(jnp.arange(HEAD_DIM // 2, dtype=jnp.float32) * (2.0 / HEAD_DIM)))
    angles = pos_ids.astype(jnp.float32)[..., None] * inv_freq
    return jnp.cos(angles), jnp.sin(angles)


def apply_rope(values, cos_tab, sin_tab):
    half_dim = values.shape[-1] // 2
    low_half = values[..., :half_dim]
    high_half = values[..., half_dim:]
    cos_wide = cos_tab[..., None, :]
    sin_wide = sin_tab[..., None, :]
    return jnp.concatenate([low_half * cos_wide - high_half * sin_wide, high_half * cos_wide + low_half * sin_wide], axis=-1)


def rope_grad(grads_in, cos_tab, sin_tab):
    half_dim = grads_in.shape[-1] // 2
    low_half = grads_in[..., :half_dim]
    high_half = grads_in[..., half_dim:]
    cos_wide = cos_tab[..., None, :]
    sin_wide = sin_tab[..., None, :]
    return jnp.concatenate([low_half * cos_wide + high_half * sin_wide, high_half * cos_wide - low_half * sin_wide], axis=-1)


def rms_norm(values, gain_vec):
    vals32 = values.astype(jnp.float32)
    inv_rms = lax.rsqrt(jnp.mean(vals32 * vals32, axis=-1, keepdims=True) + NORM_EPS)
    normed = vals32 * inv_rms
    return (normed * gain_vec.astype(jnp.float32)).astype(jnp.bfloat16), normed, inv_rms


def rms_norm_grad(d_out, normed, inv_rms, gain_vec):
    d_normed = d_out * gain_vec.astype(jnp.float32)
    grad_gain = jnp.sum(d_out * normed, axis=0)
    grad_in = inv_rms * (d_normed - normed * jnp.mean(d_normed * normed, axis=-1, keepdims=True))
    return grad_in, grad_gain


def head_probs(q_grp, k_heads):
    seq_len = k_heads.shape[0]
    scores = jnp.einsum('qngd,knd->ngqk', q_grp, k_heads, preferred_element_type=jnp.float32) * ATTN_SCALE
    causal = lax.broadcasted_iota(jnp.int32, (seq_len, seq_len), 0) >= lax.broadcasted_iota(jnp.int32, (seq_len, seq_len), 1)
    scores = jnp.where(causal, scores, -jnp.inf)
    row_max = jnp.max(scores, axis=-1, keepdims=True)
    exp_scores = jnp.exp(scores - row_max)
    return exp_scores / jnp.sum(exp_scores, axis=-1, keepdims=True)


def gather_full(local_shard):
    return lax.all_gather(local_shard, ALL_AXES, axis=0, tiled=True)


def scatter_sum(partial_sum):
    return lax.psum_scatter(partial_sum, ALL_AXES, scatter_dimension=0, tiled=True)


def to_heads(tok_major):
    return lax.all_to_all(tok_major, 'sp', 1, 0, tiled=True)


def to_tokens(head_major):
    return lax.all_to_all(head_major, 'sp', 0, 1, tiled=True)


def dot_tokens(left_op, right_op):
    return lax.dot_general(left_op, right_op, (((0,), (0,)), ((), ())), preferred_element_type=jnp.float32)


def dot_back(left_op, weight):
    return lax.dot_general(left_op, weight, (((1,), (1,)), ((), ())), preferred_element_type=jnp.float32)


def layer_step(hidden, positions, grad_out, gain_attn, gain_mlp, w_query, w_key, w_value, w_out, w_gate, w_up, w_down):
    tokens = hidden[0]
    d_layer = grad_out[0]
    tok_count = tokens.shape[0]
    cos_tab, sin_tab = rope_tables(positions[0])

    gain1_full = gather_full(gain_attn)
    u_attn, normed1, inv_rms1 = rms_norm(tokens, gain1_full)
    wq_full = gather_full(w_query)
    wk_full = gather_full(w_key)
    wv_full = gather_full(w_value)
    num_heads = wq_full.shape[1] // HEAD_DIM
    kv_heads = wk_full.shape[1] // HEAD_DIM
    q_tok = apply_rope(jnp.dot(u_attn, wq_full, preferred_element_type=jnp.float32).reshape(tok_count, num_heads, HEAD_DIM), cos_tab, sin_tab).astype(jnp.bfloat16)
    k_tok = apply_rope(jnp.dot(u_attn, wk_full, preferred_element_type=jnp.float32).reshape(tok_count, kv_heads, HEAD_DIM), cos_tab, sin_tab).astype(jnp.bfloat16)
    v_tok = jnp.dot(u_attn, wv_full, preferred_element_type=jnp.float32).astype(jnp.bfloat16).reshape(tok_count, kv_heads, HEAD_DIM)
    q_heads = to_heads(q_tok)
    k_heads = to_heads(k_tok)
    v_heads = to_heads(v_tok)
    seq_len, kv_local = k_heads.shape[0], k_heads.shape[1]
    q_grp = q_heads.reshape(seq_len, kv_local, num_heads // kv_heads, HEAD_DIM)
    attn_probs = head_probs(q_grp, k_heads)
    probs_bf = attn_probs.astype(jnp.bfloat16)
    o_heads = jnp.einsum('ngqk,knd->qngd', probs_bf, v_heads, preferred_element_type=jnp.float32).astype(jnp.bfloat16).reshape(seq_len, -1, HEAD_DIM)
    attn_out = to_tokens(o_heads).reshape(tok_count, num_heads * HEAD_DIM)
    wo_full = gather_full(w_out)
    residual = (tokens.astype(jnp.float32) + jnp.dot(attn_out, wo_full, preferred_element_type=jnp.float32)).astype(jnp.bfloat16)
    gain2_full = gather_full(gain_mlp)
    u_mlp, normed2, inv_rms2 = rms_norm(residual, gain2_full)
    wg_full = gather_full(w_gate)
    wu_full = gather_full(w_up)
    wd_full = gather_full(w_down)
    gate_pre = jnp.dot(u_mlp, wg_full, preferred_element_type=jnp.float32)
    up_pre = jnp.dot(u_mlp, wu_full, preferred_element_type=jnp.float32)
    sig_gate = jax.nn.sigmoid(gate_pre)
    silu_gate = gate_pre * sig_gate
    mlp_act = (silu_gate * up_pre).astype(jnp.bfloat16)
    layer_out = (residual.astype(jnp.float32) + jnp.dot(mlp_act, wd_full, preferred_element_type=jnp.float32)).astype(jnp.bfloat16)

    wd_back = gather_full(w_down)
    grad_w_down = scatter_sum(dot_tokens(mlp_act, d_layer))
    d_act = dot_back(d_layer, wd_back)
    d_gate = (d_act * up_pre * sig_gate * (1.0 + gate_pre * (1.0 - sig_gate))).astype(jnp.bfloat16)
    d_up = (d_act * silu_gate).astype(jnp.bfloat16)
    grad_w_gate = scatter_sum(dot_tokens(u_mlp, d_gate))
    grad_w_up = scatter_sum(dot_tokens(u_mlp, d_up))
    wg_back = gather_full(w_gate)
    wu_back = gather_full(w_up)
    d_umlp = dot_back(d_gate, wg_back) + dot_back(d_up, wu_back)
    gain2_back = gather_full(gain_mlp)
    d_res_norm, d_gain2 = rms_norm_grad(d_umlp, normed2, inv_rms2, gain2_back)
    grad_gain_mlp = scatter_sum(d_gain2)
    d_resid = d_layer.astype(jnp.float32) + d_res_norm
    d_resid_bf = d_resid.astype(jnp.bfloat16)
    grad_w_out = scatter_sum(dot_tokens(attn_out, d_resid_bf))
    wo_back = gather_full(w_out)
    d_attn = dot_back(d_resid_bf, wo_back).astype(jnp.bfloat16).reshape(tok_count, num_heads, HEAD_DIM)
    d_heads = to_heads(d_attn)
    d_grp = d_heads.reshape(seq_len, kv_local, -1, HEAD_DIM)
    d_probs = jnp.einsum('qngd,knd->ngqk', d_grp, v_heads, preferred_element_type=jnp.float32)
    grad_v = jnp.einsum('ngqk,qngd->knd', probs_bf, d_grp, preferred_element_type=jnp.float32).astype(jnp.bfloat16)
    row_dot = jnp.sum(attn_probs * d_probs, axis=-1, keepdims=True)
    d_scores = (attn_probs * (d_probs - row_dot) * ATTN_SCALE).astype(jnp.bfloat16)
    grad_q = jnp.einsum('ngqk,knd->qngd', d_scores, k_heads, preferred_element_type=jnp.float32).astype(jnp.bfloat16).reshape(seq_len, -1, HEAD_DIM)
    grad_k = jnp.einsum('ngqk,qngd->knd', d_scores, q_grp, preferred_element_type=jnp.float32).astype(jnp.bfloat16)
    dq_tok = to_tokens(grad_q)
    dk_tok = to_tokens(grad_k)
    dv_tok = to_tokens(grad_v).reshape(tok_count, kv_heads * HEAD_DIM)
    dq_pre = rope_grad(dq_tok.astype(jnp.float32), cos_tab, sin_tab).astype(jnp.bfloat16).reshape(tok_count, num_heads * HEAD_DIM)
    dk_pre = rope_grad(dk_tok.astype(jnp.float32), cos_tab, sin_tab).astype(jnp.bfloat16).reshape(tok_count, kv_heads * HEAD_DIM)
    grad_w_query = scatter_sum(dot_tokens(u_attn, dq_pre))
    grad_w_key = scatter_sum(dot_tokens(u_attn, dk_pre))
    grad_w_value = scatter_sum(dot_tokens(u_attn, dv_tok))
    wq_back = gather_full(w_query)
    wk_back = gather_full(w_key)
    wv_back = gather_full(w_value)
    d_uattn = dot_back(dq_pre, wq_back) + dot_back(dk_pre, wk_back) + dot_back(dv_tok, wv_back)
    gain1_back = gather_full(gain_attn)
    d_tok_norm, d_gain1 = rms_norm_grad(d_uattn, normed1, inv_rms1, gain1_back)
    grad_gain_attn = scatter_sum(d_gain1)
    grad_hidden = (d_resid + d_tok_norm).astype(jnp.bfloat16)
    return (layer_out[None], grad_hidden[None], grad_gain_attn, grad_gain_mlp, grad_w_query, grad_w_key, grad_w_value, grad_w_out, grad_w_gate, grad_w_up, grad_w_down)


def solution(mesh):
    act_spec = P('dp', 'sp', None)
    pos_spec = P('dp', 'sp')
    vec_spec = P(ALL_AXES)
    mat_spec = P(ALL_AXES, None)
    in_specs = (act_spec, pos_spec, act_spec, vec_spec, vec_spec) + (mat_spec,) * 7
    out_specs = (act_spec, act_spec, vec_spec, vec_spec) + (mat_spec,) * 7
    return jax.shard_map(layer_step, mesh=mesh, in_specs=in_specs, out_specs=out_specs, check_vma=False)
```

profile of v0, /device:TPU:0, one launch (start us, length us, event | category | flops | bytes accessed | tf_op | source)
XLA Modules:
  0.0 1329.0 jit_solution(1828051625737269534)
XLA Ops:
  13.4 34.9 %all-reduce.5 = (bf16[1024]{0:T(1024)(128)(2,1)S(1)}, bf16[1024]{0:T(1024)(128)(2,1)}) all-reduce(bf16[1024]{0:T(1024)(128)(2,1)S(1)} %dynamic-update-slice, bf16[1024]{0:T(1024)(128)(2,1)S(1)} %dynamic-update-slice.1), channel_id=1, replica_groups=mesh['dp'=2,'sp'=8] {'dp','sp'}, use_global_device_ids=true, to_apply=%add | all-reduce | flops 2048 | bytes 8192
  54.6 3.6 all-to-all-start.1
  58.2 29.4 %all-gather.12.cloned.1.call-done = bf16[1024,2048]{1,0:T(8,128)(2,1)} async-done(((bf16[64,2048]{1,0:T(8,128)(2,1)}), bf16[1024,2048]{1,0:T(8,128)(2,1)}) %all-gather.12.cloned.1.call-update) | async-done | bytes 4194320 | tf_op jit(solution)/shard_map/all_gather | solution.py:62
  87.6 6.4 copy.83
  94.0 4.7 fusion.71
  101.9 3.6 all-to-all-start.2
  105.5 11.0 iota_compare_fusion
  116.5 11.2 all-gather.8.cloned.1.call-done
  135.9 4.5 all-to-all-start
  143.4 53.3 %fusion.6 = (f32[2,4096]{1,0:T(2,128)S(1)}, f32[4096,4096,2]{1,0,2:T(8,128)}) fusion(pred[4096,4096]{0,1:T(8,128)(4,1)} %iota_compare_fusion, bf16[4096,128,1]{1,0,2:T(8,128)(2,1)S(1)} %bitcast.256, bf16[4096,2,128]{2,0,1:T(8,128)(2,1)S(1)} %bitcast.246), kind=kOutput, calls=%fused_computation.10 | convolution fusion | flops 8690589696 | bytes 154173440 | tf_op jit(solution)/shard_map/qngd,knd->ngqk/dot_general | solution.py:53
  196.8 46.2 %fusion.5 = f32[2,4096]{1,0:T(2,128)S(1)} fusion(f32[4096,4096,2]{1,0,2:T(8,128)} %get-tuple-element.33, f32[2,4096]{1,0:T(2,128)S(1)} %get-tuple-element.32, pred[4096,4096]{0,1:T(8,128)(4,1)} %iota_compare_fusion), kind=kLoop, calls=%fused_computation.9 | loop fusion | flops 134209536 | bytes 151060480 | tf_op jit(solution)/shard_map/reduce_sum | solution.py:58
  243.0 53.9 %fusion.17 = bf16[4096,2,128]{0,2,1:T(8,128)(2,1)S(1)} fusion(bf16[4096,128,1]{1,0,2:T(8,128)(2,1)} %bitcast.80, f32[2,4096]{1,0:T(2,128)S(1)} %fusion.5, f32[2,4096]{1,0:T(2,128)S(1)} %get-tuple-element.32, f32[4096,4096,2]{1,0,2:T(8,128)} %get-tuple-element.33, pred[4096,4096]{0,1:T(8,128)(4,1)} %iota_compare_fusion), kind=kOutput, calls=%fused_computation.25 | convolution fusion | flops 8758755328 | bytes 154206208 | tf_op jit(solution)/shard_map/ngqk,knd->qngd/dot_general | solution.py:108
  296.9 3.8 copy.86
  300.7 4.7 all-to-all-start.3
  305.5 26.5 %all-to-all-done.3 = bf16[4096,2,128]{2,1,0:T(2,128)(2,1)S(1)} async-done(((bf16[4096,2,128]{2,1,0:T(2,128)(2,1)}), bf16[4096,2,128]{2,1,0:T(2,128)(2,1)S(1)}, u32[]{:S(2)}, u32[]{:S(2)}) %all-to-all-start.3) | async-done | bytes 2097184 | tf_op jit(solution)/shard_map/all_to_all | solution.py:74
  336.6 6.3 fusion.60
  343.0 9.4 fusion.90
  352.3 8.3 fusion.92
  360.6 11.8 multiply_convert_fusion
  372.5 3.5 fusion.101
  376.0 6.6 fusion.59
  387.7 29.0 %all_to_all.108 = bf16[512,16,128]{2,0,1:T(8,128)(2,1)S(1)} all-to-all(bf16[512,16,128]{2,0,1:T(8,128)(2,1)S(1)} %bitcast.254), channel_id=1, replica_groups=mesh['dp'=2,'sp'=8] {'sp'}, dimensions={1} | all-to-all | bytes 4194304 | tf_op jit(solution)/shard_map/all_to_all | solution.py:70
  418.3 56.0 %fusion.29 = bf16[4096,1,128]{0,2,1:T(8,128)(2,1)S(1)} fusion(bf16[4096,2,128]{2,0,1:T(8,128)(2,1)S(1)} %bitcast.267, f32[2,4096]{1,0:T(2,128)S(1)} %fusion.5, f32[2,4096]{1,0:T(2,128)S(1)} %get-tuple-element.32, f32[4096,4096,2]{1,0,2:T(8,128)} %get-tuple-element.33, pred[4096,4096]{0,1:T(8,128)(4,1)} %iota_compare_fusion), kind=kOutput, calls=%fused_computation.32 | convolution fusion | flops 8758231040 | bytes 154206208 | tf_op jit(solution)/shard_map/ngqk,qngd->knd/dot_general | solution.py:145
  478.1 4.2 all-to-all-start.7
  482.4 101.1 %fusion = (f32[2,4096]{1,0:T(2,128)S(1)}, f32[4096,4096,2]{1,0,2:T(8,128)}) fusion(f32[2,4096]{1,0:T(2,128)S(1)} %fusion.5, f32[2,4096]{1,0:T(2,128)S(1)} %get-tuple-element.32, f32[4096,4096,2]{1,0,2:T(8,128)} %get-tuple-element.33, pred[4096,4096]{0,1:T(8,128)(4,1)} %iota_compare_fusion, bf16[4096,128,1]{1,0,2:T(8,128)(2,1)} %bitcast.80, ...), kind=kOutput, calls=%fused_computation.3 | convolution fusion | flops 8791252992 | bytes 288456704 | tf_op jit(solution)/shard_map/qngd,knd->ngqk/dot_general | solution.py:144
  583.5 4.3 reshape.318
  589.2 3.6 fusion.77
  592.9 110.3 %fusion.7 = bf16[2,4096,4096]{1,2,0:T(8,128)(2,1)} fusion(f32[4096,4096,2]{1,0,2:T(8,128)} %get-tuple-element.38, f32[2,4096]{1,0:T(2,128)S(1)} %get-tuple-element.37, f32[2,4096]{1,0:T(2,128)S(1)} %fusion.5, f32[2,4096]{1,0:T(2,128)S(1)} %get-tuple-element.32, f32[4096,4096,2]{1,0,2:T(8,128)} %get-tuple-element.33, pred[4096,4096]{0,1:T(8,128)(4,1)} %iota_compare_fusion), kind=kLoop, calls=%fused_computation.11 | loop fusion | flops 268435456 | bytes 352419840 | tf_op jit(solution)/shard_map/reshape.28
  703.2 28.2 %fusion.28 = bf16[4096,1,128]{0,2,1:T(8,128)(2,1)S(1)} fusion(bf16[4096,2,128]{2,0,1:T(8,128)(2,1)S(1)} %bitcast.247, bf16[2,4096,4096]{1,2,0:T(8,128)(2,1)} %fusion.7), kind=kOutput, calls=%fused_computation.31 | convolution fusion | flops 8590458880 | bytes 70254592 | tf_op jit(solution)/shard_map/ngqk,qngd->knd/dot_general | solution.py:149
  733.8 19.4 %all_to_all.109 = bf16[8,2,32768]{2,1,0:T(2,128)(2,1)S(1)} all-to-all(bf16[8,2,32768]{2,1,0:T(2,128)(2,1)S(1)} %reshape.319), channel_id=1, replica_groups=mesh['dp'=2,'sp'=8] {'sp'}, dimensions={0} | all-to-all | bytes 2097152 | tf_op jit(solution)/shard_map/all_to_all | solution.py:74
  756.7 3.5 fusion.79
  761.8 7.2 fusion.83
  770.2 8.3 fusion.67
  779.8 8.5 fusion.86
  788.3 8.5 fusion.88
  798.1 23.2 %fusion.20 = bf16[4096,2,128]{0,2,1:T(8,128)(2,1)S(1)} fusion(bf16[4096,128,1]{1,0,2:T(8,128)(2,1)S(1)} %bitcast.257, bf16[2,4096,4096]{1,2,0:T(8,128)(2,1)} %fusion.7), kind=kOutput, calls=%fused_computation.27 | convolution fusion | flops 8590983168 | bytes 70254592 | tf_op jit(solution)/shard_map/ngqk,knd->qngd/dot_general | solution.py:148
  821.3 3.8 copy.94
  825.1 52.9 %all_to_all.110 = bf16[4096,2,128]{2,1,0:T(2,128)(2,1)S(1)} all-to-all(bf16[4096,2,128]{2,1,0:T(2,128)(2,1)} %copy.94), channel_id=1, replica_groups=mesh['dp'=2,'sp'=8] {'sp'}, dimensions={0} | all-to-all | bytes 4194304 | tf_op jit(solution)/shard_map/all_to_all | solution.py:74
  878.0 4.2 copy.95
  886.7 6.0 fusion.75
  893.9 8.3 fusion.64
  906.9 4.2 fusion.49
  911.1 32.2 %all-reduce.4 = (f32[1024]{0:T(1024)S(1)}, f32[1024]{0:T(1024)S(1)}) all-reduce(f32[1024]{0:T(1024)S(1)} %get-tuple-element.13, f32[1024]{0:T(1024)S(1)} %copy-done.42), channel_id=2, replica_groups=mesh['dp'=2,'sp'=8] {'dp','sp'}, use_global_device_ids=true, to_apply=%region_8.9.clone | all-reduce | flops 2048 | bytes 16384
  944.5 3.1 fusion.65
  947.6 87.8 %reduce-scatter.20.cloned.1.call-done = f32[192,1024]{1,0:T(8,128)} async-done(((f32[3072,1024]{1,0:T(8,128)}), f32[192,1024]{1,0:T(8,128)}) %reduce-scatter.20.cloned.1.call-update) | async-done | bytes 786448 | tf_op jit(solution)/shard_map/reduce_scatter | solution.py:66
  1035.4 95.5 %reduce-scatter.18.cloned.1.call-done = f32[64,3072]{1,0:T(8,128)} async-done(((f32[1024,3072]{1,0:T(8,128)}), f32[64,3072]{1,0:T(8,128)}) %reduce-scatter.18.cloned.1.call-update) | async-done | bytes 786448 | tf_op jit(solution)/shard_map/reduce_scatter | solution.py:66
  1130.9 95.7 %reduce-scatter.16.cloned.1.call-done = f32[64,3072]{1,0:T(8,128)} async-done(((f32[1024,3072]{1,0:T(8,128)}), f32[64,3072]{1,0:T(8,128)}) %reduce-scatter.16.cloned.1.call-update) | async-done | bytes 786448 | tf_op jit(solution)/shard_map/reduce_scatter | solution.py:66
  1226.6 95.5 %reduce-scatter.8.cloned.1.call-done = f32[64,2048]{1,0:T(8,128)} async-done(((f32[1024,2048]{1,0:T(8,128)}), f32[64,2048]{1,0:T(8,128)}) %reduce-scatter.8.cloned.1.call-update) | async-done | bytes 524304 | tf_op jit(solution)/shard_map/reduce_scatter | solution.py:66
  (192 shorter events, 65.9 us)
Async XLA Ops:
  7.2 5.5 copy-start.11
  7.2 5.8 copy-start.47
  7.2 6.0 copy-start.48
  7.2 41.7 %all-gather.10.cloned.1.call-start = ((), (), s32[]{:S(2)}) async-start(), calls=%async_computation.16 | async-start | bytes 2228224 | tf_op jit(solution)/shard_map/all_gather | solution.py:62
  7.9 79.6 %all-gather.12.cloned.1.call-start = ((), (), s32[]{:S(2)}) async-start(), calls=%async_computation.17 | async-start | bytes 4456448 | tf_op jit(solution)/shard_map/all_gather | solution.py:62
  8.7 119.0 %all-gather.8.cloned.1.call-start = ((), (), s32[]{:S(2)}) async-start(), calls=%async_computation.15 | async-start | bytes 2228224 | tf_op jit(solution)/shard_map/all_gather | solution.py:62
  9.4 327.2 %all-gather.14.cloned.1.call-start = ((), (), s32[]{:S(2)}) async-start(), calls=%async_computation.18 | async-start | bytes 4456448 | tf_op jit(solution)/shard_map/all_gather | solution.py:62
  10.0 333.0 %all-gather.18.cloned.1.call-start = ((), (), s32[]{:S(2)}) async-start(), calls=%async_computation.20 | async-start | bytes 6684672 | tf_op jit(solution)/shard_map/all_gather | solution.py:62
  10.6 341.7 %all-gather.16.cloned.1.call-start = ((), (), s32[]{:S(2)}) async-start(), calls=%async_computation.19 | async-start | bytes 6684672 | tf_op jit(solution)/shard_map/all_gather | solution.py:62
  11.2 349.5 %all-gather.20.cloned.1.call-start = ((), (), s32[]{:S(2)}) async-start(), calls=%async_computation.21 | async-start | bytes 6684672 | tf_op jit(solution)/shard_map/all_gather | solution.py:62
  12.9 114.8 %copy-start.38 = (f32[512]{0:T(512)}, f32[512]{0:T(512)S(1)}, u32[]{:S(2)}) copy-start(f32[512]{0:T(512)S(1)} %add_rsqrt_fusion.1) | copy-start | bytes 6148
  48.3 79.4 %copy-start.34 = (f32[1024]{0:T(1024)}, f32[1024]{0:T(1024)S(1)}, u32[]{:S(2)}) copy-start(f32[1024]{0:T(1024)S(1)} %convert_element_type.179) | copy-start | bytes 12292
  48.9 49.8 %copy-start.17 = (f32[512,64]{0,1:T(8,128)}, f32[512,64]{0,1:T(8,128)S(1)}, u32[]{:S(2)}) copy-start(f32[512,64]{0,1:T(8,128)S(1)} %get-tuple-element.30) | copy-start | bytes 393220
  48.9 49.8 %copy-start.19 = (f32[512,64]{0,1:T(8,128)}, f32[512,64]{0,1:T(8,128)S(1)}, u32[]{:S(2)}) copy-start(f32[512,64]{0,1:T(8,128)S(1)} %get-tuple-element.31) | copy-start | bytes 393220
  54.6 46.3 %all-to-all-start.1 = ((bf16[512,8,128]{0,2,1:T(8,128)(2,1)}), bf16[512,8,128]{0,2,1:T(8,128)(2,1)S(1)}, u32[]{:S(2)}, u32[]{:S(2)}) async-start(bf16[512,8,128]{0,2,1:T(8,128)(2,1)} %pad_maximum_fusion.1), calls=%async_computation.1 | async-start | bytes 2097152 | tf_op jit(solution)/shard_map/all_to_all | solution.py:70
  101.9 34.0 %all-to-all-start.2 = ((bf16[512,16,128]{0,2,1:T(8,128)(2,1)}), bf16[512,16,128]{0,2,1:T(8,128)(2,1)S(1)}, u32[]{:S(2)}, u32[]{:S(2)}) async-start(bf16[512,16,128]{0,2,1:T(8,128)(2,1)} %pad_maximum_fusion), calls=%async_computation.2 | async-start | bytes 4194304 | tf_op jit(solution)/shard_map/all_to_all | solution.py:70
  105.5 22.2 %copy-start.12 = (bf16[1,512,1024]{2,1,0:T(8,128)(2,1)S(1)}, bf16[1,512,1024]{2,1,0:T(8,128)(2,1)}, u32[]{:S(2)}) copy-start(bf16[1,512,1024]{2,1,0:T(8,128)(2,1)} %param.12) | copy-start | bytes 3145732
  133.4 63.3 %copy-start.7 = (bf16[8,512,1,128]{3,1,0,2:T(8,128)(2,1)}, bf16[8,512,1,128]{3,1,0,2:T(8,128)(2,1)S(1)}, u32[]{:S(2)}) copy-start(bf16[8,512,1,128]{3,1,0,2:T(8,128)(2,1)S(1)} %copy.82) | copy-start | bytes 3145732
  135.9 4.5 copy-start.6
  135.9 107.1 %all-to-all-start = ((bf16[512,8,128]{2,0,1:T(8,128)(2,1)}), bf16[512,8,128]{2,0,1:T(8,128)(2,1)}, u32[]{:S(2)}, u32[]{:S(2)}) async-start(bf16[512,8,128]{2,0,1:T(8,128)(2,1)} %bitcast.263), calls=%async_computation | async-start | bytes 2097152 | tf_op jit(solution)/shard_map/all_to_all | solution.py:70
  143.4 53.4 %copy-start.3 = (bf16[8,512,2,128]{3,1,0,2:T(8,128)(2,1)}, bf16[8,512,2,128]{3,1,0,2:T(8,128)(2,1)S(1)}, u32[]{:S(2)}) copy-start(bf16[8,512,2,128]{3,1,0,2:T(8,128)(2,1)S(1)} %copy.84) | copy-start | bytes 6291460
  300.7 4.7 copy-start.43
  300.7 31.3 %all-to-all-start.3 = ((bf16[4096,2,128]{2,1,0:T(2,128)(2,1)}), bf16[4096,2,128]{2,1,0:T(2,128)(2,1)S(1)}, u32[]{:S(2)}, u32[]{:S(2)}) async-start(bf16[4096,2,128]{2,1,0:T(2,128)(2,1)} %copy.86), calls=%async_computation.3 | async-start | bytes 4194304 | tf_op jit(solution)/shard_map/all_to_all | solution.py:74
  305.5 77.1 %copy-start.36 = (f32[1024]{0:T(1024)}, f32[1024]{0:T(1024)S(1)}, u32[]{:S(2)}) copy-start(f32[1024]{0:T(1024)S(1)} %convert_element_type.193) | copy-start | bytes 12292
  333.6 3.0 copy-start.13
  336.6 6.3 copy-start.5
  342.9 39.6 %copy-start.40 = (f32[512]{0:T(512)}, f32[512]{0:T(512)S(1)}, u32[]{:S(2)}) copy-start(f32[512]{0:T(512)S(1)} %add_rsqrt_fusion) | copy-start | bytes 6148
  343.0 9.4 copy-start.31
  352.3 8.3 copy-start.29
  360.6 11.8 copy-start.44
  372.5 3.5 copy-start.49
  372.5 3.5 copy-start.50
  384.7 2.4 copy-start
  478.1 105.4 %all-to-all-start.7 = ((bf16[8,2,32768]{2,1,0:T(2,128)(2,1)}), bf16[8,2,32768]{2,1,0:T(2,128)(2,1)}, u32[]{:S(2)}, u32[]{:S(2)}) async-start(bf16[8,2,32768]{2,1,0:T(2,128)(2,1)} %reshape.317), calls=%async_computation.7 | async-start | bytes 2097152 | tf_op jit(solution)/shard_map/all_to_all | solution.py:74
  482.3 465.3 %reduce-scatter.12.cloned.1.call-start = ((), (), s32[]{:S(2)}) async-start(), calls=%async_computation.24 | async-start | bytes 4456448 | tf_op jit(solution)/shard_map/reduce_scatter | solution.py:66
  588.5 4.3 copy-start.25
  592.9 354.7 %reduce-scatter.10.cloned.1.call-start = ((), (), s32[]{:S(2)}) async-start(), calls=%async_computation.23 | async-start | bytes 4456448 | tf_op jit(solution)/shard_map/reduce_scatter | solution.py:66
  592.9 110.3 %copy-start.4 = (bf16[8,512,2,128]{3,1,0,2:T(8,128)(2,1)S(1)}, bf16[8,512,2,128]{3,1,0,2:T(8,128)(2,1)}, u32[]{:S(2)}) copy-start(bf16[8,512,2,128]{3,1,0,2:T(8,128)(2,1)} %copy-done.3) | copy-start | bytes 6291460
  760.3 187.4 %reduce-scatter.14.cloned.1.call-start = ((), (), s32[]{:S(2)}) async-start(), calls=%async_computation.25 | async-start | bytes 8912896 | tf_op jit(solution)/shard_map/reduce_scatter | solution.py:66
  769.0 266.4 %reduce-scatter.20.cloned.1.call-start = ((), (), s32[]{:S(2)}) async-start(), calls=%async_computation.28 | async-start | bytes 13369344 | tf_op jit(solution)/shard_map/reduce_scatter | solution.py:66
  778.6 352.4 %reduce-scatter.18.cloned.1.call-start = ((), (), s32[]{:S(2)}) async-start(), calls=%async_computation.27 | async-start | bytes 13369344 | tf_op jit(solution)/shard_map/reduce_scatter | solution.py:66
  788.3 438.3 %reduce-scatter.16.cloned.1.call-start = ((), (), s32[]{:S(2)}) async-start(), calls=%async_computation.26 | async-start | bytes 13369344 | tf_op jit(solution)/shard_map/reduce_scatter | solution.py:66
  796.9 525.2 %reduce-scatter.8.cloned.1.call-start = ((), (), s32[]{:S(2)}) async-start(), calls=%async_computation.22 | async-start | bytes 8912896 | tf_op jit(solution)/shard_map/reduce_scatter | solution.py:66
  893.9 8.3 copy-start.26
  893.9 8.3 copy-start.46
  904.0 2.9 copy-start.23
  906.9 4.2 copy-start.42
  906.9 37.6 %copy-start.2 = (f32[512,1024]{1,0:T(8,128)S(1)}, f32[512,1024]{1,0:T(8,128)}, u32[]{:S(2)}) copy-start(f32[512,1024]{1,0:T(8,128)} %copy-done) | copy-start | bytes 6291460
  (22 other events, 29.0 us)
Sparse Core Ops, SparseCore 0:
  10.3 31.5 all-gather.9
  44.1 43.4 all-gather.11
  89.8 37.8 all-gather.7
  129.8 41.5 all-gather.13
  173.5 41.7 all-gather.17
  217.4 41.7 all-gather.15
  261.5 41.7 all-gather.19
  593.0 64.7 reduce-scatter.11
  760.4 62.4 reduce-scatter.9
  825.6 115.9 reduce-scatter.13
  946.8 88.6 reduce-scatter.19
  1040.5 90.4 reduce-scatter.17
  1136.1 90.4 reduce-scatter.15
  1229.3 92.7 reduce-scatter.7
where the time goes:
time: 1340 us; the launch traced here: 1330 us
  waiting for transfers between devices  449 us (34%)
  matrix products  434 us (32%)
  other arithmetic  183 us (14%)
  blocking collectives  168 us (13%)
  local copies, waits for them, and re-layouts  59.4 us (4%)
  starting transfers between devices  21.2 us (2%)
  between operations  15.1 us (1%)
    reduce_scatter x7, waiting for transfers between devices, scatter_sum(): lax.psum_scatter(partial_sum, ALL_AXES, scatter_dimension=0, tiled=True)  374 us
    another operation x3, other arithmetic  111 us
    dot_general x1, matrix products, layer_step(): jnp.einsum('qngd,knd->ngqk', d_grp, v_heads, preferred_element_type=jnp.f...  101 us
    all_to_all x2, blocking collectives, to_tokens(): return lax.all_to_all(head_major, 'sp', 0, 1, tiled=True)  72.3 us
    unnamed x2, blocking collectives  67.1 us
    dot_general x1, matrix products, layer_step(): jnp.einsum('ngqk,qngd->knd', probs_bf, d_grp, preferred_element_type=jnp....  56 us
    dot_general x1, matrix products, layer_step(): jnp.einsum('ngqk,knd->qngd', probs_bf, v_heads, preferred_element_type=jn...  53.9 us
    dot_general x1, matrix products, head_probs(): jnp.einsum('qngd,knd->ngqk', q_grp, k_heads, preferred_element_type=jnp.f...  53.3 us
  transfers between devices with their start and end apart: 19, of which 8 were waited for; matrix products, arithmetic and copies ran while one was open for 43% of the time, Pallas kernels for 0%

commit v1 on v0

--- a/solution.py
+++ b/solution.py
@@ -1,6 +1,11 @@
+import functools
+import math
+
 import jax
 import jax.numpy as jnp
 from jax import lax
+from jax.experimental import pallas as pl
+from jax.experimental.pallas import tpu as pltpu
 from jax.sharding import PartitionSpec as P
 
 HEAD_DIM = 128
@@ -48,14 +53,140 @@
     return grad_in, grad_gain
 
 
-def head_probs(q_grp, k_heads):
-    seq_len = k_heads.shape[0]
-    scores = jnp.einsum('qngd,knd->ngqk', q_grp, k_heads, preferred_element_type=jnp.float32) * ATTN_SCALE
-    causal = lax.broadcasted_iota(jnp.int32, (seq_len, seq_len), 0) >= lax.broadcasted_iota(jnp.int32, (seq_len, seq_len), 1)
-    scores = jnp.where(causal, scores, -jnp.inf)
-    row_max = jnp.max(scores, axis=-1, keepdims=True)
-    exp_scores = jnp.exp(scores - row_max)
-    return exp_scores / jnp.sum(exp_scores, axis=-1, keepdims=True)
+LOG2E = math.log2(math.e)
+SCALE2 = ATTN_SCALE * LOG2E
+NT = (((1,), (1,)), ((), ()))
+NN = (((1,), (0,)), ((), ()))
+BIG = -1e30
+
+
+def fwd_kernel(bq, bk, q_ref, k_ref, vt_ref, o_ref, lse_ref):
+    i = pl.program_id(0)
+    heads = q_ref.shape[1] // HEAD_DIM
+    qs = [q_ref[:, h * HEAD_DIM:(h + 1) * HEAD_DIM] for h in range(heads)]
+
+    def block(j, carry, masked):
+        rows = pl.ds(pl.multiple_of(j * bk, bk), bk)
+        k = k_ref[rows, :]
+        vt = vt_ref[:, rows]
+        out = []
+        for h in range(heads):
+            m, l, acc = carry[h]
+            s = lax.dot_general(k, qs[h], NT, preferred_element_type=jnp.float32)
+            if masked:
+                kpos = j * bk + lax.broadcasted_iota(jnp.int32, (bk, bq), 0)
+                qpos = i * bq + lax.broadcasted_iota(jnp.int32, (bk, bq), 1)
+                s = jnp.where(qpos >= kpos, s, BIG)
+            m_new = jnp.maximum(m, jnp.max(s, axis=0, keepdims=True))
+            p = jnp.exp2((s - m_new) * SCALE2)
+            alpha = jnp.exp2((m - m_new) * SCALE2)
+            l = l * alpha + jnp.sum(p, axis=0, keepdims=True)
+            acc = acc * alpha + lax.dot_general(vt, p.astype(jnp.bfloat16), NN, preferred_element_type=jnp.float32)
+            out.append((m_new, l, acc))
+        return tuple(out)
+
+    init = tuple((jnp.full((1, bq), BIG, jnp.float32), jnp.zeros((1, bq), jnp.float32), jnp.zeros((HEAD_DIM, bq), jnp.float32)) for _ in range(heads))
+    full = i * bq // bk
+    carry = lax.fori_loop(0, full, lambda j, c: block(j, c, False), init)
+    for d in range(max(1, bq // bk)):
+        carry = block(full + d, carry, True)
+    for h in range(heads):
+        m, l, acc = carry[h]
+        o = acc / l
+        o_ref[:, h * HEAD_DIM:(h + 1) * HEAD_DIM] = o.T.astype(jnp.bfloat16)
+        lse_ref[h:h + 1, :] = m * SCALE2 + jnp.log2(l)
+
+
+def flash_fwd(q, k, vt, bq=512, bk=512):
+    seq, width = q.shape
+    heads = width // HEAD_DIM
+    return pl.pallas_call(
+        functools.partial(fwd_kernel, bq, bk),
+        grid=(seq // bq,),
+        in_specs=[pl.BlockSpec((bq, width), lambda i: (i, 0)),
+                  pl.BlockSpec((seq, HEAD_DIM), lambda i: (0, 0)),
+                  pl.BlockSpec((HEAD_DIM, seq), lambda i: (0, 0))],
+        out_specs=[pl.BlockSpec((bq, width), lambda i: (i, 0)),
+                   pl.BlockSpec((heads, bq), lambda i: (0, i))],
+        out_shape=[jax.ShapeDtypeStruct((seq, width), jnp.bfloat16), jax.ShapeDtypeStruct((heads, seq), jnp.float32)],
+        cost_estimate=pl.CostEstimate(flops=2 * seq * seq * width * 2, bytes_accessed=8 << 20, transcendentals=seq * seq),
+        compiler_params=pltpu.CompilerParams(vmem_limit_bytes=56 << 20),
+        name="flash_fwd",
+    )(q, k, vt)
+
+
+def bwd_kernel(bq, bk, q_ref, d_ref, k_ref, kt_ref, v_ref, lse_ref, rd_ref, dq_ref, dk_ref, dv_ref, dqt, dka, dva):
+    j = pl.program_id(0)
+    nk = pl.num_programs(0)
+    seq, width = q_ref.shape
+    heads = width // HEAD_DIM
+    nq = seq // bq
+    k = k_ref[...]
+    v = v_ref[...]
+    kt = kt_ref[...]
+
+    @pl.when(j == 0)
+    def _():
+        dqt[...] = jnp.zeros_like(dqt)
+
+    dka[...] = jnp.zeros_like(dka)
+    dva[...] = jnp.zeros_like(dva)
+
+    def block(i, masked):
+        rows = pl.ds(pl.multiple_of(i * bq, bq), bq)
+        for h in range(heads):
+            cols = slice(h * HEAD_DIM, (h + 1) * HEAD_DIM)
+            q = q_ref[rows, cols]
+            d = d_ref[rows, cols]
+            s = lax.dot_general(k, q, NT, preferred_element_type=jnp.float32)
+            dp = lax.dot_general(v, d, NT, preferred_element_type=jnp.float32)
+            p = jnp.exp2(s * SCALE2 - lse_ref[h:h + 1, rows])
+            if masked:
+                kpos = j * bk + lax.broadcasted_iota(jnp.int32, (bk, bq), 0)
+                qpos = i * bq + lax.broadcasted_iota(jnp.int32, (bk, bq), 1)
+                p = jnp.where(qpos >= kpos, p, 0.0)
+            ds = (p * (dp - rd_ref[h:h + 1, rows]) * ATTN_SCALE).astype(jnp.bfloat16)
+            dva[...] += lax.dot_general(p.astype(jnp.bfloat16), d, NN, preferred_element_type=jnp.float32)
+            dka[...] += lax.dot_general(ds, q, NN, preferred_element_type=jnp.float32)
+            dqt[cols, rows] += lax.dot_general(kt, ds, NN, preferred_element_type=jnp.float32)
+
+    first = j * bk // bq
+    ndiag = max(1, bk // bq)
+    for t in range(ndiag):
+        block(first + t, True)
+    lax.fori_loop(first + ndiag, nq, lambda i, c: (block(i, False), c)[1], 0)
+    dk_ref[...] = dka[...].astype(jnp.bfloat16)
+    dv_ref[...] = dva[...].astype(jnp.bfloat16)
+
+    @pl.when(j == nk - 1)
+    def _():
+        def fin(i, c):
+            rows = pl.ds(pl.multiple_of(i * bq, bq), bq)
+            for h in range(heads):
+                cols = slice(h * HEAD_DIM, (h + 1) * HEAD_DIM)
+                dq_ref[rows, cols] = dqt[cols, rows].T.astype(jnp.bfloat16)
+            return c
+        lax.fori_loop(0, nq, fin, 0)
+
+
+def flash_bwd(q, d, k, kt, v, lse, rd, bq=512, bk=512):
+    seq, width = q.shape
+    heads = width // HEAD_DIM
+    whole = lambda j: (0, 0)
+    return pl.pallas_call(
+        functools.partial(bwd_kernel, bq, bk),
+        grid=(seq // bk,),
+        in_specs=[pl.BlockSpec((seq, width), whole), pl.BlockSpec((seq, width), whole),
+                  pl.BlockSpec((bk, HEAD_DIM), lambda j: (j, 0)), pl.BlockSpec((HEAD_DIM, bk), lambda j: (0, j)),
+                  pl.BlockSpec((bk, HEAD_DIM), lambda j: (j, 0)),
+                  pl.BlockSpec((heads, seq), whole), pl.BlockSpec((heads, seq), whole)],
+        out_specs=[pl.BlockSpec((seq, width), whole), pl.BlockSpec((bk, HEAD_DIM), lambda j: (j, 0)), pl.BlockSpec((bk, HEAD_DIM), lambda j: (j, 0))],
+        out_shape=[jax.ShapeDtypeStruct((seq, width), jnp.bfloat16), jax.ShapeDtypeStruct((seq, HEAD_DIM), jnp.bfloat16), jax.ShapeDtypeStruct((seq, HEAD_DIM), jnp.bfloat16)],
+        scratch_shapes=[pltpu.VMEM((width, seq), jnp.float32), pltpu.VMEM((bk, HEAD_DIM), jnp.float32), pltpu.VMEM((bk, HEAD_DIM), jnp.float32)],
+        cost_estimate=pl.CostEstimate(flops=5 * seq * seq * width * 2 // 2, bytes_accessed=16 << 20, transcendentals=seq * seq),
+        compiler_params=pltpu.CompilerParams(vmem_limit_bytes=56 << 20),
+        name="flash_bwd",
+    )(q, d, k, kt, v, lse, rd)
 
 
 def gather_full(local_shard):
@@ -102,10 +233,11 @@
     k_heads = to_heads(k_tok)
     v_heads = to_heads(v_tok)
     seq_len, kv_local = k_heads.shape[0], k_heads.shape[1]
-    q_grp = q_heads.reshape(seq_len, kv_local, num_heads // kv_heads, HEAD_DIM)
-    attn_probs = head_probs(q_grp, k_heads)
-    probs_bf = attn_probs.astype(jnp.bfloat16)
-    o_heads = jnp.einsum('ngqk,knd->qngd', probs_bf, v_heads, preferred_element_type=jnp.float32).astype(jnp.bfloat16).reshape(seq_len, -1, HEAD_DIM)
+    q_flat = q_heads.reshape(seq_len, -1)
+    k_flat = k_heads.reshape(seq_len, HEAD_DIM)
+    v_flat = v_heads.reshape(seq_len, HEAD_DIM)
+    o_flat, lse = flash_fwd(q_flat, k_flat, v_flat.T, 1024, 512)
+    o_heads = o_flat.reshape(seq_len, -1, HEAD_DIM)
     attn_out = to_tokens(o_heads).reshape(tok_count, num_heads * HEAD_DIM)
     wo_full = gather_full(w_out)
     residual = (tokens.astype(jnp.float32) + jnp.dot(attn_out, wo_full, preferred_element_type=jnp.float32)).astype(jnp.bfloat16)
@@ -140,13 +272,12 @@
     wo_back = gather_full(w_out)
     d_attn = dot_back(d_resid_bf, wo_back).astype(jnp.bfloat16).reshape(tok_count, num_heads, HEAD_DIM)
     d_heads = to_heads(d_attn)
-    d_grp = d_heads.reshape(seq_len, kv_local, -1, HEAD_DIM)
-    d_probs = jnp.einsum('qngd,knd->ngqk', d_grp, v_heads, preferred_element_type=jnp.float32)
-    grad_v = jnp.einsum('ngqk,qngd->knd', probs_bf, d_grp, preferred_element_type=jnp.float32).astype(jnp.bfloat16)
-    row_dot = jnp.sum(attn_probs * d_probs, axis=-1, keepdims=True)
-    d_scores = (attn_probs * (d_probs - row_dot) * ATTN_SCALE).astype(jnp.bfloat16)
-    grad_q = jnp.einsum('ngqk,knd->qngd', d_scores, k_heads, preferred_element_type=jnp.float32).astype(jnp.bfloat16).reshape(seq_len, -1, HEAD_DIM)
-    grad_k = jnp.einsum('ngqk,qngd->knd', d_scores, q_grp, preferred_element_type=jnp.float32).astype(jnp.bfloat16)
+    d_flat = d_heads.reshape(seq_len, -1)
+    row_dot = jnp.sum((o_flat.astype(jnp.float32) * d_flat.astype(jnp.float32)).reshape(seq_len, -1, HEAD_DIM), axis=-1).T
+    dq_flat, dk_flat, dv_flat = flash_bwd(q_flat, d_flat, k_flat, k_flat.T, v_flat, lse, row_dot, 512, 512)
+    grad_q = dq_flat.reshape(seq_len, -1, HEAD_DIM)
+    grad_k = dk_flat.reshape(seq_len, kv_local, HEAD_DIM)
+    grad_v = dv_flat.reshape(seq_len, kv_local, HEAD_DIM)
     dq_tok = to_tokens(grad_q)
     dk_tok = to_tokens(grad_k)
     dv_tok = to_tokens(grad_v).reshape(tok_count, kv_heads * HEAD_DIM)

time: 1340 us -> 1150 us (0.86)
  matrix products: 434 us -> 123 us
  other arithmetic: 183 us -> 31.5 us
  waiting for transfers between devices: 449 us -> 573 us
  Pallas kernels: 0 us -> 101 us
  blocking collectives: 168 us -> 198 us
  local copies, waits for them, and re-layouts: 59.4 us -> 84.5 us
    dot_general x6 -> x0, matrix products: 316 us -> none  [the longest x1 101 us: layer_step(): jnp.einsum('qngd,knd->ngqk', d_grp, v_heads, preferred_element_type=jnp.f...]
    another operation x3 -> x2, other arithmetic: 111 us -> 1.1 us
    pallas_call x0 -> x2, Pallas kernels: none -> 101 us  [the longest x1 57.6 us: flash_bwd(): pl.pallas_call(functools.partial(bwd_kernel, bq, bk), grid=(seq // bk,),...]
    reduce_scatter x7, waiting for transfers between devices: 374 us -> 421 us  [scatter_sum(): lax.psum_scatter(partial_sum, ALL_AXES, scatter_dimension=0, tiled=True)]
    reduce_sum x1, other arithmetic: 46.2 us -> 9.49 us  [layer_step(): jnp.sum((o_flat.astype(jnp.float32) * d_flat.astype(jnp.float32)).reshape...]
    all_to_all x3, waiting for transfers between devices: 2.46 us -> 37.9 us  [to_heads(): return lax.all_to_all(tok_major, 'sp', 1, 0, tiled=True)]
    all_gather x7, waiting for transfers between devices: 40.7 us -> 72.8 us  [gather_full(): return lax.all_gather(local_shard, ALL_AXES, axis=0, tiled=True)]
    all_to_all x2 -> x3, blocking collectives: 72.3 us -> 101 us  [to_tokens(): return lax.all_to_all(head_major, 'sp', 0, 1, tiled=True)]
  transfers between devices with their start and end apart: 19 -> 18, of which waited for: 8 -> 11; matrix products, arithmetic and copies ran while one was open for 43% -> 14% of each run, Pallas kernels for 0% -> 4%
where the time goes in v1:
time: 1150 us; the launch traced here: 1140 us
  waiting for transfers between devices  573 us (50%)
  blocking collectives  198 us (17%)
  matrix products  123 us (11%)
  Pallas kernels  101 us (9%)
  local copies, waits for them, and re-layouts  84.5 us (7%)
  other arithmetic  31.5 us (3%)
  starting transfers between devices  15.4 us (1%)
  between operations  14.8 us (1%)
    reduce_scatter x7, waiting for transfers between devices, scatter_sum(): lax.psum_scatter(partial_sum, ALL_AXES, scatter_dimension=0, tiled=True)  421 us
    all_to_all x3, blocking collectives, to_tokens(): return lax.all_to_all(head_major, 'sp', 0, 1, tiled=True)  101 us
    all_gather x7, waiting for transfers between devices, gather_full(): return lax.all_gather(local_shard, ALL_AXES, axis=0, tiled=True)  72.8 us
    unnamed x2, blocking collectives  66.8 us
    pallas_call x1, Pallas kernels, flash_bwd(): pl.pallas_call(functools.partial(bwd_kernel, bq, bk), grid=(seq // bk,),...  57.6 us
    dot_general x7, matrix products, dot_tokens(): lax.dot_general(left_op, right_op, (((0,), (0,)), ((), ())), preferred_el...  46.8 us
    pallas_call x1, Pallas kernels, flash_fwd(): pl.pallas_call(functools.partial(fwd_kernel, bq, bk), grid=(seq // bq,),...  43.5 us
    all_to_all x3, waiting for transfers between devices, to_heads(): return lax.all_to_all(tok_major, 'sp', 1, 0, tiled=True)  37.9 us
  transfers between devices with their start and end apart: 18, of which 11 were waited for; matrix products, arithmetic and copies ran while one was open for 14% of the time, Pallas kernels for 4%

profile of v1, /device:TPU:0, one launch (start us, length us, event | category | flops | bytes accessed | tf_op | source)
XLA Modules:
  0.0 1141.4 jit_solution(12910775608874145167)
XLA Ops:
  13.6 34.8 %all-reduce.5 = (bf16[1024]{0:T(1024)(128)(2,1)S(1)}, bf16[1024]{0:T(1024)(128)(2,1)S(1)}) all-reduce(bf16[1024]{0:T(1024)(128)(2,1)S(1)} %dynamic-update-slice, bf16[1024]{0:T(1024)(128)(2,1)S(1)} %dynamic-update-slice.1), channel_id=1, replica_groups=mesh['dp'=2,'sp'=8] {'dp','sp'}, use_global_device_ids=true, to_apply=%add | all-reduce | flops 2048 | bytes 8192
  50.0 3.9 copy.79
  58.3 3.6 all-to-all-start.1
  61.9 16.4 %all-gather.12.cloned.1.call-done = bf16[1024,1024]{1,0:T(8,128)(2,1)} async-done(((bf16[64,1024]{1,0:T(8,128)(2,1)}), bf16[1024,1024]{1,0:T(8,128)(2,1)}) %all-gather.12.cloned.1.call-update) | async-done | bytes 2097168 | tf_op jit(solution)/shard_map/all_gather | solution.py:193
  82.3 35.3 %all-gather.8.cloned.1.call-done = bf16[1024,2048]{1,0:T(8,128)(2,1)} async-done(((bf16[64,2048]{1,0:T(8,128)(2,1)}), bf16[1024,2048]{1,0:T(8,128)(2,1)}) %all-gather.8.cloned.1.call-update) | async-done | bytes 4194320 | tf_op jit(solution)/shard_map/all_gather | solution.py:193
  117.6 6.4 copy.77
  124.0 3.6 all-to-all-start.2
  127.7 4.7 fusion.42
  134.6 11.2 all-to-all-done.2
  145.8 3.8 all-to-all-start
  155.5 26.7 %all-to-all-done = bf16[512,16,128]{0,2,1:T(8,128)(2,1)S(1)} async-done(((bf16[512,16,128]{0,2,1:T(8,128)(2,1)}), bf16[512,16,128]{0,2,1:T(8,128)(2,1)S(1)}, u32[]{:S(2)}, u32[]{:S(2)}) %all-to-all-start) | async-done | bytes 2097184 | tf_op jit(solution)/shard_map/all_to_all | solution.py:201
  182.2 3.8 copy.78
  189.2 43.5 %flash_fwd.1 = (bf16[4096,256]{1,0:T(8,128)(2,1)}, f32[2,4096]{1,0:T(2,128)}) custom-call(bf16[4096,256]{1,0:T(8,128)(2,1)} %bitcast.185, bf16[4096,128]{1,0:T(8,128)(2,1)} %copy.82.k_ref, bf16[128,4096]{1,0:T(8,128)(2,1)} %copy.83.vt_ref), custom_call_target="tpu_custom_call" | custom-call | flops 17179869184 | bytes 8388608 | tf_op jit(solution)/shard_map/flash_fwd/pallas_call | solution.py:103
  232.7 4.0 reshape.256
  236.7 3.6 all-to-all-start.3
  240.6 36.7 %all-to-all-done.3 = bf16[4096,2,128]{2,1,0:T(2,128)(2,1)S(1)} async-done(((bf16[4096,2,128]{2,1,0:T(2,128)(2,1)}), bf16[4096,2,128]{2,1,0:T(2,128)(2,1)S(1)}, u32[]{:S(2)}, u32[]{:S(2)}) %all-to-all-start.3) | async-done | bytes 2097184 | tf_op jit(solution)/shard_map/all_to_all | solution.py:205
  282.0 6.3 fusion.29
  288.3 9.3 fusion.61
  297.6 8.4 fusion.59
  306.0 21.0 %all-gather.20.cloned.1.call-done = bf16[3072,1024]{1,0:T(8,128)(2,1)} async-done(((bf16[192,1024]{1,0:T(8,128)(2,1)}), bf16[3072,1024]{1,0:T(8,128)(2,1)}) %all-gather.20.cloned.1.call-update) | async-done | bytes 6291472 | tf_op jit(solution)/shard_map/all_gather | solution.py:193
  327.0 11.6 %multiply_convert_fusion = (bf16[512,3072]{1,0:T(8,128)(2,1)S(1)}, bf16[512,3072]{1,0:T(8,128)(2,1)S(1)}, bf16[512,3072]{1,0:T(8,128)(2,1)}) fusion(f32[512,3072]{1,0:T(8,128)} %fusion.61, f32[512,3072]{1,0:T(8,128)} %fusion.59, bf16[3072,1024]{1,0:T(8,128)(2,1)} %all-gather.20.cloned.1.call-done, bf16[1,512,1024]{2,1,0:T(8,128)(2,1)S(1)} %copy-done.15), kind=kOutput, calls=%fused_computation | convolution fusion | flops 3244818432 | bytes 29360128 | tf_op jit(solution)/shard_map/dot_general | solution.py:213
  338.6 8.7 fusion.68
  347.4 3.9 fusion.28
  356.5 30.2 %all_to_all.108 = bf16[512,16,128]{2,0,1:T(8,128)(2,1)S(1)} all-to-all(bf16[512,16,128]{2,0,1:T(8,128)(2,1)S(1)} %bitcast.173), channel_id=1, replica_groups=mesh['dp'=2,'sp'=8] {'sp'}, dimensions={1} | all-to-all | bytes 4194304 | tf_op jit(solution)/shard_map/all_to_all | solution.py:201
  393.7 5.8 reshape.260
  399.5 9.5 reduce_sum.66
  411.8 57.6 %flash_bwd.1 = (bf16[4096,256]{1,0:T(8,128)(2,1)}, bf16[4096,128]{1,0:T(8,128)(2,1)}, bf16[4096,128]{1,0:T(8,128)(2,1)}) custom-call(bf16[4096,256]{1,0:T(8,128)(2,1)} %bitcast.186, bf16[4096,256]{1,0:T(8,128)(2,1)} %bitcast.189, bf16[4096,128]{1,0:T(8,128)(2,1)} %copy.82.k_ref, bf16[128,4096]{1,0:T(8,128)(2,1)} %bitcast.182, bf16[4096,128]{1,0:T(8,128)(2,1)} %bitcast.180, ...), custom_call_target="tpu_custom_call" | custom-call | flops 21474836480 | bytes 16777216 | tf_op jit(solution)/shard_map/flash_bwd/pallas_call | solution.py:176
  473.7 18.8 %all_to_all.109 = bf16[8,2,32768]{2,1,0:T(2,128)(2,1)S(1)} all-to-all(bf16[8,2,32768]{2,1,0:T(2,128)(2,1)} %reshape.277), channel_id=1, replica_groups=mesh['dp'=2,'sp'=8] {'sp'}, dimensions={0} | all-to-all | bytes 2097152 | tf_op jit(solution)/shard_map/all_to_all | solution.py:205
  492.5 3.5 reshape.278
  502.5 3.5 fusion.48
  509.8 29.0 %all_to_all.110 = bf16[8,2,32768]{2,1,0:T(2,128)(2,1)S(1)} all-to-all(bf16[8,2,32768]{2,1,0:T(2,128)(2,1)} %reshape.275), channel_id=1, replica_groups=mesh['dp'=2,'sp'=8] {'sp'}, dimensions={0} | all-to-all | bytes 2097152 | tf_op jit(solution)/shard_map/all_to_all | solution.py:205
  545.3 5.0 fusion.46
  550.4 7.1 fusion.52
  558.8 8.4 fusion.57
  567.3 8.4 fusion.55
  576.9 8.4 fusion.36
  585.4 4.0 reshape.261
  589.4 53.2 %all_to_all.111 = bf16[4096,2,128]{2,1,0:T(2,128)(2,1)} all-to-all(bf16[4096,2,128]{2,1,0:T(2,128)(2,1)} %reshape.261), channel_id=1, replica_groups=mesh['dp'=2,'sp'=8] {'sp'}, dimensions={0} | all-to-all | bytes 4194304 | tf_op jit(solution)/shard_map/all_to_all | solution.py:205
  642.6 6.7 copy.90
  653.7 6.0 fusion.44
  659.7 8.5 fusion.33
  672.9 4.2 fusion.18
  677.1 32.0 %all-reduce.4 = (f32[1024]{0:T(1024)S(1)}, f32[1024]{0:T(1024)S(1)}) all-reduce(f32[1024]{0:T(1024)S(1)} %get-tuple-element.23, f32[1024]{0:T(1024)S(1)} %get-tuple-element.21), channel_id=2, replica_groups=mesh['dp'=2,'sp'=8] {'dp','sp'}, use_global_device_ids=true, to_apply=%region_6.0.clone | all-reduce | flops 2048 | bytes 16384
  713.4 40.4 %reduce-scatter.14.cloned.1.call-done = f32[128,1024]{1,0:T(8,128)} async-done(((f32[2048,1024]{1,0:T(8,128)}), f32[128,1024]{1,0:T(8,128)}) %reduce-scatter.14.cloned.1.call-update) | async-done | bytes 524304 | tf_op jit(solution)/shard_map/reduce_scatter | solution.py:197
  753.8 93.9 %reduce-scatter.16.cloned.1.call-done = f32[64,3072]{1,0:T(8,128)} async-done(((f32[1024,3072]{1,0:T(8,128)}), f32[64,3072]{1,0:T(8,128)}) %reduce-scatter.16.cloned.1.call-update) | async-done | bytes 786448 | tf_op jit(solution)/shard_map/reduce_scatter | solution.py:197
  847.7 95.5 %reduce-scatter.18.cloned.1.call-done = f32[64,3072]{1,0:T(8,128)} async-done(((f32[1024,3072]{1,0:T(8,128)}), f32[64,3072]{1,0:T(8,128)}) %reduce-scatter.18.cloned.1.call-update) | async-done | bytes 786448 | tf_op jit(solution)/shard_map/reduce_scatter | solution.py:197
  943.2 95.7 %reduce-scatter.20.cloned.1.call-done = f32[192,1024]{1,0:T(8,128)} async-done(((f32[3072,1024]{1,0:T(8,128)}), f32[192,1024]{1,0:T(8,128)}) %reduce-scatter.20.cloned.1.call-update) | async-done | bytes 786448 | tf_op jit(solution)/shard_map/reduce_scatter | solution.py:197
  1038.9 95.5 %reduce-scatter.8.cloned.1.call-done = f32[64,2048]{1,0:T(8,128)} async-done(((f32[1024,2048]{1,0:T(8,128)}), f32[64,2048]{1,0:T(8,128)}) %reduce-scatter.8.cloned.1.call-update) | async-done | bytes 524304 | tf_op jit(solution)/shard_map/reduce_scatter | solution.py:197
  (138 shorter events, 84.6 us)
Async XLA Ops:
  7.2 42.0 %copy-start.5 = (bf16[1,512,1024]{2,1,0:T(8,128)(2,1)S(1)}, bf16[1,512,1024]{2,1,0:T(8,128)(2,1)}, u32[]{:S(2)}) copy-start(bf16[1,512,1024]{2,1,0:T(8,128)(2,1)} %param.12) | copy-start | bytes 3145732
  7.2 42.8 %all-gather.10.cloned.1.call-start = ((), (), s32[]{:S(2)}) async-start(), calls=%async_computation.16 | async-start | bytes 2228224 | tf_op jit(solution)/shard_map/all_gather | solution.py:193
  7.9 70.4 %all-gather.12.cloned.1.call-start = ((), (), s32[]{:S(2)}) async-start(), calls=%async_computation.17 | async-start | bytes 2228224 | tf_op jit(solution)/shard_map/all_gather | solution.py:193
  8.7 109.0 %all-gather.8.cloned.1.call-start = ((), (), s32[]{:S(2)}) async-start(), calls=%async_computation.15 | async-start | bytes 4456448 | tf_op jit(solution)/shard_map/all_gather | solution.py:193
  9.4 272.6 %all-gather.14.cloned.1.call-start = ((), (), s32[]{:S(2)}) async-start(), calls=%async_computation.18 | async-start | bytes 4456448 | tf_op jit(solution)/shard_map/all_gather | solution.py:193
  10.0 278.3 %all-gather.16.cloned.1.call-start = ((), (), s32[]{:S(2)}) async-start(), calls=%async_computation.19 | async-start | bytes 6684672 | tf_op jit(solution)/shard_map/all_gather | solution.py:193
  10.6 287.1 %all-gather.18.cloned.1.call-start = ((), (), s32[]{:S(2)}) async-start(), calls=%async_computation.20 | async-start | bytes 6684672 | tf_op jit(solution)/shard_map/all_gather | solution.py:193
  11.1 315.9 %all-gather.20.cloned.1.call-start = ((), (), s32[]{:S(2)}) async-start(), calls=%async_computation.21 | async-start | bytes 6684672 | tf_op jit(solution)/shard_map/all_gather | solution.py:193
  58.3 65.7 %all-to-all-start.1 = ((bf16[512,8,128]{0,2,1:T(8,128)(2,1)}), bf16[512,8,128]{0,2,1:T(8,128)(2,1)S(1)}, u32[]{:S(2)}, u32[]{:S(2)}) async-start(bf16[512,8,128]{0,2,1:T(8,128)(2,1)} %pad_maximum_fusion.1), calls=%async_computation.1 | async-start | bytes 2097152 | tf_op jit(solution)/shard_map/all_to_all | solution.py:201
  124.0 8.4 copy-start.4
  124.0 21.8 %all-to-all-start.2 = ((bf16[512,8,128]{2,0,1:T(8,128)(2,1)}), bf16[512,8,128]{2,0,1:T(8,128)(2,1)S(1)}, u32[]{:S(2)}, u32[]{:S(2)}) async-start(bf16[512,8,128]{2,0,1:T(8,128)(2,1)} %bitcast.162), calls=%async_computation.2 | async-start | bytes 2097152 | tf_op jit(solution)/shard_map/all_to_all | solution.py:201
  145.8 8.4 copy-start.3
  145.8 36.4 %all-to-all-start = ((bf16[512,16,128]{0,2,1:T(8,128)(2,1)}), bf16[512,16,128]{0,2,1:T(8,128)(2,1)S(1)}, u32[]{:S(2)}, u32[]{:S(2)}) async-start(bf16[512,16,128]{0,2,1:T(8,128)(2,1)} %pad_maximum_fusion), calls=%async_computation | async-start | bytes 4194304 | tf_op jit(solution)/shard_map/all_to_all | solution.py:201
  236.7 40.7 %all-to-all-start.3 = ((bf16[4096,2,128]{2,1,0:T(2,128)(2,1)}), bf16[4096,2,128]{2,1,0:T(2,128)(2,1)S(1)}, u32[]{:S(2)}, u32[]{:S(2)}) async-start(bf16[4096,2,128]{2,1,0:T(2,128)(2,1)} %reshape.256), calls=%async_computation.3 | async-start | bytes 4194304 | tf_op jit(solution)/shard_map/all_to_all | solution.py:205
  240.3 473.1 %reduce-scatter.10.cloned.1.call-start = ((), (), s32[]{:S(2)}) async-start(), calls=%async_computation.23 | async-start | bytes 4456448 | tf_op jit(solution)/shard_map/reduce_scatter | solution.py:197
  279.0 3.0 copy-start.6
  281.9 6.4 copy-start
  288.3 9.3 copy-start.17
  297.6 29.4 %copy-start.15 = (bf16[1,512,1024]{2,1,0:T(8,128)(2,1)S(1)}, bf16[1,512,1024]{2,1,0:T(8,128)(2,1)}, u32[]{:S(2)}) copy-start(bf16[1,512,1024]{2,1,0:T(8,128)(2,1)} %param.14) | copy-start | bytes 3145732
  338.6 8.7 copy-start.24
  338.6 8.7 copy-start.23
  338.6 8.7 copy-start.20
  347.4 4.0 copy-start.18
  351.3 2.2 copy-start.21
  388.8 2.3 copy-start.1
  499.3 3.1 copy-start.7
  501.4 1.0 copy-start.12
  506.0 207.4 %reduce-scatter.12.cloned.1.call-start = ((), (), s32[]{:S(2)}) async-start(), calls=%async_computation.24 | async-start | bytes 4456448 | tf_op jit(solution)/shard_map/reduce_scatter | solution.py:197
  550.4 203.4 %reduce-scatter.14.cloned.1.call-start = ((), (), s32[]{:S(2)}) async-start(), calls=%async_computation.25 | async-start | bytes 8912896 | tf_op jit(solution)/shard_map/reduce_scatter | solution.py:197
  557.6 1.2 copy-start.19
  557.6 290.1 %reduce-scatter.16.cloned.1.call-start = ((), (), s32[]{:S(2)}) async-start(), calls=%async_computation.26 | async-start | bytes 13369344 | tf_op jit(solution)/shard_map/reduce_scatter | solution.py:197
  567.2 376.0 %reduce-scatter.18.cloned.1.call-start = ((), (), s32[]{:S(2)}) async-start(), calls=%async_computation.27 | async-start | bytes 13369344 | tf_op jit(solution)/shard_map/reduce_scatter | solution.py:197
  575.7 1.2 copy-start.16
  575.7 463.2 %reduce-scatter.20.cloned.1.call-start = ((), (), s32[]{:S(2)}) async-start(), calls=%async_computation.28 | async-start | bytes 13369344 | tf_op jit(solution)/shard_map/reduce_scatter | solution.py:197
  585.3 549.1 %reduce-scatter.8.cloned.1.call-start = ((), (), s32[]{:S(2)}) async-start(), calls=%async_computation.22 | async-start | bytes 8912896 | tf_op jit(solution)/shard_map/reduce_scatter | solution.py:197
  652.2 1.5 copy-start.8
  652.4 1.3 copy-start.10
  659.7 8.5 copy-start.14
  659.7 8.5 copy-start.22
  668.2 1.6 copy-start.9
  668.2 1.9 copy-start.13
  670.0 2.2 copy-start.2
  670.0 2.9 copy-start.11
Sparse Core Ops, SparseCore 0:
  10.2 31.4 all-gather.9
  44.0 34.2 all-gather.11
  80.5 37.0 all-gather.7
  119.7 52.3 all-gather.13
  174.2 48.1 all-gather.15
  224.5 58.4 all-gather.17
  285.2 41.7 all-gather.19
  506.1 69.5 reduce-scatter.9
  578.6 78.0 reduce-scatter.11
  659.4 94.4 reduce-scatter.13
  759.0 88.6 reduce-scatter.15
  852.8 90.4 reduce-scatter.17
  948.4 90.4 reduce-scatter.19
  1041.6 92.7 reduce-scatter.7

commit v2 on v1

v2 whole, which is shorter than its diff:
```python
import functools
import math

import jax
import jax.numpy as jnp
from jax import lax
from jax.experimental import pallas as pl
from jax.experimental.pallas import tpu as pltpu
from jax.sharding import PartitionSpec as P

HEAD_DIM = 128
ROPE_BASE = 10000.0
NORM_EPS = 1e-5
ATTN_SCALE = HEAD_DIM ** -0.5
ALL_AXES = ('dp', 'sp')


def rope_tables(pos_ids):
    inv_freq = ROPE_BASE ** (-(jnp.arange(HEAD_DIM // 2, dtype=jnp.float32) * (2.0 / HEAD_DIM)))
    angles = pos_ids.astype(jnp.float32)[..., None] * inv_freq
    return jnp.cos(angles), jnp.sin(angles)


def apply_rope(values, cos_tab, sin_tab):
    half_dim = values.shape[-1] // 2
    low_half = values[..., :half_dim]
    high_half = values[..., half_dim:]
    cos_wide = cos_tab[..., None, :]
    sin_wide = sin_tab[..., None, :]
    return jnp.concatenate([low_half * cos_wide - high_half * sin_wide, high_half * cos_wide + low_half * sin_wide], axis=-1)


def rope_grad(grads_in, cos_tab, sin_tab):
    half_dim = grads_in.shape[-1] // 2
    low_half = grads_in[..., :half_dim]
    high_half = grads_in[..., half_dim:]
    cos_wide = cos_tab[..., None, :]
    sin_wide = sin_tab[..., None, :]
    return jnp.concatenate([low_half * cos_wide + high_half * sin_wide, high_half * cos_wide - low_half * sin_wide], axis=-1)


def rms_norm(values, gain_vec):
    vals32 = values.astype(jnp.float32)
    inv_rms = lax.rsqrt(jnp.mean(vals32 * vals32, axis=-1, keepdims=True) + NORM_EPS)
    normed = vals32 * inv_rms
    return (normed * gain_vec.astype(jnp.float32)).astype(jnp.bfloat16), normed, inv_rms


def rms_norm_grad(d_out, normed, inv_rms, gain_vec):
    d_normed = d_out * gain_vec.astype(jnp.float32)
    grad_gain = jnp.sum(d_out * normed, axis=0)
    grad_in = inv_rms * (d_normed - normed * jnp.mean(d_normed * normed, axis=-1, keepdims=True))
    return grad_in, grad_gain


LOG2E = math.log2(math.e)
SCALE2 = ATTN_SCALE * LOG2E
NT = (((1,), (1,)), ((), ()))
NN = (((1,), (0,)), ((), ()))
BIG = -1e30


def fwd_kernel(bq, bk, q_ref, k_ref, vt_ref, o_ref, lse_ref):
    i = pl.program_id(0)
    heads = q_ref.shape[1] // HEAD_DIM
    qs = [q_ref[:, h * HEAD_DIM:(h + 1) * HEAD_DIM] for h in range(heads)]

    def block(j, carry, masked):
        rows = pl.ds(pl.multiple_of(j * bk, bk), bk)
        k = k_ref[rows, :]
        vt = vt_ref[:, rows]
        out = []
        for h in range(heads):
            m, l, acc = carry[h]
            s = lax.dot_general(k, qs[h], NT, preferred_element_type=jnp.float32)
            if masked:
                kpos = j * bk + lax.broadcasted_iota(jnp.int32, (bk, bq), 0)
                qpos = i * bq + lax.broadcasted_iota(jnp.int32, (bk, bq), 1)
                s = jnp.where(qpos >= kpos, s, BIG)
            m_new = jnp.maximum(m, jnp.max(s, axis=0, keepdims=True))
            p = jnp.exp2((s - m_new) * SCALE2)
            alpha = jnp.exp2((m - m_new) * SCALE2)
            l = l * alpha + jnp.sum(p, axis=0, keepdims=True)
            acc = acc * alpha + lax.dot_general(vt, p.astype(jnp.bfloat16), NN, preferred_element_type=jnp.float32)
            out.append((m_new, l, acc))
        return tuple(out)

    init = tuple((jnp.full((1, bq), BIG, jnp.float32), jnp.zeros((1, bq), jnp.float32), jnp.zeros((HEAD_DIM, bq), jnp.float32)) for _ in range(heads))
    full = i * bq // bk
    carry = lax.fori_loop(0, full, lambda j, c: block(j, c, False), init)
    for d in range(max(1, bq // bk)):
        carry = block(full + d, carry, True)
    for h in range(heads):
        m, l, acc = carry[h]
        o = acc / l
        o_ref[:, h * HEAD_DIM:(h + 1) * HEAD_DIM] = o.T.astype(jnp.bfloat16)
        lse_ref[h:h + 1, :] = m * SCALE2 + jnp.log2(l)


def flash_fwd(q, k, vt, bq=512, bk=512):
    seq, width = q.shape
    heads = width // HEAD_DIM
    return pl.pallas_call(
        functools.partial(fwd_kernel, bq, bk),
        grid=(seq // bq,),
        in_specs=[pl.BlockSpec((bq, width), lambda i: (i, 0)),
                  pl.BlockSpec((seq, HEAD_DIM), lambda i: (0, 0)),
                  pl.BlockSpec((HEAD_DIM, seq), lambda i: (0, 0))],
        out_specs=[pl.BlockSpec((bq, width), lambda i: (i, 0)),
                   pl.BlockSpec((heads, bq), lambda i: (0, i))],
        out_shape=[jax.ShapeDtypeStruct((seq, width), jnp.bfloat16), jax.ShapeDtypeStruct((heads, seq), jnp.float32)],
        cost_estimate=pl.CostEstimate(flops=2 * seq * seq * width * 2, bytes_accessed=8 << 20, transcendentals=seq * seq),
        compiler_params=pltpu.CompilerParams(vmem_limit_bytes=56 << 20),
        name="flash_fwd",
    )(q, k, vt)


def bwd_kernel(bq, bk, q_ref, o_ref, d_ref, k_ref, kt_ref, v_ref, lse_ref, out_ref, dqt, dka, dva, rd):
    j = pl.program_id(0)
    nk = pl.num_programs(0)
    seq, width = q_ref.shape
    heads = width // HEAD_DIM
    nq = seq // bq
    k = k_ref[...]
    v = v_ref[...]
    kt = kt_ref[...]

    @pl.when(j == 0)
    def _():
        dqt[...] = jnp.zeros_like(dqt)

        def prep(i, c):
            rows = pl.ds(pl.multiple_of(i * bq, bq), bq)
            for h in range(heads):
                cols = slice(h * HEAD_DIM, (h + 1) * HEAD_DIM)
                prod = o_ref[rows, cols].astype(jnp.float32) * d_ref[rows, cols].astype(jnp.float32)
                rd[h:h + 1, rows] = jnp.sum(prod.T, axis=0, keepdims=True)
            return c
        lax.fori_loop(0, nq, prep, 0)

    dka[...] = jnp.zeros_like(dka)
    dva[...] = jnp.zeros_like(dva)

    def block(i, masked):
        rows = pl.ds(pl.multiple_of(i * bq, bq), bq)
        for h in range(heads):
            cols = slice(h * HEAD_DIM, (h + 1) * HEAD_DIM)
            q = q_ref[rows, cols]
            d = d_ref[rows, cols]
            s = lax.dot_general(k, q, NT, preferred_element_type=jnp.float32)
            dp = lax.dot_general(v, d, NT, preferred_element_type=jnp.float32)
            p = jnp.exp2(s * SCALE2 - lse_ref[h:h + 1, rows])
            if masked:
                kpos = j * bk + lax.broadcasted_iota(jnp.int32, (bk, bq), 0)
                qpos = i * bq + lax.broadcasted_iota(jnp.int32, (bk, bq), 1)
                p = jnp.where(qpos >= kpos, p, 0.0)
            ds = (p * (dp - rd[h:h + 1, rows]) * ATTN_SCALE).astype(jnp.bfloat16)
            dva[...] += lax.dot_general(p.astype(jnp.bfloat16), d, NN, preferred_element_type=jnp.float32)
            dka[...] += lax.dot_general(ds, q, NN, preferred_element_type=jnp.float32)
            dqt[cols, rows] += lax.dot_general(kt, ds, NN, preferred_element_type=jnp.float32)

    first = j * bk // bq
    ndiag = max(1, bk // bq)
    for t in range(ndiag):
        block(first + t, True)
    lax.fori_loop(first + ndiag, nq, lambda i, c: (block(i, False), c)[1], 0)
    own = pl.ds(pl.multiple_of(j * bk, bk), bk)
    out_ref[own, width:width + HEAD_DIM] = dka[...].astype(jnp.bfloat16)
    out_ref[own, width + HEAD_DIM:] = dva[...].astype(jnp.bfloat16)

    @pl.when(j == nk - 1)
    def _():
        def fin(i, c):
            rows = pl.ds(pl.multiple_of(i * bq, bq), bq)
            for h in range(heads):
                cols = slice(h * HEAD_DIM, (h + 1) * HEAD_DIM)
                out_ref[rows, cols] = dqt[cols, rows].T.astype(jnp.bfloat16)
            return c
        lax.fori_loop(0, nq, fin, 0)


def flash_bwd(q, o, d, k, kt, v, lse, bq=512, bk=512):
    seq, width = q.shape
    heads = width // HEAD_DIM
    whole = lambda j: (0, 0)
    return pl.pallas_call(
        functools.partial(bwd_kernel, bq, bk),
        grid=(seq // bk,),
        in_specs=[pl.BlockSpec((seq, width), whole), pl.BlockSpec((seq, width), whole), pl.BlockSpec((seq, width), whole),
                  pl.BlockSpec((bk, HEAD_DIM), lambda j: (j, 0)), pl.BlockSpec((HEAD_DIM, bk), lambda j: (0, j)),
                  pl.BlockSpec((bk, HEAD_DIM), lambda j: (j, 0)),
                  pl.BlockSpec((heads, seq), whole)],
        out_specs=pl.BlockSpec((seq, width + 2 * HEAD_DIM), whole),
        out_shape=jax.ShapeDtypeStruct((seq, width + 2 * HEAD_DIM), jnp.bfloat16),
        scratch_shapes=[pltpu.VMEM((width, seq), jnp.float32), pltpu.VMEM((bk, HEAD_DIM), jnp.float32), pltpu.VMEM((bk, HEAD_DIM), jnp.float32),
                        pltpu.VMEM((heads, seq), jnp.float32)],
        cost_estimate=pl.CostEstimate(flops=5 * seq * seq * width * 2 // 2, bytes_accessed=16 << 20, transcendentals=seq * seq),
        compiler_params=pltpu.CompilerParams(vmem_limit_bytes=56 << 20),
        name="flash_bwd",
    )(q, o, d, k, kt, v, lse)


MESH = pl.DeviceIdType.MESH
ORDERS = ('xyz', 'yzx', 'zxy')


class Spot:
    def __init__(self):
        self.z = lax.axis_index('dp')
        self.s = lax.axis_index('sp')
        self.y = self.s // 4
        self.x = (self.s // 2) % 2
        self.c = self.s % 2
        self.bits = {'z': self.z, 'y': self.y, 'x': self.x}

    def peer(self, dim):
        if dim == 'z':
            return (1 - self.z, self.s)
        if dim == 'y':
            return (self.z, self.s + 4 - 8 * self.y)
        if dim == 'x':
            return (self.z, self.s + 2 - 4 * self.x)
        return (self.z, self.s + 1 - 2 * self.c)

    def others(self):
        return [(self.z, (self.s + t) % 8) for t in range(1, 8)]

    def region(self, freed, flipped=''):
        return tuple(slice(None) if d in freed else (1 - self.bits[d] if d in flipped else self.bits[d]) for d in 'zyx')


def greet(targets):
    bar = pltpu.get_barrier_semaphore()
    for t in targets:
        pl.semaphore_signal(bar, inc=1, device_id=t, device_id_type=MESH)
    pl.semaphore_wait(bar, len(targets))


class Wires:
    def __init__(self, send_sem, recv_sem):
        self.send_sem, self.recv_sem, self.n = send_sem, recv_sem, 0

    def copy(self, src, dst, target):
        i = self.n
        self.n += 1
        return pltpu.make_async_remote_copy(src_ref=src, dst_ref=dst, send_sem=self.send_sem.at[i], recv_sem=self.recv_sem.at[i], device_id=target, device_id_type=MESH)


class PlaneGather:
    N = 13

    def __init__(self, here, wires, src, out, local_sem):
        h = src.shape[0] // 2
        A, B = slice(0, h), slice(h, 2 * h)
        s = here.s
        sx, sy, sc = here.peer('x')[1], here.peer('y')[1], here.peer('c')[1]
        sd = here.s + 2 - 4 * here.x + 4 - 8 * here.y
        nx, ny, nc = here.peer('x'), here.peer('y'), here.peer('c')
        self.local = pltpu.make_async_copy(src, out.at[s], local_sem)
        mk = wires.copy
        self.x1 = {k: mk(src.at[r], out.at[s, r], nx) for k, r in (('A', A), ('B', B))}
        self.y1 = {k: mk(src.at[r], out.at[s, r], ny) for k, r in (('B', B), ('A', A))}
        self.c1 = mk(src, out.at[s], nc)
        self.fy = mk(out.at[sx, A], out.at[sx, A], ny)
        self.fx = mk(out.at[sy, B], out.at[sy, B], nx)
        self.cc = {}
        for name, idx in (('x', sx), ('y', sy), ('d', sd)):
            for k, r in (('A', A), ('B', B)):
                self.cc[name + k] = mk(out.at[idx, r], out.at[idx, r], nc)

    def start(self):
        self.x1['A'].start(); self.y1['B'].start(); self.x1['B'].start(); self.y1['A'].start()
        self.c1.start(); self.local.start()

    def finish(self):
        self.x1['A'].wait_recv(); self.fy.start(); self.cc['xA'].start()
        self.y1['B'].wait_recv(); self.fx.start(); self.cc['yB'].start()
        self.x1['B'].wait_recv(); self.cc['xB'].start()
        self.y1['A'].wait_recv(); self.cc['yA'].start()
        self.fy.wait_recv(); self.cc['dA'].start()
        self.fx.wait_recv(); self.cc['dB'].start()
        self.c1.wait_recv()
        for k in self.cc:
            self.cc[k].wait_recv()
        for c in (*self.x1.values(), *self.y1.values(), self.c1, self.fy, self.fx, *self.cc.values()):
            c.wait_send()
        self.local.wait()


def plane_targets(here):
    return [here.peer('x'), here.peer('y'), here.peer('c')]


def plane_gather_kernel(src, out, send_sem, recv_sem, local_sem):
    here = Spot()
    greet(plane_targets(here))
    g = PlaneGather(here, Wires(send_sem, recv_sem), src, out, local_sem)
    g.start()
    g.finish()


def plane_gather(src, cid, name):
    rows, cols = src.shape
    n = PlaneGather.N
    return pl.pallas_call(
        plane_gather_kernel,
        in_specs=[pl.BlockSpec(memory_space=pltpu.VMEM)],
        out_specs=pl.BlockSpec(memory_space=pl.ANY),
        out_shape=jax.ShapeDtypeStruct((8, rows, cols), src.dtype),
        scratch_shapes=[pltpu.SemaphoreType.DMA((n,)), pltpu.SemaphoreType.DMA((n,)), pltpu.SemaphoreType.DMA],
        compiler_params=pltpu.CompilerParams(collective_id=cid, has_side_effects=True),
        name=name,
    )(src)


def entry_kernel(x_ref, w_ref, meta_ref, pos_ref, xa, wa, ma, pa, send_sem, recv_sem, local_sem):
    here = Spot()
    z, s = here.z, here.s
    peers = here.others()
    nz = here.peer('z')
    greet(peers + [nz])
    wires = Wires(send_sem, recv_sem)
    first = []
    for t in peers:
        for src, dst in ((w_ref.at[t[1]], wa.at[z, s]), (meta_ref, ma.at[z, s]), (pos_ref, pa.at[s])):
            first.append(wires.copy(src, dst, t))
    locals_ = [pltpu.make_async_copy(w_ref.at[s], wa.at[z, s], local_sem.at[1]),
               pltpu.make_async_copy(meta_ref, ma.at[z, s], local_sem.at[2]),
               pltpu.make_async_copy(pos_ref, pa.at[s], local_sem.at[3])]
    g = PlaneGather(here, wires, x_ref, xa, local_sem.at[0])
    cross = [wires.copy(wa.at[z], wa.at[z], nz), wires.copy(ma.at[z], ma.at[z], nz)]
    for c in first:
        c.start()
    for c in locals_:
        c.start()
    g.start()
    for c in first:
        c.wait_recv()
    for c in locals_:
        c.wait()
    for c in cross:
        c.start()
    g.finish()
    for c in cross:
        c.wait()
    for c in first:
        c.wait_send()


def entry(x, w, meta, pos, cid):
    n = PlaneGather.N + 21 + 2
    vm = pl.BlockSpec(memory_space=pltpu.VMEM)
    an = pl.BlockSpec(memory_space=pl.ANY)
    return pl.pallas_call(
        entry_kernel,
        in_specs=[vm] * 4, out_specs=[an] * 4,
        out_shape=[jax.ShapeDtypeStruct((8, *x.shape), x.dtype), jax.ShapeDtypeStruct((2, 8, *w.shape[1:]), w.dtype),
                   jax.ShapeDtypeStruct((2, 8, *meta.shape), meta.dtype), jax.ShapeDtypeStruct((8, *pos.shape), pos.dtype)],
        scratch_shapes=[pltpu.SemaphoreType.DMA((n,)), pltpu.SemaphoreType.DMA((n,)), pltpu.SemaphoreType.DMA((4,))],
        compiler_params=pltpu.CompilerParams(collective_id=cid, has_side_effects=True),
        name="entry",
    )(x, w, meta, pos)


def regroup_kernel(src, out, send_sem, recv_sem, local_sem, stage):
    here = Spot()
    s = here.s
    rows, width = out.shape[0], src.shape[1]
    peers = here.others()
    greet(peers)
    wires = Wires(send_sem, recv_sem)
    piece = lambda i: pl.ds(pl.multiple_of(i * rows, rows), rows)
    mine = pl.ds(pl.multiple_of(s * width, width), width)
    cs = [wires.copy(src.at[piece(t[1])], out.at[:, mine], t) for t in peers]
    for c in cs:
        c.start()
    a = pltpu.make_async_copy(src.at[piece(s)], stage, local_sem.at[0])
    a.start(); a.wait()
    b = pltpu.make_async_copy(stage, out.at[:, mine], local_sem.at[1])
    b.start(); b.wait()
    for c in cs:
        c.wait()


def regroup(src, cid, name):
    seq, width = src.shape
    rows = seq // 8
    an = pl.BlockSpec(memory_space=pl.ANY)
    return pl.pallas_call(
        regroup_kernel, in_specs=[an], out_specs=an,
        out_shape=jax.ShapeDtypeStruct((rows, 8 * width), src.dtype),
        scratch_shapes=[pltpu.SemaphoreType.DMA((7,)), pltpu.SemaphoreType.DMA((7,)), pltpu.SemaphoreType.DMA((2,)), pltpu.VMEM((rows, width), src.dtype)],
        compiler_params=pltpu.CompilerParams(collective_id=cid, has_side_effects=True),
        name=name,
    )(src)


class CubeGather:
    def __init__(self, here, wires, jobs):
        self.steps = []
        for i in range(3):
            cs = []
            for out, suffix, order in jobs:
                reg = here.region(order[:i]) + suffix
                cs.append(wires.copy(out.at[reg], out.at[reg], here.peer(order[i])))
            self.steps.append(cs)

    def start(self, i):
        for c in self.steps[i]:
            c.start()

    def arrive(self, i):
        for c in self.steps[i]:
            c.wait_recv()

    def drain(self):
        for cs in self.steps:
            for c in cs:
                c.wait_send()


def col_chunks(cols):
    n = cols // 128
    a = -(-n // 3)
    b = -(-(n - a) // 2)
    return [(0, a * 128), (a * 128, b * 128), ((a + b) * 128, (n - a - b) * 128)]


def cube_targets(here):
    return [here.peer(d) for d in 'xyzc']


def wgather_plan(here, wires, local_sem, ins, outs):
    w1, w3, w2, wo = ins
    o1, o3, o2, oo = outs
    c = here.c
    zyx = here.region('')
    nc = here.peer('c')
    pre = [wires.copy(w1.at[1 - c], o1.at[zyx + (c,)], nc), wires.copy(w3.at[1 - c], o3.at[zyx + (c,)], nc)]
    loc = [pltpu.make_async_copy(w1.at[c], o1.at[zyx + (c,)], local_sem.at[0]),
           pltpu.make_async_copy(w3.at[c], o3.at[zyx + (c,)], local_sem.at[1]),
           pltpu.make_async_copy(w2, o2.at[zyx], local_sem.at[2]),
           pltpu.make_async_copy(wo, oo.at[zyx + (c,)], local_sem.at[3])]
    jobs = [(o1, (), ORDERS[0]), (o3, (), ORDERS[1]), (o2, (), ORDERS[2])]
    for (off, n), order in zip(col_chunks(wo.shape[1]), ORDERS):
        jobs.append((oo, (c, slice(None), slice(off, off + n)), order))
    cube = CubeGather(here, wires, jobs)
    post = [wires.copy(oo.at[:, :, :, c], oo.at[:, :, :, c], nc)]
    return pre, loc, cube, post

NW = 2 + 6 * 3 + 1

def wgather_kernel(w1, w3, w2, wo, o1, o3, o2, oo, send_sem, recv_sem, local_sem):
    here = Spot()
    greet(cube_targets(here))
    pre, loc, cube, post = wgather_plan(here, Wires(send_sem, recv_sem), local_sem, (w1, w3, w2, wo), (o1, o3, o2, oo))
    for c in pre + loc: c.start()
    for c in loc: c.wait()
    for c in pre: c.wait()
    for i in range(3):
        cube.start(i)
        cube.arrive(i)
    for c in post: c.start()
    for c in post: c.wait()
    cube.drain()

def wgather_shapes(w1, w3, w2, wo):
    return [jax.ShapeDtypeStruct((2, 2, 2, *w.shape), w.dtype) if k < 3 else jax.ShapeDtypeStruct((2, 2, 2, 2, *w.shape), w.dtype) for k, w in enumerate((w1, w3, w2, wo))]

def wgather(w1, w3, w2, wo, cid):
    vm = pl.BlockSpec(memory_space=pltpu.VMEM); an = pl.BlockSpec(memory_space=pl.ANY)
    return pl.pallas_call(
        wgather_kernel, in_specs=[vm] * 4, out_specs=[an] * 4, out_shape=wgather_shapes(w1, w3, w2, wo),
        scratch_shapes=[pltpu.SemaphoreType.DMA((NW,)), pltpu.SemaphoreType.DMA((NW,)), pltpu.SemaphoreType.DMA((4,))],
        compiler_params=pltpu.CompilerParams(collective_id=cid, has_side_effects=True), name="wgather",
    )(w1, w3, w2, wo)

def halve_kernel(nd, n, *refs):
    ins, outs = refs[:n], refs[n:2 * n]
    send_sem, recv_sem = refs[2 * n:]
    here = Spot()
    greet([here.peer(d) for d in 'xyz'])
    wires = Wires(send_sem, recv_sem)
    cs = []
    for k in range(n):
        order = ORDERS[k % 3]
        live = [d for d in 'zyx' if d in order[:nd]]
        d = order[nd - 1]
        reg = tuple(1 - here.bits[d] if e == d else slice(None) for e in live)
        cs.append(wires.copy(ins[k].at[reg], outs[k], here.peer(d)))
    for c in cs: c.start()
    for c in cs: c.wait()

def halve(arrs, nd, cid, name):
    n = len(arrs)
    outs = [jax.ShapeDtypeStruct((*((2,) * (nd - 1)), *a.shape[nd:]), a.dtype) for a in arrs]
    an = pl.BlockSpec(memory_space=pl.ANY)
    return pl.pallas_call(
        functools.partial(halve_kernel, nd, n), in_specs=[an] * n, out_specs=[an] * n, out_shape=outs,
        scratch_shapes=[pltpu.SemaphoreType.DMA((n,)), pltpu.SemaphoreType.DMA((n,))],
        compiler_params=pltpu.CompilerParams(collective_id=cid, has_side_effects=True), name=name,
    )(*arrs)


def ggather_kernel(wg, og, send_sem, recv_sem, local_sem):
    here = Spot()
    greet(cube_targets(here))
    c = here.c
    wires = Wires(send_sem, recv_sem)
    loc = pltpu.make_async_copy(wg, og.at[here.region('') + (c,)], local_sem)
    jobs = [(og, (c, slice(None), slice(off, off + n)), order) for (off, n), order in zip(col_chunks(wg.shape[1]), ORDERS)]
    cube = CubeGather(here, wires, jobs)
    post = wires.copy(og.at[:, :, :, c], og.at[:, :, :, c], here.peer('c'))
    loc.start()
    loc.wait()
    for i in range(3):
        cube.start(i)
        cube.arrive(i)
    post.start()
    post.wait()
    cube.drain()


def ggather(wg, cid):
    return pl.pallas_call(
        ggather_kernel, in_specs=[pl.BlockSpec(memory_space=pltpu.VMEM)], out_specs=pl.BlockSpec(memory_space=pl.ANY),
        out_shape=jax.ShapeDtypeStruct((2, 2, 2, 2, *wg.shape), wg.dtype),
        scratch_shapes=[pltpu.SemaphoreType.DMA((10,)), pltpu.SemaphoreType.DMA((10,)), pltpu.SemaphoreType.DMA],
        compiler_params=pltpu.CompilerParams(collective_id=cid, has_side_effects=True), name="ggather",
    )(wg)


def owner_kernel(a, b, oa, ob, send_sem, recv_sem, local_sem):
    here = Spot()
    peers = here.others()
    greet(peers)
    wires = Wires(send_sem, recv_sem)
    s = here.s
    cs = [wires.copy(r.at[t[1]], o.at[s], t) for t in peers for r, o in ((a, oa), (b, ob))]
    loc = [pltpu.make_async_copy(a.at[s], oa.at[s], local_sem.at[0]), pltpu.make_async_copy(b.at[s], ob.at[s], local_sem.at[1])]
    for c in cs + loc:
        c.start()
    for c in cs + loc:
        c.wait()


def owner(a, b, cid):
    vm = pl.BlockSpec(memory_space=pltpu.VMEM)
    return pl.pallas_call(
        owner_kernel, in_specs=[vm] * 2, out_specs=[vm] * 2,
        out_shape=[jax.ShapeDtypeStruct(t.shape, t.dtype) for t in (a, b)],
        scratch_shapes=[pltpu.SemaphoreType.DMA((14,)), pltpu.SemaphoreType.DMA((14,)), pltpu.SemaphoreType.DMA((2,))],
        compiler_params=pltpu.CompilerParams(collective_id=cid, has_side_effects=True), name="owner",
    )(a, b)


def dot_tokens(left_op, right_op):
    return lax.dot_general(left_op, right_op, (((0,), (0,)), ((), ())), preferred_element_type=jnp.float32)


def dot_back(left_op, weight):
    return lax.dot_general(left_op, weight, (((1,), (1,)), ((), ())), preferred_element_type=jnp.float32)


def dot_on(left_op, weight):
    return jnp.dot(left_op, weight, preferred_element_type=jnp.float32)


def swap_core(t):
    return lax.ppermute(t, 'sp', [(i, i ^ 1) for i in range(8)])


def swap_z(t):
    return lax.ppermute(t, 'dp', [(0, 1), (1, 0)])


def halve_sum(arrs, nd, cid, name):
    here = Spot()
    got = halve(arrs, nd, cid, name)
    out = []
    for i, (g, r) in enumerate(zip(arrs, got)):
        order = ORDERS[i % 3]
        live = [d for d in 'zyx' if d in order[:nd]]
        d = order[nd - 1]
        out.append(lax.dynamic_index_in_dim(g, here.bits[d], live.index(d), False) + r)
    return out


def split_cols(w):
    rows, cols = w.shape
    return w.reshape(rows, 8, 2, cols // 16).transpose(2, 0, 1, 3).reshape(2, rows, cols // 2)


def join_cols(mine, other, c):
    rows, half = mine.shape
    m, o = mine.reshape(rows, 8, 1, half // 8), other.reshape(rows, 8, 1, half // 8)
    first = jnp.where(c == 0, m, o)
    second = jnp.where(c == 0, o, m)
    return jnp.concatenate([first, second], axis=2).reshape(rows, 2 * half)


def layer_step(hidden, positions, grad_out, gain_attn, gain_mlp, w_query, w_key, w_value, w_out, w_gate, w_up, w_down):
    tokens = hidden[0]
    d_layer = grad_out[0]
    tok, dim = tokens.shape
    here = Spot()
    z, s, c = here.z, here.s, here.c
    rows = w_query.shape[0]
    grp_q = w_query.shape[1] // 8
    grp_k = w_key.shape[1] // 8
    grp = grp_q + 2 * grp_k
    seq = 8 * tok

    w_grp = jnp.concatenate([w_query.reshape(rows, 8, grp_q), w_key.reshape(rows, 8, grp_k), w_value.reshape(rows, 8, grp_k)], axis=2)
    w_flat = w_grp.reshape(rows, 8 * grp)
    pad = HEAD_DIM - gain_attn.shape[0]
    meta = jnp.pad(jnp.stack([jnp.pad(gain_attn, (0, pad)), jnp.pad(gain_mlp, (0, pad))]), ((0, 14), (0, 0)))
    x_all, w_own, meta_all, pos_all = entry(tokens, w_grp.transpose(1, 0, 2), meta, positions[0].reshape(-1, 128), 1)
    x_all = x_all.reshape(seq, dim)
    w_own = w_own.reshape(dim, grp)
    gain1 = meta_all[:, :, 0, :rows].reshape(dim)
    gain2 = meta_all[:, :, 1, :rows].reshape(dim)
    cos_tab, sin_tab = rope_tables(pos_all.reshape(seq))

    u_all = rms_norm(x_all, gain1)[0]
    qkv = dot_on(u_all, w_own)
    heads = (grp_q + grp_k) // HEAD_DIM
    qk = apply_rope(qkv[:, :grp_q + grp_k].reshape(seq, heads, HEAD_DIM), cos_tab, sin_tab).astype(jnp.bfloat16).reshape(seq, grp_q + grp_k)
    q_own, k_own = qk[:, :grp_q], qk[:, grp_q:]
    v_own = qkv[:, grp_q + grp_k:].astype(jnp.bfloat16)
    k_t, v_t = k_own.T, v_own.T
    o_own, lse = flash_fwd(q_own, k_own, v_t, 1024, 512)

    w1, w3, w2, wo = wgather(split_cols(w_gate), split_cols(w_up), w_down, w_out, 2)
    ffn_half = w1.shape[-1]
    w1, w3 = w1.reshape(dim, ffn_half), w3.reshape(dim, ffn_half)
    w2 = w2.reshape(ffn_half, dim)
    wo = wo.reshape(-1, dim)
    attn_out = regroup(o_own, 3, 'regroup_o')
    residual = (tokens.astype(jnp.float32) + dot_on(attn_out, wo)).astype(jnp.bfloat16)
    u_mlp, normed2, inv_rms2 = rms_norm(residual, gain2)
    u_pair = jnp.concatenate([u_mlp, swap_core(u_mlp)], axis=0)
    d_pair = jnp.concatenate([d_layer, swap_core(d_layer)], axis=0)
    gate_pre = dot_on(u_pair, w1)
    up_pre = dot_on(u_pair, w3)
    sig_gate = jax.nn.sigmoid(gate_pre)
    silu_gate = gate_pre * sig_gate
    mlp_act = (silu_gate * up_pre).astype(jnp.bfloat16)
    y_part = dot_on(mlp_act, w2)
    layer_out = (residual.astype(jnp.float32) + (y_part[:tok] + swap_core(y_part[tok:]))).astype(jnp.bfloat16)

    d_act = dot_back(d_pair, w2)
    d_gate = (d_act * up_pre * sig_gate * (1.0 + gate_pre * (1.0 - sig_gate))).astype(jnp.bfloat16)
    d_up = (d_act * silu_gate).astype(jnp.bfloat16)
    d_part = dot_back(d_gate, w1) + dot_back(d_up, w3)
    d_umlp = d_part[:tok] + swap_core(d_part[tok:])
    d_res_norm, d_gain2 = rms_norm_grad(d_umlp, normed2, inv_rms2, gain2)
    d_resid = d_layer.astype(jnp.float32) + d_res_norm
    d_resid_bf = d_resid.astype(jnp.bfloat16)
    g1 = dot_tokens(u_pair, d_gate).reshape(2, 2, 2, dim // 8, ffn_half)
    g3 = dot_tokens(u_pair, d_up).reshape(2, 2, 2, dim // 8, ffn_half)
    g2 = dot_tokens(mlp_act, d_pair).reshape(2, 2, 2, ffn_half // 8, dim)

    dh_all = plane_gather(d_resid_bf, 4, 'gather_dh').reshape(seq, dim)
    wo_own = lax.dynamic_slice_in_dim(wo, s * grp_q, grp_q, 0)
    d_own = dot_back(dh_all, wo_own).astype(jnp.bfloat16)
    go = dot_tokens(o_own, dh_all).reshape(2, grp_q // 2, dim)
    g_mlp = halve_sum([g1, g3, g2], 3, 6, 'halve3')
    dqkv = flash_bwd(q_own, o_own, d_own, k_own, k_t, v_own, lse, 512, 512)
    back = rope_grad(dqkv[:, :grp_q + grp_k].astype(jnp.float32).reshape(seq, heads, HEAD_DIM), cos_tab, sin_tab).astype(jnp.bfloat16)
    dqkv_pre = jnp.concatenate([back.reshape(seq, grp_q + grp_k), dqkv[:, grp_q + grp_k:]], axis=1)

    go_mine = lax.dynamic_index_in_dim(go, z, 0, False) + swap_z(lax.dynamic_index_in_dim(go, 1 - z, 0, False))
    grad_w_out = lax.ppermute(go_mine, ALL_AXES, [(zz * 8 + ss, 2 * ss + zz) for zz in range(2) for ss in range(8)])
    dqkv_tok = regroup(dqkv_pre, 5, 'regroup_dqkv')
    g_mlp = halve_sum(g_mlp, 2, 7, 'halve2')
    gq = dot_tokens(u_all, dqkv_pre).reshape(2, dim // 2, grp)
    gq_mine = lax.dynamic_index_in_dim(gq, z, 0, False) + swap_z(lax.dynamic_index_in_dim(gq, 1 - z, 0, False))
    wg = ggather(w_flat, 9).reshape(dim, 8 * grp)
    d_uattn = dot_back(dqkv_tok, wg)
    _, normed1, inv_rms1 = rms_norm(tokens, gain1)
    d_tok_norm, d_gain1 = rms_norm_grad(d_uattn, normed1, inv_rms1, gain1)
    grad_hidden = (d_resid + d_tok_norm).astype(jnp.bfloat16)

    gains = jnp.concatenate([d_gain1.reshape(2, 8, rows), d_gain2.reshape(2, 8, rows)], axis=2)
    gains_mine = lax.dynamic_index_in_dim(gains, z, 0, False) + swap_z(lax.dynamic_index_in_dim(gains, 1 - z, 0, False))
    gains_mine = jnp.broadcast_to(gains_mine[:, None, :], (8, 8, 2 * rows))
    got_q, got_g = owner(gq_mine.reshape(8, rows, grp), gains_mine, 10)
    got_q = got_q.transpose(1, 0, 2)
    grad_w_query = got_q[:, :, :grp_q].reshape(rows, 8 * grp_q)
    grad_w_key = got_q[:, :, grp_q:grp_q + grp_k].reshape(rows, 8 * grp_k)
    grad_w_value = got_q[:, :, grp_q + grp_k:].reshape(rows, 8 * grp_k)
    grad_gains = jnp.sum(got_g[:, 0, :], axis=0)
    grad_gain_attn, grad_gain_mlp = grad_gains[:rows], grad_gains[rows:]

    m1, m3, grad_w_down = halve_sum(g_mlp, 1, 8, 'halve1')
    pair = jnp.stack([m1.reshape(2, rows, ffn_half), m3.reshape(2, rows, ffn_half)], axis=1)
    keep = lax.dynamic_index_in_dim(pair, c, 0, False)
    other = swap_core(lax.dynamic_index_in_dim(pair, 1 - c, 0, False))
    grad_w_gate = join_cols(keep[0], other[0], c)
    grad_w_up = join_cols(keep[1], other[1], c)
    return (layer_out[None], grad_hidden[None], grad_gain_attn, grad_gain_mlp, grad_w_query, grad_w_key, grad_w_value, grad_w_out, grad_w_gate, grad_w_up, grad_w_down)


def solution(mesh):
    act_spec = P('dp', 'sp', None)
    pos_spec = P('dp', 'sp')
    vec_spec = P(ALL_AXES)
    mat_spec = P(ALL_AXES, None)
    in_specs = (act_spec, pos_spec, act_spec, vec_spec, vec_spec) + (mat_spec,) * 7
    out_specs = (act_spec, act_spec, vec_spec, vec_spec) + (mat_spec,) * 7
    return jax.shard_map(layer_step, mesh=mesh, in_specs=in_specs, out_specs=out_specs, check_vma=False)
```

time: 1150 us -> 830 us (0.72)
  waiting for transfers between devices: 573 us -> 16.8 us
  Pallas kernels: 101 us -> 545 us
  blocking collectives: 198 us -> 0 us
  other arithmetic: 31.5 us -> 82.2 us
  matrix products: 123 us -> 99.3 us
  between operations: 14.8 us -> 1.75 us
    pallas_call x0 -> x10, Pallas kernels: none -> 440 us  [the longest x3 124 us: halve(): pl.pallas_call(functools.partial(halve_kernel, nd, n), in_specs=[an] * n,...]
    reduce_scatter x7 -> x0, waiting for transfers between devices: 421 us -> none  [scatter_sum(): lax.psum_scatter(partial_sum, ALL_AXES, scatter_dimension=0, tiled=True)]
    all_to_all x4 -> x0, blocking collectives: 131 us -> none  [the longest x3 101 us: to_tokens(): return lax.all_to_all(head_major, 'sp', 0, 1, tiled=True)]
    all_to_all x4 -> x0, waiting for transfers between devices: 74.6 us -> none  [the longest x3 37.9 us: to_heads(): return lax.all_to_all(tok_major, 'sp', 1, 0, tiled=True)]
    all_gather x7 -> x0, waiting for transfers between devices: 72.8 us -> none  [gather_full(): return lax.all_gather(local_shard, ALL_AXES, axis=0, tiled=True)]
    unnamed x2 -> x0, blocking collectives: 66.8 us -> none
    add x3 -> x12, other arithmetic: 5.48 us -> 27.4 us  [the longest x9 23.4 us: halve_sum(): lax.dynamic_index_in_dim(g, here.bits[d], live.index(d), False) + r]
    unnamed x64 -> x109, local copies, waits for them, and re-layouts: 29.9 us -> 10.3 us
  transfers between devices with their start and end apart: 18 -> 9, of which waited for: 11 -> 1; matrix products, arithmetic and copies ran while one was open for 14% -> 15% of each run, Pallas kernels for 4% -> 20%
where the time goes in v2:
time: 830 us; the launch traced here: 825 us
  Pallas kernels  545 us (66%)
  matrix products  99.3 us (12%)
  other arithmetic  82.2 us (10%)
  local copies, waits for them, and re-layouts  74.9 us (9%)
  waiting for transfers between devices  16.8 us (2%)
    pallas_call x3, Pallas kernels, halve(): pl.pallas_call(functools.partial(halve_kernel, nd, n), in_specs=[an] * n,...  124 us
    pallas_call x1, Pallas kernels, wgather(): pl.pallas_call(wgather_kernel, in_specs=[vm] * 4, out_specs=[an] * 4, out...  88 us
    pallas_call x2, Pallas kernels, regroup(): pl.pallas_call(regroup_kernel, in_specs=[an], out_specs=an, out_shape=jax...  72.3 us
    pallas_call x1, Pallas kernels, flash_bwd(): pl.pallas_call(functools.partial(bwd_kernel, bq, bk), grid=(seq // bk,),...  60.6 us
    pallas_call x1, Pallas kernels, entry(): pl.pallas_call(entry_kernel, in_specs=[vm] * 4, out_specs=[an] * 4, out_s...  49.7 us
    pallas_call x1, Pallas kernels, flash_fwd(): pl.pallas_call(functools.partial(fwd_kernel, bq, bk), grid=(seq // bq,),...  43.7 us
    pallas_call x1, Pallas kernels, ggather(): pl.pallas_call(ggather_kernel, in_specs=[pl.BlockSpec(memory_space=pltpu....  41.2 us
    pallas_call x1, Pallas kernels, plane_gather(): pl.pallas_call(plane_gather_kernel, in_specs=[pl.BlockSpec(memory_space=p...  40.2 us
  transfers between devices with their start and end apart: 9, of which 1 were waited for; matrix products, arithmetic and copies ran while one was open for 15% of the time, Pallas kernels for 20%

profile of v2, /device:TPU:0, one launch (start us, length us, event | category | flops | bytes accessed | tf_op | source)
XLA Modules:
  0.0 825.0 jit_solution(2386649360252949246)
XLA Ops:
  4.1 49.7 %entry.1 = (bf16[8,512,1024]{2,1,0:T(8,128)(2,1)}, bf16[2,8,64,512]{3,2,1,0:T(8,128)(2,1)}, bf16[2,8,16,128]{3,2,1,0:T(8,128)(2,1)}, s32[8,4,128]{2,1,0:T(4,128)}) custom-call(bf16[512,1024]{1,0:T(8,128)(2,1)} %bitcast.184, bf16[8,64,512]{2,1,0:T(8,128)(2,1)} %bitcast.193, bf16[16,128]{1,0:T(8,128)(2,1)} %fusion.44.meta_ref, s32[4,128]{1,0:T(4,128)} %bitcast.217), custom_call_target="tpu_custom_call" | custom-call | tf_op jit(solution)/shard_map/entry/pallas_call | solution.py:354
  54.8 5.2 multiply_reduce_fusion
  60.6 2.7 multiply_convert_fusion
  63.3 7.0 fusion.57
  70.3 3.2 slice.107
  73.6 3.7 multiply_cosine_fusion
  80.2 2.7 slice.112
  89.6 43.7 %flash_fwd.1 = (bf16[4096,256]{1,0:T(8,128)(2,1)}, f32[2,4096]{1,0:T(2,128)}) custom-call(bf16[4096,256]{1,0:T(8,128)(2,1)} %copy.45.q_ref, bf16[4096,128]{1,0:T(8,128)(2,1)} %copy.46.k_ref, bf16[128,4096]{1,0:T(8,128)(2,1)} %copy.47.vt_ref), custom_call_target="tpu_custom_call" | custom-call | flops 17179869184 | bytes 8388608 | tf_op jit(solution)/shard_map/flash_fwd/pallas_call | solution.py:103
  133.3 25.1 %regroup_o.1 = bf16[512,2048]{1,0:T(8,128)(2,1)} custom-call(bf16[4096,256]{1,0:T(8,128)(2,1)} %get-tuple-element.36.src.o_ref), custom_call_target="tpu_custom_call" | custom-call | tf_op jit(solution)/shard_map/regroup_o/pallas_call | solution.py:389
  162.2 88.0 %wgather.1 = (bf16[2,2,2,2,64,1536]{5,4,3,2,1,0:T(8,128)(2,1)}, bf16[2,2,2,2,64,1536]{5,4,3,2,1,0:T(8,128)(2,1)}, bf16[2,2,2,192,1024]{4,3,2,1,0:T(8,128)(2,1)}, bf16[2,2,2,2,128,1024]{5,4,3,2,1,0:T(8,128)(2,1)}) custom-call(bf16[2,64,1536]{2,1,0:T(8,128)(2,1)} %reshape.339.w1, bf16[2,64,1536]{2,1,0:T(8,128)(2,1)} %reshape.341.w3, bf16[192,1024]{1,0:T(8,128)(2,1)} %w2.1, ...), custom_call_target="tpu_custom_call" | custom-call | tf_op jit(solution)/shard_map/wgather/pallas_call | solution.py:472
  250.2 5.3 fusion.26
  257.3 7.9 fusion.1
  266.1 41.2 %ggather.1 = bf16[2,2,2,2,64,4096]{5,4,3,2,1,0:T(8,128)(2,1)} custom-call(bf16[64,4096]{1,0:T(8,128)(2,1)} %bitcast.201), custom_call_target="tpu_custom_call" | custom-call | tf_op jit(solution)/shard_map/ggather/pallas_call | solution.py:525
  307.3 11.5 %copy.55 = bf16[1024,4096]{1,0:T(8,128)(2,1)} copy(bf16[1024,4096]{0,1:T(8,128)(2,1)} %bitcast.170) | data formatting | bytes 16777216 | tf_op jit(solution)/shard_map/dot_general | solution.py:558
  318.8 4.5 copy.64
  324.2 8.8 %fusion.51 = f32[1024,1536]{1,0:T(8,128)} fusion(bf16[1024,1536]{1,0:T(8,128)(2,1)} %bitcast.224, bf16[512,1024]{1,0:T(8,128)(2,1)} %collective-permute-done, bf16[512,1024]{1,0:T(8,128)(2,1)} %fusion.20), kind=kOutput, calls=%fused_computation.130 | convolution fusion | flops 3225419776 | bytes 11534336 | tf_op jit(solution)/shard_map/dot_general | solution.py:566
  332.9 7.1 fusion.50
  340.0 9.2 %multiply_convert_fusion.1 = (bf16[1024,1536]{1,0:T(8,128)(2,1)S(1)}, bf16[1024,1536]{1,0:T(8,128)(2,1)S(1)}, bf16[1024,1536]{1,0:T(8,128)(2,1)S(1)}) fusion(f32[1024,1536]{1,0:T(8,128)} %fusion.51, f32[1024,1536]{1,0:T(8,128)} %fusion.50, bf16[1536,1024]{1,0:T(8,128)(2,1)S(1)} %bitcast.220, bf16[512,1024]{1,0:T(8,128)(2,1)} %collective-permute-done.2, ...), kind=kOutput, calls=%fused_computation.5 | convolution fusion | flops 3249012736 | bytes 27262976 | tf_op jit(solution)/shard_map/dot_general | solution.py:562
  349.3 3.4 fusion.59
  352.7 3.5 convolution_add_fusion
  358.4 7.0 fusion.49
  365.4 7.1 fusion.48
  372.5 7.2 fusion.28
  379.7 70.3 %halve3.1 = (f32[2,2,128,1536]{3,2,1,0:T(8,128)}, f32[2,2,128,1536]{3,2,1,0:T(8,128)}, f32[2,2,192,1024]{3,2,1,0:T(8,128)}) custom-call(f32[2,2,2,128,1536]{4,3,2,1,0:T(8,128)} %bitcast.175, f32[2,2,2,128,1536]{4,3,2,1,0:T(8,128)} %bitcast.173, f32[2,2,2,192,1024]{4,3,2,1,0:T(8,128)} %bitcast.177), custom_call_target="tpu_custom_call" | custom-call | tf_op jit(solution)/shard_map/halve3/pallas_call | solution.py:498
  450.0 5.3 bitcast_add_fusion.2.refs_0_
  455.4 4.8 bitcast_add_fusion.1.refs_1_
  462.8 35.9 %halve2.1 = (f32[2,128,1536]{2,1,0:T(8,128)}, f32[2,128,1536]{2,1,0:T(8,128)}, f32[2,192,1024]{2,1,0:T(8,128)}) custom-call(f32[2,2,128,1536]{3,2,1,0:T(8,128)} %bitcast_add_fusion.2.refs_0_, f32[2,2,128,1536]{3,2,1,0:T(8,128)} %bitcast_add_fusion.1.refs_1_, f32[2,2,192,1024]{3,2,1,0:T(8,128)} %bitcast_add_fusion.refs_2_), custom_call_target="tpu_custom_call" | custom-call | tf_op jit(solution)/shard_map/halve2/pallas_call | solution.py:498
  498.7 3.0 bitcast_add_fusion.5.refs_0_
  506.0 18.3 %halve1.1 = (f32[128,1536]{1,0:T(8,128)}, f32[128,1536]{1,0:T(8,128)}, f32[192,1024]{1,0:T(8,128)}) custom-call(f32[2,128,1536]{2,1,0:T(8,128)} %bitcast_add_fusion.5.refs_0_, f32[2,128,1536]{2,1,0:T(8,128)} %bitcast_add_fusion.4.refs_1_, f32[2,192,1024]{2,1,0:T(8,128)} %bitcast_add_fusion.3.refs_2_), custom_call_target="tpu_custom_call" | custom-call | tf_op jit(solution)/shard_map/halve1/pallas_call | solution.py:498
  528.1 3.4 fusion.58
  548.9 3.1 fusion.25
  552.3 6.1 fusion.52
  558.4 40.2 %gather_dh.1 = bf16[8,512,1024]{2,1,0:T(8,128)(2,1)} custom-call(bf16[512,1024]{1,0:T(8,128)(2,1)} %get-tuple-element.59.src), custom_call_target="tpu_custom_call" | custom-call | tf_op jit(solution)/shard_map/gather_dh/pallas_call | solution.py:305
  598.6 7.1 convolution_convert_fusion.d_ref
  605.7 60.6 %flash_bwd.1 = bf16[4096,512]{1,0:T(8,128)(2,1)} custom-call(bf16[4096,256]{1,0:T(8,128)(2,1)} %copy.45.q_ref, bf16[4096,256]{1,0:T(8,128)(2,1)} %get-tuple-element.36.src.o_ref, bf16[4096,256]{1,0:T(8,128)(2,1)} %convolution_convert_fusion.d_ref, bf16[4096,128]{1,0:T(8,128)(2,1)} %copy.46.k_ref, bf16[128,4096]{1,0:T(8,128)(2,1)} %get-tuple-element.68.kt_ref, ...), custom_call_target="tpu_custom_call" | custom-call | flops 21474836480 | bytes 16777216 | tf_op jit(solution)/shard_map/flash_bwd/pallas_call | solution.py:186
  668.6 5.0 slice_convert_fusion
  673.6 6.8 copy.52
  680.5 3.8 add_convert_fusion
  684.7 2.9 copy.53
  687.5 4.5 pad_maximum_fusion.src
  692.1 47.3 %regroup_dqkv.1 = bf16[512,4096]{1,0:T(8,128)(2,1)} custom-call(bf16[4096,512]{1,0:T(8,128)(2,1)} %pad_maximum_fusion.src), custom_call_target="tpu_custom_call" | custom-call | tf_op jit(solution)/shard_map/regroup_dqkv/pallas_call | solution.py:389
  739.4 7.6 fusion.3
  749.4 5.9 fusion.60
  757.0 9.7 %fusion.17 = (f32[1024]{0:T(1024)S(1)}, f32[512]{0:T(512)S(1)}, f32[512,1024]{1,0:T(8,128)}) fusion(f32[512]{0:T(512)S(1)} %copy-done.41, bf16[1,512,1024]{2,1,0:T(8,128)(2,1)S(1)} %copy-done.16, f32[1024]{0:T(1024)S(1)} %copy-done.39, bf16[512,4096]{1,0:T(8,128)(2,1)S(1)} %copy-done.23, bf16[1024,4096]{1,0:T(8,128)(2,1)} %bitcast.187), kind=kOutput, calls=%fused_computation.42 | convolution fusion | flops 4298635776 | bytes 15740928 | tf_op jit(solution)/shard_map/dot_general | solution.py:562
  768.2 16.8 %collective-permute-done.6 = f32[128,1024]{1,0:T(8,128)} collective-permute-done((f32[128,1024]{1,0:T(8,128)}, f32[128,1024]{1,0:T(8,128)}, u32[]{:S(2)}, u32[]{:S(2)}) %collective-permute-start.6) | collective-permute-done | bytes 524320 | tf_op jit(solution)/shard_map/ppermute | solution.py:574
  787.0 3.3 fusion.31
  790.3 2.7 bitcast_add_fusion.6
  793.6 24.5 %owner.1 = (f32[8,64,512]{2,1,0:T(8,128)}, f32[8,8,128]{2,1,0:T(8,128)}) custom-call(f32[8,64,512]{2,1,0:T(8,128)} %bitcast.192, f32[8,8,128]{2,1,0:T(8,128)} %broadcast_in_dim.8.b), custom_call_target="tpu_custom_call" | custom-call | tf_op jit(solution)/shard_map/owner/pallas_call | solution.py:549
  (192 shorter events, 69.8 us)
Async XLA Ops:
  54.8 202.5 %copy-start.38 = (f32[1024]{0:T(1024)}, f32[1024]{0:T(1024)S(1)}, u32[]{:S(2)}) copy-start(f32[1024]{0:T(1024)S(1)} %reshape.362) | copy-start | bytes 12292
  54.8 5.8 copy-start.2
  70.3 3.2 copy-start.40
  88.2 45.0 %copy-start.24 = (bf16[4096,128]{1,0:T(8,128)(2,1)}, bf16[4096,128]{1,0:T(8,128)(2,1)S(1)}, u32[]{:S(2)}) copy-start(bf16[4096,128]{1,0:T(8,128)(2,1)S(1)} %copy.65.v_ref) | copy-start | bytes 3145732
  133.3 25.1 %copy-start.36 = (bf16[64,3072]{1,0:T(8,128)(2,1)S(1)}, bf16[64,3072]{1,0:T(8,128)(2,1)}, u32[]{:S(2)}) copy-start(bf16[64,3072]{1,0:T(8,128)(2,1)} %param.21) | copy-start | bytes 1179652
  133.3 27.0 %copy-start.37 = (bf16[64,3072]{1,0:T(8,128)(2,1)S(1)}, bf16[64,3072]{1,0:T(8,128)(2,1)}, u32[]{:S(2)}) copy-start(bf16[64,3072]{1,0:T(8,128)(2,1)} %param.22) | copy-start | bytes 1179652
  159.0 91.1 %copy-start.15 = (bf16[1,512,1024]{2,1,0:T(8,128)(2,1)S(1)}, bf16[1,512,1024]{2,1,0:T(8,128)(2,1)}, u32[]{:S(2)}) copy-start(bf16[1,512,1024]{2,1,0:T(8,128)(2,1)} %param.12) | copy-start | bytes 3145732
  255.4 9.8 %copy-start.13 = (bf16[512,1024]{1,0:T(8,128)(2,1)}, bf16[512,1024]{1,0:T(8,128)(2,1)S(1)}, u32[]{:S(2)}) copy-start(bf16[512,1024]{1,0:T(8,128)(2,1)S(1)} %get-tuple-element.90) | copy-start | bytes 3145732
  256.8 67.4 %collective-permute-start = (bf16[512,1024]{1,0:T(8,128)(2,1)}, bf16[512,1024]{1,0:T(8,128)(2,1)}, u32[]{:S(2)}, u32[]{:S(2)}) collective-permute-start(bf16[512,1024]{1,0:T(8,128)(2,1)} %fusion.20), channel_id=1, source_target_pairs={{0,1},{1,0},{2,3},{3,2},{4,5},{5,4},{6,7},{7,6},{8,9},{9,8},{10,11... | collective-permute-start | bytes 3145736 | tf_op jit(solution)/shard_map/ppermute | solution.py:570
  257.1 82.9 %collective-permute-start.2 = (bf16[512,1024]{1,0:T(8,128)(2,1)}, bf16[512,1024]{1,0:T(8,128)(2,1)}, u32[]{:S(2)}, u32[]{:S(2)}) collective-permute-start(bf16[512,1024]{1,0:T(8,128)(2,1)} %bitcast.18), channel_id=1, source_target_pairs={{0,1},{1,0},{2,3},{3,2},{4,5},{5,4},{6,7},{7,6},{8,9},{9,8},{10,11... | collective-permute-start | bytes 3145736 | tf_op jit(solution)/shard_map/ppermute | solution.py:570
  257.3 7.9 copy-start.26
  324.2 8.8 %copy-start.44 = (bf16[2,2,2,2,64,1536]{5,4,3,2,1,0:T(8,128)(2,1)S(1)}, bf16[2,2,2,2,64,1536]{5,4,3,2,1,0:T(8,128)(2,1)}, u32[]{:S(2)}) copy-start(bf16[2,2,2,2,64,1536]{5,4,3,2,1,0:T(8,128)(2,1)} %get-tuple-element.39) | copy-start | bytes 9437188
  332.9 7.1 copy-start.42
  340.0 9.2 %copy-start.45 = (bf16[2,2,2,2,64,1536]{5,4,3,2,1,0:T(8,128)(2,1)S(1)}, bf16[2,2,2,2,64,1536]{5,4,3,2,1,0:T(8,128)(2,1)}, u32[]{:S(2)}) copy-start(bf16[2,2,2,2,64,1536]{5,4,3,2,1,0:T(8,128)(2,1)} %get-tuple-element.38) | copy-start | bytes 9437188
  349.3 23.2 %copy-start.47 = (bf16[1024,1536]{1,0:T(8,128)(2,1)}, bf16[1024,1536]{1,0:T(8,128)(2,1)S(1)}, u32[]{:S(2)}) copy-start(bf16[1024,1536]{1,0:T(8,128)(2,1)S(1)} %get-tuple-element.63) | copy-start | bytes 9437188
  356.2 9.1 %copy-start.11 = (f32[1024,1024]{1,0:T(8,128)}, f32[1024,1024]{1,0:T(8,128)S(1)}, u32[]{:S(2)}) copy-start(f32[1024,1024]{1,0:T(8,128)S(1)} %convolution_add_fusion) | copy-start | bytes 12582916
  358.0 190.9 %collective-permute-start.3 = (f32[512,1024]{1,0:T(8,128)}, f32[512,1024]{1,0:T(8,128)}, u32[]{:S(2)}, u32[]{:S(2)}) collective-permute-start(f32[512,1024]{1,0:T(8,128)} %slice.116), channel_id=1, source_target_pairs={{0,1},{1,0},{2,3},{3,2},{4,5},{5,4},{6,7},{7,6},{8,9},{9,8},{10,11... | collective-permute-start | bytes 6291464 | tf_op jit(solution)/shard_map/ppermute | solution.py:570
  450.0 5.4 copy-start.6
  450.0 10.1 %slice-start = ((s8[6291456]{0:T(1024)(128)(4,1)}), s8[4194304]{0:T(1024)(128)(4,1)S(1)}, s32[]{:S(2)}) async-start(s8[6291456]{0:T(1024)(128)(4,1)} %bitcast.178), calls=%async_computation | async-start | bytes 8388608
  455.4 4.8 slice-start.1
  455.4 4.8 copy-start.27
  462.8 35.9 %copy-start.3 = (f32[2,2,128,1536]{3,2,1,0:T(8,128)S(1)}, f32[2,2,128,1536]{3,2,1,0:T(8,128)}, u32[]{:S(2)}) copy-start(f32[2,2,128,1536]{3,2,1,0:T(8,128)} %bitcast_add_fusion.2.refs_0_) | copy-start | bytes 9437188
  498.6 3.0 copy-start.4
  506.0 18.3 %copy-start.10 = (f32[2,128,1536]{2,1,0:T(8,128)S(1)}, f32[2,128,1536]{2,1,0:T(8,128)}, u32[]{:S(2)}) copy-start(f32[2,128,1536]{2,1,0:T(8,128)} %bitcast_add_fusion.5.refs_0_) | copy-start | bytes 4718596
  506.0 19.7 %copy-start.9 = (f32[2,128,1536]{2,1,0:T(8,128)S(1)}, f32[2,128,1536]{2,1,0:T(8,128)}, u32[]{:S(2)}) copy-start(f32[2,128,1536]{2,1,0:T(8,128)} %bitcast_add_fusion.4.refs_1_) | copy-start | bytes 4718596
  524.3 3.8 copy-start.48
  528.1 11.4 %collective-permute-start.8 = (f32[2,64,1536]{2,1,0:T(8,128)}, f32[2,64,1536]{2,1,0:T(8,128)}, u32[]{:S(2)}, u32[]{:S(2)}) collective-permute-start(f32[2,64,1536]{2,1,0:T(8,128)} %get-tuple-element.71), channel_id=1, source_target_pairs={{0,1},{1,0},{2,3},{3,2},{4,5},{5,4},{6,7},{7,6},{8,9},{9,8},{10,11... | collective-permute-start | bytes 2359304 | tf_op jit(solution)/shard_map/ppermute | solution.py:570
  533.5 3.9 copy-start.8
  535.0 17.0 %collective-permute-start.1 = (f32[512,1024]{1,0:T(8,128)}, f32[512,1024]{1,0:T(8,128)}, u32[]{:S(2)}, u32[]{:S(2)}) collective-permute-start(f32[512,1024]{1,0:T(8,128)} %slice.114), channel_id=1, source_target_pairs={{0,1},{1,0},{2,3},{3,2},{4,5},{5,4},{6,7},{7,6},{8,9},{9,8},{10,11... | collective-permute-start | bytes 6291464 | tf_op jit(solution)/shard_map/ppermute | solution.py:570
  545.6 3.3 copy-start.14
  548.9 3.4 copy-start.12
  673.6 6.8 copy-start.18
  673.6 6.8 copy-start.20
  692.1 47.3 %copy-start.7 = (bf16[4096,384]{1,0:T(8,128)(2,1)S(1)}, bf16[4096,384]{1,0:T(8,128)(2,1)}, u32[]{:S(2)}) copy-start(bf16[4096,384]{1,0:T(8,128)(2,1)} %copy.53) | copy-start | bytes 9437188
  739.4 10.0 %copy-start.30 = (bf16[256,4096]{1,0:T(8,128)(2,1)S(1)}, bf16[256,4096]{1,0:T(8,128)(2,1)}, u32[]{:S(2)}) copy-start(bf16[256,4096]{1,0:T(8,128)(2,1)} %copy.64) | copy-start | bytes 6291460
  747.0 8.3 %copy-start.28 = (f32[2,512,512]{2,1,0:T(8,128)}, f32[2,512,512]{2,1,0:T(8,128)S(1)}, u32[]{:S(2)}) copy-start(f32[2,512,512]{2,1,0:T(8,128)S(1)} %fusion.3) | copy-start | bytes 6291460
  748.1 42.2 %collective-permute-start.4 = (f32[512,512]{1,0:T(8,128)}, f32[512,512]{1,0:T(8,128)}, u32[]{:S(2)}, u32[]{:S(2)}) collective-permute-start(f32[512,512]{1,0:T(8,128)} %dynamic-slice_bitcast_fusion), channel_id=1, source_target_pairs={{0,8},{8,0},{1,9},{9,1},{2,10},{10,2},{3,11},{11,3},{4,12},{12,4},... | collective-permute-start | bytes 3145736 | tf_op jit(solution)/shard_map/ppermute | solution.py:574
  749.4 7.7 copy-start.16
  749.4 7.7 copy-start.23
  749.4 7.7 copy-start.39
  749.4 7.7 copy-start.41
  756.2 28.7 %collective-permute-start.6 = (f32[128,1024]{1,0:T(8,128)}, f32[128,1024]{1,0:T(8,128)}, u32[]{:S(2)}, u32[]{:S(2)}) collective-permute-start(f32[128,1024]{1,0:T(8,128)} %dynamic-slice_bitcast_fusion.1), channel_id=1, source_target_pairs={{0,8},{8,0},{1,9},{9,1},{2,10},{10,2},{3,11},{11,3},{4,12},{12,4},... | collective-permute-start | bytes 1572872 | tf_op jit(solution)/shard_map/ppermute | solution.py:574
  757.0 29.9 %copy-start.21 = (f32[512,1024]{1,0:T(8,128)S(1)}, f32[512,1024]{1,0:T(8,128)}, u32[]{:S(2)}) copy-start(f32[512,1024]{1,0:T(8,128)} %get-tuple-element.60) | copy-start | bytes 6291460
  766.9 23.3 %collective-permute-start.5 = (f32[8,128]{1,0:T(8,128)S(1)}, f32[8,128]{1,0:T(8,128)S(1)}, u32[]{:S(2)}, u32[]{:S(2)}) collective-permute-start(f32[8,128]{1,0:T(8,128)S(1)} %fusion.40), channel_id=1, source_target_pairs={{0,8},{8,0},{1,9},{9,1},{2,10},{10,2},{3,11},{11,3},{4,12},{12,4},... | collective-permute-start | bytes 12296 | tf_op jit(solution)/shard_map/ppermute | solution.py:574
  786.2 4.1 collective-permute-start.7
  787.0 3.4 copy-start.29
  793.0 30.9 %copy-start.35 = (f32[128,1024]{1,0:T(8,128)S(1)}, f32[128,1024]{1,0:T(8,128)}, u32[]{:S(2)}) copy-start(f32[128,1024]{1,0:T(8,128)} %copy-done.34) | copy-start | bytes 1572868
  793.0 31.7 %copy-start.1 = (bf16[64,1024]{1,0:T(8,128)(2,1)S(1)}, bf16[64,1024]{1,0:T(8,128)(2,1)}, u32[]{:S(2)}) copy-start(bf16[64,1024]{1,0:T(8,128)(2,1)} %param.18) | copy-start | bytes 393220
  (12 other events, 24.8 us)

commit v3 on v1

v3 whole, which is shorter than its diff:
```python
import functools
import math

import jax
import jax.numpy as jnp
from jax import lax
from jax.experimental import pallas as pl
from jax.experimental.pallas import tpu as pltpu
from jax.sharding import PartitionSpec as P

HEAD_DIM = 128
ROPE_BASE = 10000.0
NORM_EPS = 1e-5
ATTN_SCALE = HEAD_DIM ** -0.5
ALL_AXES = ('dp', 'sp')


def rope_tables(pos_ids):
    inv_freq = ROPE_BASE ** (-(jnp.arange(HEAD_DIM // 2, dtype=jnp.float32) * (2.0 / HEAD_DIM)))
    angles = pos_ids.astype(jnp.float32)[..., None] * inv_freq
    return jnp.cos(angles), jnp.sin(angles)


def rms_norm(values, gain_vec):
    vals32 = values.astype(jnp.float32)
    inv_rms = lax.rsqrt(jnp.mean(vals32 * vals32, axis=-1, keepdims=True) + NORM_EPS)
    normed = vals32 * inv_rms
    return (normed * gain_vec.astype(jnp.float32)).astype(jnp.bfloat16), normed, inv_rms


def rms_norm_grad(d_out, normed, inv_rms, gain_vec):
    d_normed = d_out * gain_vec.astype(jnp.float32)
    grad_gain = jnp.sum(d_out * normed, axis=0)
    grad_in = inv_rms * (d_normed - normed * jnp.mean(d_normed * normed, axis=-1, keepdims=True))
    return grad_in, grad_gain


MESH = pl.DeviceIdType.MESH
ORDERS = ('xyz', 'yzx', 'zxy')


class Spot:
    def __init__(self):
        self.z = lax.axis_index('dp')
        self.s = lax.axis_index('sp')
        self.y = self.s // 4
        self.x = (self.s // 2) % 2
        self.c = self.s % 2
        self.bits = {'z': self.z, 'y': self.y, 'x': self.x}

    def peer(self, dim):
        if dim == 'z':
            return (1 - self.z, self.s)
        if dim == 'y':
            return (self.z, self.s + 4 - 8 * self.y)
        if dim == 'x':
            return (self.z, self.s + 2 - 4 * self.x)
        return (self.z, self.s + 1 - 2 * self.c)

    def others(self):
        return [(self.z, (self.s + t) % 8) for t in range(1, 8)]

    def region(self, freed, flipped=''):
        return tuple(slice(None) if d in freed else (1 - self.bits[d] if d in flipped else self.bits[d]) for d in 'zyx')


def greet(targets):
    bar = pltpu.get_barrier_semaphore()
    for t in targets:
        pl.semaphore_signal(bar, inc=1, device_id=t, device_id_type=MESH)
    pl.semaphore_wait(bar, len(targets))


class Wires:
    def __init__(self, send_sem, recv_sem):
        self.send_sem, self.recv_sem, self.n = send_sem, recv_sem, 0

    def copy(self, src, dst, target):
        i = self.n
        self.n += 1
        return pltpu.make_async_remote_copy(src_ref=src, dst_ref=dst, send_sem=self.send_sem.at[i], recv_sem=self.recv_sem.at[i], device_id=target, device_id_type=MESH)


class CubeGather:
    def __init__(self, here, wires, jobs):
        self.stages = [[], [], []]
        self.need = [[], []]
        self.rest = []
        for out, suffix, (a, b, e) in jobs:
            def mk(freed, flipped, d):
                reg = here.region(freed, flipped) + suffix
                return wires.copy(out.at[reg], out.at[reg], here.peer(d))
            first = [mk('', '', d) for d in (a, b, e)]
            second = [mk('', a, d) for d in (b, e)]
            third = [mk(a, b, e)]
            self.stages[0] += first
            self.stages[1] += second
            self.stages[2] += third
            self.need[0].append(first[0])
            self.need[1] += [first[1], second[0]]
            self.rest += [first[2], second[1]] + third

    def start(self, i):
        for c in self.need[i - 1] if i else ():
            c.wait_recv()
        for c in self.stages[i]:
            c.start()

    def arrive(self):
        for c in self.rest:
            c.wait_recv()

    def drain(self):
        for st in self.stages:
            for c in st:
                c.wait_send()


def col_chunks(cols, parts):
    n, out, off = cols // 128, [], 0
    for p in range(parts, 0, -1):
        w = -(-n // p)
        out.append((off, w * 128))
        off += w * 128
        n -= w
    return out


def cube_targets(here):
    return [here.peer(d) for d in 'xyzc']


def comm_params(cid, **kw):
    return pltpu.CompilerParams(collective_id=cid, has_side_effects=True, **kw)


def busy(us):
    return pl.CostEstimate(flops=int(us * 1e8), bytes_accessed=1 << 20, transcendentals=0)


NW = 2 + 6 * 6 + 1


class WeightGather:
    def __init__(self, here, wires, local_sem, ins, outs):
        w1, w3, w2, wo = ins
        o1, o3, o2, oo = outs
        c, zyx, nc = here.c, here.region(''), here.peer('c')
        self.pre = [wires.copy(w1.at[1 - c], o1.at[zyx + (c,)], nc), wires.copy(w3.at[1 - c], o3.at[zyx + (c,)], nc)]
        self.loc = [pltpu.make_async_copy(w1.at[c], o1.at[zyx + (c,)], local_sem.at[0]),
                    pltpu.make_async_copy(w3.at[c], o3.at[zyx + (c,)], local_sem.at[1]),
                    pltpu.make_async_copy(w2, o2.at[zyx], local_sem.at[2]),
                    pltpu.make_async_copy(wo, oo.at[zyx + (c,)], local_sem.at[3])]
        jobs = [(o1, (), ORDERS[0]), (o3, (), ORDERS[1]), (o2, (), ORDERS[2])]
        for (off, n), order in zip(col_chunks(wo.shape[1], 3), ORDERS):
            jobs.append((oo, (c, slice(None), slice(off, off + n)), order))
        self.cube = CubeGather(here, wires, jobs)
        self.post = wires.copy(oo.at[:, :, :, c], oo.at[:, :, :, c], nc)

    def begin(self):
        for c in self.pre + self.loc:
            c.start()
        for c in self.loc:
            c.wait()
        for c in self.pre:
            c.wait()
        self.cube.start(0)

    def end(self):
        self.cube.arrive()
        self.post.start()
        self.post.wait()
        self.cube.drain()


def gathered(ws):
    return [jax.ShapeDtypeStruct((2, 2, 2, *w.shape), w.dtype) if k < 3 else jax.ShapeDtypeStruct((2, 2, 2, 2, *w.shape), w.dtype) for k, w in enumerate(ws)]


def halve_copies(here, wires, nd, ins, outs):
    cs = []
    for i, (a, o) in enumerate(zip(ins, outs)):
        order = ORDERS[i % 3]
        d = order[nd - 1]
        reg = tuple(1 - here.bits[d] if e == d else slice(None) for e in 'zyx' if e in order[:nd])
        cs.append(wires.copy(a.at[reg], o, here.peer(d)))
    return cs


def halve_shapes(arrs, nd):
    return [jax.ShapeDtypeStruct((*((2,) * (nd - 1)), *a.shape[nd:]), a.dtype) for a in arrs]


def halve_add(arrs, got, nd):
    here = Spot()
    out = []
    for i, (g, r) in enumerate(zip(arrs, got)):
        order = ORDERS[i % 3]
        live = [d for d in 'zyx' if d in order[:nd]]
        d = order[nd - 1]
        out.append(lax.dynamic_index_in_dim(g, here.bits[d], live.index(d), False) + r)
    return out


def proj_kernel(nrot, x_ref, g_ref, w_ref, cos_ref, sin_ref, u_ref, q_ref, k_ref, v_ref, kt_ref, vt_ref):
    x = x_ref[...].astype(jnp.float32)
    inv = lax.rsqrt(jnp.mean(x * x, axis=-1, keepdims=True) + NORM_EPS)
    u = (x * inv * g_ref[0:1, :].astype(jnp.float32)).astype(jnp.bfloat16)
    u_ref[...] = u
    cos, sin = cos_ref[...], sin_ref[...]
    for h in range(nrot + 2):
        t = jnp.dot(u, w_ref[:, h * HEAD_DIM:(h + 1) * HEAD_DIM], preferred_element_type=jnp.float32)
        if h <= nrot:
            t = t * cos + pltpu.roll(t, HEAD_DIM // 2, 1) * sin
        if h < nrot:
            q_ref[:, h * HEAD_DIM:(h + 1) * HEAD_DIM] = t.astype(jnp.bfloat16)
        else:
            n_ref, t_ref = (k_ref, kt_ref) if h == nrot else (v_ref, vt_ref)
            n_ref[...] = t.astype(jnp.bfloat16)
            t_ref[...] = t.T.astype(jnp.bfloat16)


def project(x, gain, w, cosw, sinw, bt=512):
    seq, dim = x.shape
    grp = w.shape[1]
    nq = grp // HEAD_DIM - 2
    row = lambda i: (i, 0)
    whole = lambda i: (0, 0)
    bf = jnp.bfloat16
    return pl.pallas_call(
        functools.partial(proj_kernel, nq), grid=(seq // bt,),
        in_specs=[pl.BlockSpec((bt, dim), row), pl.BlockSpec((16, dim), whole), pl.BlockSpec((dim, grp), whole),
                  pl.BlockSpec((bt, HEAD_DIM), row), pl.BlockSpec((bt, HEAD_DIM), row)],
        out_specs=[pl.BlockSpec((bt, dim), row), pl.BlockSpec((bt, nq * HEAD_DIM), row), pl.BlockSpec((bt, HEAD_DIM), row), pl.BlockSpec((bt, HEAD_DIM), row),
                   pl.BlockSpec((HEAD_DIM, bt), lambda i: (0, i)), pl.BlockSpec((HEAD_DIM, bt), lambda i: (0, i))],
        out_shape=[jax.ShapeDtypeStruct((seq, dim), bf), jax.ShapeDtypeStruct((seq, nq * HEAD_DIM), bf), jax.ShapeDtypeStruct((seq, HEAD_DIM), bf),
                   jax.ShapeDtypeStruct((seq, HEAD_DIM), bf), jax.ShapeDtypeStruct((HEAD_DIM, seq), bf), jax.ShapeDtypeStruct((HEAD_DIM, seq), bf)],
        cost_estimate=pl.CostEstimate(flops=2 * seq * dim * grp, bytes_accessed=32 << 20, transcendentals=0),
        compiler_params=pltpu.CompilerParams(vmem_limit_bytes=48 << 20), name="project",
    )(x, gain, w, cosw, sinw)


LOG2E = math.log2(math.e)
SCALE2 = ATTN_SCALE * LOG2E
NT = (((1,), (1,)), ((), ()))
NN = (((1,), (0,)), ((), ()))
BIG = -1e30


def fwd_kernel(bq, bk, q_ref, k_ref, vt_ref, w1, w3, w2, wo, o_ref, lse_ref, o1, o3, o2, oo, send_sem, recv_sem, local_sem):
    i = pl.program_id(0)
    last = pl.num_programs(0) - 1
    here = Spot()
    carry_over = WeightGather(here, Wires(send_sem, recv_sem), local_sem, (w1, w3, w2, wo), (o1, o3, o2, oo))

    @pl.when(i == 0)
    def _():
        greet(cube_targets(here))
        carry_over.begin()

    @pl.when(i == 2)
    def _():
        carry_over.cube.start(1)

    heads = q_ref.shape[1] // HEAD_DIM
    qs = [q_ref[:, h * HEAD_DIM:(h + 1) * HEAD_DIM] for h in range(heads)]

    def block(j, carry, masked):
        rows = pl.ds(pl.multiple_of(j * bk, bk), bk)
        k = k_ref[rows, :]
        vt = vt_ref[:, rows]
        out = []
        for h in range(heads):
            m, l, acc = carry[h]
            s = lax.dot_general(k, qs[h], NT, preferred_element_type=jnp.float32)
            if masked:
                kpos = j * bk + lax.broadcasted_iota(jnp.int32, (bk, bq), 0)
                qpos = i * bq + lax.broadcasted_iota(jnp.int32, (bk, bq), 1)
                s = jnp.where(qpos >= kpos, s, BIG)
            m_new = jnp.maximum(m, jnp.max(s, axis=0, keepdims=True))
            p = jnp.exp2((s - m_new) * SCALE2)
            alpha = jnp.exp2((m - m_new) * SCALE2)
            l = l * alpha + jnp.sum(p, axis=0, keepdims=True)
            acc = acc * alpha + lax.dot_general(vt, p.astype(jnp.bfloat16), NN, preferred_element_type=jnp.float32)
            out.append((m_new, l, acc))
        return tuple(out)

    init = tuple((jnp.full((1, bq), BIG, jnp.float32), jnp.zeros((1, bq), jnp.float32), jnp.zeros((HEAD_DIM, bq), jnp.float32)) for _ in range(heads))
    full = i * bq // bk
    carry = lax.fori_loop(0, full, lambda j, c: block(j, c, False), init)
    for d in range(max(1, bq // bk)):
        carry = block(full + d, carry, True)
    for h in range(heads):
        m, l, acc = carry[h]
        o = acc / l
        o_ref[:, h * HEAD_DIM:(h + 1) * HEAD_DIM] = o.T.astype(jnp.bfloat16)
        lse_ref[h:h + 1, :] = m * SCALE2 + jnp.log2(l)

    @pl.when(i == last)
    def _():
        carry_over.cube.start(2)
        carry_over.end()


def flash_fwd(q, k, vt, ws, cid, bq=1024, bk=512):
    seq, width = q.shape
    heads = width // HEAD_DIM
    vm = pl.BlockSpec(memory_space=pltpu.VMEM)
    an = pl.BlockSpec(memory_space=pl.ANY)
    return pl.pallas_call(
        functools.partial(fwd_kernel, bq, bk),
        grid=(seq // bq,),
        in_specs=[pl.BlockSpec((bq, width), lambda i: (i, 0)),
                  pl.BlockSpec((seq, HEAD_DIM), lambda i: (0, 0)),
                  pl.BlockSpec((HEAD_DIM, seq), lambda i: (0, 0))] + [vm] * 4,
        out_specs=[pl.BlockSpec((bq, width), lambda i: (i, 0)),
                   pl.BlockSpec((heads, bq), lambda i: (0, i))] + [an] * 4,
        out_shape=[jax.ShapeDtypeStruct((seq, width), jnp.bfloat16), jax.ShapeDtypeStruct((heads, seq), jnp.float32)] + gathered(ws),
        scratch_shapes=[pltpu.SemaphoreType.DMA((NW,)), pltpu.SemaphoreType.DMA((NW,)), pltpu.SemaphoreType.DMA((4,))],
        cost_estimate=pl.CostEstimate(flops=2 * seq * seq * width * 2, bytes_accessed=8 << 20, transcendentals=seq * seq),
        compiler_params=comm_params(cid, vmem_limit_bytes=56 << 20),
        name="flash_fwd",
    )(q, k, vt, *ws)


def bwd_kernel(bq, bk, q_ref, o_ref, d_ref, k_ref, kt_ref, v_ref, lse_ref, cos_ref, sin_ref, g1, g3, g2, out_ref, r1, r3, r2, dqt, dka, dva, rd, send_sem, recv_sem):
    j = pl.program_id(0)
    nk = pl.num_programs(0)
    seq, width = q_ref.shape
    heads = width // HEAD_DIM
    nq = seq // bq
    k = k_ref[...]
    v = v_ref[...]
    kt = kt_ref[...]
    here = Spot()
    carry_over = halve_copies(here, Wires(send_sem, recv_sem), 3, (g1, g3, g2), (r1, r3, r2))

    def turned(t, rows):
        t = t.astype(jnp.bfloat16).astype(jnp.float32)
        return (t * cos_ref[rows, :] - pltpu.roll(t, HEAD_DIM // 2, 1) * sin_ref[rows, :]).astype(jnp.bfloat16)

    @pl.when(j == 0)
    def _():
        greet([here.peer(d) for d in 'xyz'])
        for cp in carry_over:
            cp.start()
        dqt[...] = jnp.zeros_like(dqt)

        def prep(i, c):
            rows = pl.ds(pl.multiple_of(i * bq, bq), bq)
            for h in range(heads):
                cols = slice(h * HEAD_DIM, (h + 1) * HEAD_DIM)
                prod = o_ref[rows, cols].astype(jnp.float32) * d_ref[rows, cols].astype(jnp.float32)
                rd[h:h + 1, rows] = jnp.sum(prod.T, axis=0, keepdims=True)
            return c
        lax.fori_loop(0, nq, prep, 0)

    dka[...] = jnp.zeros_like(dka)
    dva[...] = jnp.zeros_like(dva)

    def block(i, masked):
        rows = pl.ds(pl.multiple_of(i * bq, bq), bq)
        for h in range(heads):
            cols = slice(h * HEAD_DIM, (h + 1) * HEAD_DIM)
            q = q_ref[rows, cols]
            d = d_ref[rows, cols]
            s = lax.dot_general(k, q, NT, preferred_element_type=jnp.float32)
            dp = lax.dot_general(v, d, NT, preferred_element_type=jnp.float32)
            p = jnp.exp2(s * SCALE2 - lse_ref[h:h + 1, rows])
            if masked:
                kpos = j * bk + lax.broadcasted_iota(jnp.int32, (bk, bq), 0)
                qpos = i * bq + lax.broadcasted_iota(jnp.int32, (bk, bq), 1)
                p = jnp.where(qpos >= kpos, p, 0.0)
            ds = (p * (dp - rd[h:h + 1, rows]) * ATTN_SCALE).astype(jnp.bfloat16)
            dva[...] += lax.dot_general(p.astype(jnp.bfloat16), d, NN, preferred_element_type=jnp.float32)
            dka[...] += lax.dot_general(ds, q, NN, preferred_element_type=jnp.float32)
            dqt[cols, rows] += lax.dot_general(kt, ds, NN, preferred_element_type=jnp.float32)

    first = j * bk // bq
    ndiag = max(1, bk // bq)
    for t in range(ndiag):
        block(first + t, True)
    lax.fori_loop(first + ndiag, nq, lambda i, c: (block(i, False), c)[1], 0)
    own = pl.ds(pl.multiple_of(j * bk, bk), bk)
    out_ref[own, width:width + HEAD_DIM] = turned(dka[...], own)
    out_ref[own, width + HEAD_DIM:] = dva[...].astype(jnp.bfloat16)

    @pl.when(j == nk - 1)
    def _():
        def fin(i, c):
            rows = pl.ds(pl.multiple_of(i * bq, bq), bq)
            for h in range(heads):
                cols = slice(h * HEAD_DIM, (h + 1) * HEAD_DIM)
                out_ref[rows, cols] = turned(dqt[cols, rows].T, rows)
            return c
        lax.fori_loop(0, nq, fin, 0)
        for cp in carry_over:
            cp.wait()


def flash_bwd(q, o, d, k, kt, v, lse, cosw, sinw, gs, cid, bq=512, bk=512):
    seq, width = q.shape
    heads = width // HEAD_DIM
    whole = lambda j: (0, 0)
    an = pl.BlockSpec(memory_space=pl.ANY)
    return pl.pallas_call(
        functools.partial(bwd_kernel, bq, bk),
        grid=(seq // bk,),
        in_specs=[pl.BlockSpec((seq, width), whole), pl.BlockSpec((seq, width), whole), pl.BlockSpec((seq, width), whole),
                  pl.BlockSpec((bk, HEAD_DIM), lambda j: (j, 0)), pl.BlockSpec((HEAD_DIM, bk), lambda j: (0, j)),
                  pl.BlockSpec((bk, HEAD_DIM), lambda j: (j, 0)),
                  pl.BlockSpec((heads, seq), whole), pl.BlockSpec((seq, HEAD_DIM), whole), pl.BlockSpec((seq, HEAD_DIM), whole)] + [an] * 3,
        out_specs=[pl.BlockSpec((seq, width + 2 * HEAD_DIM), whole)] + [an] * 3,
        out_shape=[jax.ShapeDtypeStruct((seq, width + 2 * HEAD_DIM), jnp.bfloat16)] + halve_shapes(gs, 3),
        scratch_shapes=[pltpu.VMEM((width, seq), jnp.float32), pltpu.VMEM((bk, HEAD_DIM), jnp.float32), pltpu.VMEM((bk, HEAD_DIM), jnp.float32),
                        pltpu.VMEM((heads, seq), jnp.float32), pltpu.SemaphoreType.DMA((3,)), pltpu.SemaphoreType.DMA((3,))],
        cost_estimate=pl.CostEstimate(flops=5 * seq * seq * width * 2 // 2, bytes_accessed=16 << 20, transcendentals=seq * seq),
        compiler_params=comm_params(cid, vmem_limit_bytes=58 << 20),
        name="flash_bwd",
    )(q, o, d, k, kt, v, lse, cosw, sinw, *gs)


class PlaneGather:
    N = 13

    def __init__(self, here, wires, src, out, local_sem):
        h = src.shape[0] // 2
        A, B = slice(0, h), slice(h, 2 * h)
        s = here.s
        sx, sy, sc = here.peer('x')[1], here.peer('y')[1], here.peer('c')[1]
        sd = here.s + 2 - 4 * here.x + 4 - 8 * here.y
        nx, ny, nc = here.peer('x'), here.peer('y'), here.peer('c')
        self.local = pltpu.make_async_copy(src, out.at[s], local_sem)
        mk = wires.copy
        self.x1 = {k: mk(src.at[r], out.at[s, r], nx) for k, r in (('A', A), ('B', B))}
        self.y1 = {k: mk(src.at[r], out.at[s, r], ny) for k, r in (('B', B), ('A', A))}
        self.c1 = mk(src, out.at[s], nc)
        self.fy = mk(out.at[sx, A], out.at[sx, A], ny)
        self.fx = mk(out.at[sy, B], out.at[sy, B], nx)
        self.cc = {}
        for name, idx in (('x', sx), ('y', sy), ('d', sd)):
            for k, r in (('A', A), ('B', B)):
                self.cc[name + k] = mk(out.at[idx, r], out.at[idx, r], nc)

    def start_first(self):
        self.x1['A'].start()
        self.y1['B'].start()
        self.c1.start()
        self.local.start()

    def start_second(self):
        self.x1['B'].start()
        self.y1['A'].start()

    def relay(self):
        self.x1['A'].wait_recv()
        self.fy.start()
        self.cc['xA'].start()
        self.y1['B'].wait_recv()
        self.fx.start()
        self.cc['yB'].start()
        self.x1['B'].wait_recv()
        self.cc['xB'].start()
        self.y1['A'].wait_recv()
        self.cc['yA'].start()

    def finish(self):
        self.fy.wait_recv()
        self.cc['dA'].start()
        self.fx.wait_recv()
        self.cc['dB'].start()
        self.c1.wait_recv()
        for k in self.cc:
            self.cc[k].wait_recv()
        for c in (*self.x1.values(), *self.y1.values(), self.c1, self.fy, self.fx, *self.cc.values()):
            c.wait_send()
        self.local.wait()


NG = PlaneGather.N + 2 * 6 + 1


def dh_kernel(src, wg, out, og, send_sem, recv_sem, local_sem):
    here = Spot()
    greet(cube_targets(here))
    wires = Wires(send_sem, recv_sem)
    c = here.c
    loc = pltpu.make_async_copy(wg, og.at[here.region('') + (c,)], local_sem.at[1])
    g = PlaneGather(here, wires, src, out, local_sem.at[0])
    jobs = [(og, (c, slice(None), slice(off, off + n)), order) for (off, n), order in zip(col_chunks(wg.shape[1], 2), ('xyz', 'yxz'))]
    cube = CubeGather(here, wires, jobs)
    post = wires.copy(og.at[:, :, :, c], og.at[:, :, :, c], here.peer('c'))
    loc.start()
    loc.wait()
    cube.start(0)
    g.start_first()
    cube.start(1)
    g.start_second()
    g.relay()
    cube.start(2)
    g.finish()
    cube.arrive()
    post.start()
    post.wait()
    cube.drain()


def gather_dh(src, wg, cid):
    rows, cols = src.shape
    vm = pl.BlockSpec(memory_space=pltpu.VMEM)
    an = pl.BlockSpec(memory_space=pl.ANY)
    return pl.pallas_call(
        dh_kernel, in_specs=[vm] * 2, out_specs=[an] * 2,
        out_shape=[jax.ShapeDtypeStruct((8, rows, cols), src.dtype), jax.ShapeDtypeStruct((2, 2, 2, 2, *wg.shape), wg.dtype)],
        scratch_shapes=[pltpu.SemaphoreType.DMA((NG,)), pltpu.SemaphoreType.DMA((NG,)), pltpu.SemaphoreType.DMA((2,))],
        cost_estimate=busy(50), compiler_params=comm_params(cid), name="gather_dh",
    )(src, wg)


def entry_kernel(x_ref, w_ref, meta_ref, pos_ref, xa, wa, ma, pa, send_sem, recv_sem, local_sem):
    here = Spot()
    z, s = here.z, here.s
    peers = here.others()
    nz = here.peer('z')
    greet(peers + [nz])
    wires = Wires(send_sem, recv_sem)
    first = []
    for t in peers:
        for src, dst in ((w_ref.at[t[1]], wa.at[z, s]), (meta_ref, ma.at[z, s]), (pos_ref, pa.at[s])):
            first.append(wires.copy(src, dst, t))
    locals_ = [pltpu.make_async_copy(w_ref.at[s], wa.at[z, s], local_sem.at[1]),
               pltpu.make_async_copy(meta_ref, ma.at[z, s], local_sem.at[2]),
               pltpu.make_async_copy(pos_ref, pa.at[s], local_sem.at[3])]
    g = PlaneGather(here, wires, x_ref, xa, local_sem.at[0])
    cross = [wires.copy(wa.at[z], wa.at[z], nz), wires.copy(ma.at[z], ma.at[z], nz)]
    for c in first:
        c.start()
    for c in locals_:
        c.start()
    g.start_first()
    g.start_second()
    for c in first:
        c.wait_recv()
    for c in locals_:
        c.wait()
    for c in cross:
        c.start()
    g.relay()
    g.finish()
    for c in cross:
        c.wait()
    for c in first:
        c.wait_send()


def entry(x, w, meta, pos, cid):
    n = PlaneGather.N + 21 + 2
    vm = pl.BlockSpec(memory_space=pltpu.VMEM)
    an = pl.BlockSpec(memory_space=pl.ANY)
    return pl.pallas_call(
        entry_kernel,
        in_specs=[vm] * 4, out_specs=[an] * 4,
        out_shape=[jax.ShapeDtypeStruct((8, *x.shape), x.dtype), jax.ShapeDtypeStruct((2, 8, *w.shape[1:]), w.dtype),
                   jax.ShapeDtypeStruct((2, 8, *meta.shape), meta.dtype), jax.ShapeDtypeStruct((8, *pos.shape), pos.dtype)],
        scratch_shapes=[pltpu.SemaphoreType.DMA((n,)), pltpu.SemaphoreType.DMA((n,)), pltpu.SemaphoreType.DMA((4,))],
        cost_estimate=busy(45), compiler_params=comm_params(cid),
        name="entry",
    )(x, w, meta, pos)


def regroup_kernel(n, *refs):
    src, gs, out, rs = refs[0], refs[1:1 + n], refs[1 + n], refs[2 + n:2 + 2 * n]
    send_sem, recv_sem, local_sem, stage = refs[2 + 2 * n:]
    here = Spot()
    s = here.s
    rows, width = out.shape[0], src.shape[1]
    peers = here.others()
    greet(peers + ([here.peer('z')] if n else []))
    wires = Wires(send_sem, recv_sem)
    piece = lambda i: pl.ds(pl.multiple_of(i * rows, rows), rows)
    mine = pl.ds(pl.multiple_of(s * width, width), width)
    cs = [wires.copy(src.at[piece(t[1])], out.at[:, mine], t) for t in peers]
    cs += halve_copies(here, wires, 2, gs, rs)
    for c in cs:
        c.start()
    a = pltpu.make_async_copy(src.at[piece(s)], stage, local_sem.at[0])
    a.start()
    a.wait()
    b = pltpu.make_async_copy(stage, out.at[:, mine], local_sem.at[1])
    b.start()
    b.wait()
    for c in cs:
        c.wait()


def regroup(src, gs, cid, name):
    seq, width = src.shape
    rows, n = seq // 8, len(gs)
    an = pl.BlockSpec(memory_space=pl.ANY)
    out = pl.pallas_call(
        functools.partial(regroup_kernel, n), in_specs=[an] * (1 + n), out_specs=[an] * (1 + n),
        out_shape=[jax.ShapeDtypeStruct((rows, 8 * width), src.dtype)] + halve_shapes(gs, 2),
        scratch_shapes=[pltpu.SemaphoreType.DMA((7 + n,)), pltpu.SemaphoreType.DMA((7 + n,)), pltpu.SemaphoreType.DMA((2,)), pltpu.VMEM((rows, width), src.dtype)],
        cost_estimate=busy(70 if n else 25), compiler_params=comm_params(cid), name=name,
    )(src, *gs)
    return out[0], out[1:]


def owner_kernel(n, *refs):
    a, b, gs, oa, ob, rs = refs[0], refs[1], refs[2:2 + n], refs[2 + n], refs[3 + n], refs[4 + n:4 + 2 * n]
    send_sem, recv_sem, local_sem = refs[4 + 2 * n:]
    here = Spot()
    peers = here.others()
    greet(peers + [here.peer('z')])
    wires = Wires(send_sem, recv_sem)
    s = here.s
    cs = halve_copies(here, wires, 1, gs, rs)
    cs += [wires.copy(r.at[t[1]], o.at[s], t) for t in peers for r, o in ((a, oa), (b, ob))]
    loc = [pltpu.make_async_copy(a.at[s], oa.at[s], local_sem.at[0]), pltpu.make_async_copy(b.at[s], ob.at[s], local_sem.at[1])]
    for c in cs + loc:
        c.start()
    for c in cs + loc:
        c.wait()


def owner(a, b, gs, cid):
    n = len(gs)
    vm = pl.BlockSpec(memory_space=pltpu.VMEM)
    an = pl.BlockSpec(memory_space=pl.ANY)
    out = pl.pallas_call(
        functools.partial(owner_kernel, n), in_specs=[vm] * 2 + [an] * n, out_specs=[vm] * 2 + [an] * n,
        out_shape=[jax.ShapeDtypeStruct(t.shape, t.dtype) for t in (a, b)] + halve_shapes(gs, 1),
        scratch_shapes=[pltpu.SemaphoreType.DMA((14 + n,)), pltpu.SemaphoreType.DMA((14 + n,)), pltpu.SemaphoreType.DMA((2,))],
        cost_estimate=busy(30), compiler_params=comm_params(cid), name="owner",
    )(a, b, *gs)
    return out[0], out[1], out[2:]


def dot_tokens(left_op, right_op):
    return lax.dot_general(left_op, right_op, (((0,), (0,)), ((), ())), preferred_element_type=jnp.float32)


def dot_back(left_op, weight):
    return lax.dot_general(left_op, weight, (((1,), (1,)), ((), ())), preferred_element_type=jnp.float32)


def dot_on(left_op, weight):
    return jnp.dot(left_op, weight, preferred_element_type=jnp.float32)


def swap_core(t):
    return lax.ppermute(t, 'sp', [(i, i ^ 1) for i in range(8)])


def swap_z(t):
    return lax.ppermute(t, 'dp', [(0, 1), (1, 0)])


def split_cols(w):
    rows, cols = w.shape
    return w.reshape(rows, 8, 2, cols // 16).transpose(2, 0, 1, 3).reshape(2, rows, cols // 2)


def join_cols(mine, other, c):
    rows, half = mine.shape
    m, o = mine.reshape(rows, 8, 1, half // 8), other.reshape(rows, 8, 1, half // 8)
    first = jnp.where(c == 0, m, o)
    second = jnp.where(c == 0, o, m)
    return jnp.concatenate([first, second], axis=2).reshape(rows, 2 * half)


def layer_step(hidden, positions, grad_out, gain_attn, gain_mlp, w_query, w_key, w_value, w_out, w_gate, w_up, w_down):
    tokens = hidden[0]
    d_layer = grad_out[0]
    tok, dim = tokens.shape
    here = Spot()
    z, s, c = here.z, here.s, here.c
    rows = w_query.shape[0]
    grp_q = w_query.shape[1] // 8
    grp_k = w_key.shape[1] // 8
    grp = grp_q + 2 * grp_k
    seq = 8 * tok

    w_grp = jnp.concatenate([w_query.reshape(rows, 8, grp_q), w_key.reshape(rows, 8, grp_k), w_value.reshape(rows, 8, grp_k)], axis=2)
    w_flat = w_grp.reshape(rows, 8 * grp)
    pad = HEAD_DIM - gain_attn.shape[0]
    meta = jnp.pad(jnp.stack([jnp.pad(gain_attn, (0, pad)), jnp.pad(gain_mlp, (0, pad))]), ((0, 14), (0, 0)))
    x_all, w_own, meta_all, pos_all = entry(tokens, w_grp.transpose(1, 0, 2), meta, positions[0].reshape(-1, 128), 1)
    x_all = x_all.reshape(seq, dim)
    w_own = w_own.reshape(dim, grp)
    gain1 = meta_all[:, :, 0, :rows].reshape(dim)
    gain2 = meta_all[:, :, 1, :rows].reshape(dim)
    cos_tab, sin_tab = rope_tables(pos_all.reshape(seq))

    cosw = jnp.concatenate([cos_tab, cos_tab], axis=1)
    sinw = jnp.concatenate([-sin_tab, sin_tab], axis=1)
    u_all, q_own, k_own, v_own, k_t, v_t = project(x_all, jnp.broadcast_to(gain1[None], (16, dim)), w_own, cosw, sinw)
    o_own, lse, w1, w3, w2, wo = flash_fwd(q_own, k_own, v_t, (split_cols(w_gate), split_cols(w_up), w_down, w_out), 2)
    ffn_half = w1.shape[-1]
    w1, w3 = w1.reshape(dim, ffn_half), w3.reshape(dim, ffn_half)
    w2 = w2.reshape(ffn_half, dim)
    wo = wo.reshape(-1, dim)
    attn_out, _ = regroup(o_own, (), 3, 'regroup_o')
    residual = (tokens.astype(jnp.float32) + dot_on(attn_out, wo)).astype(jnp.bfloat16)
    u_mlp, normed2, inv_rms2 = rms_norm(residual, gain2)
    u_pair = jnp.concatenate([u_mlp, swap_core(u_mlp)], axis=0)
    d_pair = jnp.concatenate([d_layer, swap_core(d_layer)], axis=0)
    gate_pre = dot_on(u_pair, w1)
    up_pre = dot_on(u_pair, w3)
    sig_gate = jax.nn.sigmoid(gate_pre)
    silu_gate = gate_pre * sig_gate
    mlp_act = (silu_gate * up_pre).astype(jnp.bfloat16)
    y_part = dot_on(mlp_act, w2)
    layer_out = (residual.astype(jnp.float32) + (y_part[:tok] + swap_core(y_part[tok:]))).astype(jnp.bfloat16)

    d_act = dot_back(d_pair, w2)
    d_gate = (d_act * up_pre * sig_gate * (1.0 + gate_pre * (1.0 - sig_gate))).astype(jnp.bfloat16)
    d_up = (d_act * silu_gate).astype(jnp.bfloat16)
    d_part = dot_back(d_gate, w1) + dot_back(d_up, w3)
    d_umlp = d_part[:tok] + swap_core(d_part[tok:])
    d_res_norm, d_gain2 = rms_norm_grad(d_umlp, normed2, inv_rms2, gain2)
    d_resid = d_layer.astype(jnp.float32) + d_res_norm
    d_resid_bf = d_resid.astype(jnp.bfloat16)
    g1 = dot_tokens(u_pair, d_gate).reshape(2, 2, 2, dim // 8, ffn_half)
    g3 = dot_tokens(u_pair, d_up).reshape(2, 2, 2, dim // 8, ffn_half)
    g2 = dot_tokens(mlp_act, d_pair).reshape(2, 2, 2, ffn_half // 8, dim)

    dh_all, wg = gather_dh(d_resid_bf, w_flat, 4)
    dh_all = dh_all.reshape(seq, dim)
    wg = wg.reshape(dim, 8 * grp)
    wo_own = lax.dynamic_slice_in_dim(wo, s * grp_q, grp_q, 0)
    d_own = dot_back(dh_all, wo_own).astype(jnp.bfloat16)
    go = dot_tokens(o_own, dh_all).reshape(2, grp_q // 2, dim)
    dqkv_pre, *got = flash_bwd(q_own, o_own, d_own, k_own, k_t, v_own, lse, cosw, sinw, (g1, g3, g2), 6)
    g_mlp = halve_add((g1, g3, g2), got, 3)

    go_mine = lax.dynamic_index_in_dim(go, z, 0, False) + swap_z(lax.dynamic_index_in_dim(go, 1 - z, 0, False))
    grad_w_out = lax.ppermute(go_mine, ALL_AXES, [(zz * 8 + ss, 2 * ss + zz) for zz in range(2) for ss in range(8)])
    dqkv_tok, got = regroup(dqkv_pre, g_mlp, 5, 'regroup_dqkv')
    g_mlp = halve_add(g_mlp, got, 2)
    gq = dot_tokens(u_all, dqkv_pre).reshape(2, dim // 2, grp)
    gq_mine = lax.dynamic_index_in_dim(gq, z, 0, False) + swap_z(lax.dynamic_index_in_dim(gq, 1 - z, 0, False))
    d_uattn = dot_back(dqkv_tok, wg)
    _, normed1, inv_rms1 = rms_norm(tokens, gain1)
    d_tok_norm, d_gain1 = rms_norm_grad(d_uattn, normed1, inv_rms1, gain1)
    grad_hidden = (d_resid + d_tok_norm).astype(jnp.bfloat16)

    gains = jnp.concatenate([d_gain1.reshape(2, 8, rows), d_gain2.reshape(2, 8, rows)], axis=2)
    gains_mine = lax.dynamic_index_in_dim(gains, z, 0, False) + swap_z(lax.dynamic_index_in_dim(gains, 1 - z, 0, False))
    gains_mine = jnp.broadcast_to(gains_mine[:, None, :], (8, 8, 2 * rows))
    got_q, got_g, got = owner(gq_mine.reshape(8, rows, grp), gains_mine, g_mlp, 10)
    got_q = got_q.transpose(1, 0, 2)
    grad_w_query = got_q[:, :, :grp_q].reshape(rows, 8 * grp_q)
    grad_w_key = got_q[:, :, grp_q:grp_q + grp_k].reshape(rows, 8 * grp_k)
    grad_w_value = got_q[:, :, grp_q + grp_k:].reshape(rows, 8 * grp_k)
    grad_gains = jnp.sum(got_g[:, 0, :], axis=0)
    grad_gain_attn, grad_gain_mlp = grad_gains[:rows], grad_gains[rows:]

    m1, m3, grad_w_down = halve_add(g_mlp, got, 1)
    pair = jnp.stack([m1.reshape(2, rows, ffn_half), m3.reshape(2, rows, ffn_half)], axis=1)
    keep = lax.dynamic_index_in_dim(pair, c, 0, False)
    other = swap_core(lax.dynamic_index_in_dim(pair, 1 - c, 0, False))
    grad_w_gate = join_cols(keep[0], other[0], c)
    grad_w_up = join_cols(keep[1], other[1], c)
    return (layer_out[None], grad_hidden[None], grad_gain_attn, grad_gain_mlp, grad_w_query, grad_w_key, grad_w_value, grad_w_out, grad_w_gate, grad_w_up, grad_w_down)


def solution(mesh):
    act_spec = P('dp', 'sp', None)
    pos_spec = P('dp', 'sp')
    vec_spec = P(ALL_AXES)
    mat_spec = P(ALL_AXES, None)
    in_specs = (act_spec, pos_spec, act_spec, vec_spec, vec_spec) + (mat_spec,) * 7
    out_specs = (act_spec, act_spec, vec_spec, vec_spec) + (mat_spec,) * 7
    return jax.shard_map(layer_step, mesh=mesh, in_specs=in_specs, out_specs=out_specs, check_vma=False)
```

time: 1150 us -> 664 us (0.58)
  waiting for transfers between devices: 573 us -> 0.02 us
  Pallas kernels: 101 us -> 465 us
  blocking collectives: 198 us -> 0 us
  local copies, waits for them, and re-layouts: 84.5 us -> 35.2 us
  matrix products: 123 us -> 93.2 us
  other arithmetic: 31.5 us -> 54.2 us
  between operations: 14.8 us -> 1.69 us
    reduce_scatter x7 -> x0, waiting for transfers between devices: 421 us -> none  [scatter_sum(): lax.psum_scatter(partial_sum, ALL_AXES, scatter_dimension=0, tiled=True)]
    pallas_call x0 -> x6, Pallas kernels: none -> 291 us  [the longest x2 107 us: regroup(): pl.pallas_call(functools.partial(regroup_kernel, n), in_specs=[an] * (1 +...]
    all_to_all x4 -> x0, blocking collectives: 131 us -> none  [the longest x3 101 us: to_tokens(): return lax.all_to_all(head_major, 'sp', 0, 1, tiled=True)]
    all_to_all x4 -> x0, waiting for transfers between devices: 74.6 us -> none  [the longest x3 37.9 us: to_heads(): return lax.all_to_all(tok_major, 'sp', 1, 0, tiled=True)]
    all_gather x7 -> x0, waiting for transfers between devices: 72.8 us -> none  [gather_full(): return lax.all_gather(local_shard, ALL_AXES, axis=0, tiled=True)]
    unnamed x2 -> x0, blocking collectives: 66.8 us -> none
    pallas_call x1, Pallas kernels: 43.5 us -> 95.7 us  [flash_fwd(): pl.pallas_call(functools.partial(fwd_kernel, bq, bk), grid=(seq // bq,),...]
    pallas_call x1, Pallas kernels: 57.6 us -> 77.9 us  [flash_bwd(): pl.pallas_call(functools.partial(bwd_kernel, bq, bk), grid=(seq // bk,),...]
  transfers between devices with their start and end apart: 18 -> 9, of which waited for: 11 -> 0; matrix products, arithmetic and copies ran while one was open for 14% -> 15% of each run, Pallas kernels for 4% -> 24%
where the time goes in v3:
time: 664 us; the launch traced here: 656 us
  Pallas kernels  465 us (70%)
  matrix products  93.2 us (14%)
  other arithmetic  54.2 us (8%)
  local copies, waits for them, and re-layouts  35.2 us (5%)
  starting transfers between devices  7.3 us (1%)
    pallas_call x2, Pallas kernels, regroup(): pl.pallas_call(functools.partial(regroup_kernel, n), in_specs=[an] * (1 +...  107 us
    pallas_call x1, Pallas kernels, flash_fwd(): pl.pallas_call(functools.partial(fwd_kernel, bq, bk), grid=(seq // bq,),...  95.7 us
    pallas_call x1, Pallas kernels, flash_bwd(): pl.pallas_call(functools.partial(bwd_kernel, bq, bk), grid=(seq // bk,),...  77.9 us
    pallas_call x1, Pallas kernels, gather_dh(): pl.pallas_call(dh_kernel, in_specs=[vm] * 2, out_specs=[an] * 2, out_shap...  76.6 us
    pallas_call x1, Pallas kernels, entry(): pl.pallas_call(entry_kernel, in_specs=[vm] * 4, out_specs=[an] * 4, out_s...  49.8 us
    pallas_call x1, Pallas kernels, owner(): pl.pallas_call(functools.partial(owner_kernel, n), in_specs=[vm] * 2 + [a...  42.1 us
    dot_general x5, matrix products, dot_tokens(): lax.dot_general(left_op, right_op, (((0,), (0,)), ((), ())), preferred_el...  36.6 us
    dot_general x5, matrix products, dot_back(): lax.dot_general(left_op, weight, (((1,), (1,)), ((), ())), preferred_elem...  31.5 us
  transfers between devices with their start and end apart: 9, of which 0 were waited for; matrix products, arithmetic and copies ran while one was open for 15% of the time, Pallas kernels for 24%

profile of v3, /device:TPU:0, one launch (start us, length us, event | category | flops | bytes accessed | tf_op | source)
XLA Modules:
  0.0 656.2 jit_solution(13603179092056789157)
XLA Ops:
  4.8 49.8 %entry.1 = (bf16[8,512,1024]{2,1,0:T(8,128)(2,1)}, bf16[2,8,64,512]{3,2,1,0:T(8,128)(2,1)}, bf16[2,8,16,128]{3,2,1,0:T(8,128)(2,1)}, s32[8,4,128]{2,1,0:T(4,128)}) custom-call(bf16[512,1024]{1,0:T(8,128)(2,1)} %bitcast.150, bf16[8,64,512]{2,1,0:T(8,128)(2,1)} %bitcast.175, bf16[16,128]{1,0:T(8,128)(2,1)} %fusion.41.meta_ref, s32[4,128]{1,0:T(4,128)} %bitcast.186), custom_call_target="tpu_custom_call" | custom-call | flops 4499999744 | bytes 1048576 | tf_op jit(solution)/shard_map/entry/pallas_call | solution.py:560
  57.0 1.2 reshape.249.w1
  58.9 1.2 reshape.251.w3
  60.2 7.5 %fusion.31 = (f32[4096,64]{1,0:T(8,128)S(1)}, f32[4096,64]{1,0:T(8,128)S(1)}, f32[4096,64]{1,0:T(8,128)S(1)}) fusion(f32[64]{0:T(128)S(1)} %negate_power_fusion, f32[4096]{0:T(1024)S(1)} %bitcast.185), kind=kLoop, calls=%fused_computation.72 | loop fusion | flops 524288 | bytes 3162368 | tf_op jit(solution)/shard_map/neg | solution.py:696
  67.7 1.9 pad_maximum_fusion.cos_ref
  69.6 2.0 pad_maximum_fusion.1.sin_ref
  71.7 15.7 %project.1 = (bf16[4096,1024]{1,0:T(8,128)(2,1)}, bf16[4096,256]{1,0:T(8,128)(2,1)}, bf16[4096,128]{1,0:T(8,128)(2,1)S(1)}, bf16[4096,128]{1,0:T(8,128)(2,1)S(1)...) custom-call(bf16[4096,1024]{1,0:T(8,128)(2,1)} %bitcast.188, ...), custom_call_target="tpu_custom_call" | custom-call | flops 4294967296 | bytes 33554432 | tf_op jit(solution)/shard_map/project/pallas_call | solution.py:230
  91.3 95.7 %flash_fwd.1 = (bf16[4096,256]{1,0:T(8,128)(2,1)}, f32[2,4096]{1,0:T(2,128)}, bf16[2,2,2,2,64,1536]{5,4,3,2,1,0:T(8,128)(2,1)}, bf16[2,2,2,2,64,1536]{5,4,3,2,1,...) custom-call(bf16[4096,256]{1,0:T(8,128)(2,1)} %get-tuple-element.46.q_ref, ...), custom_call_target="tpu_custom_call" | custom-call | flops 17179869184 | bytes 8388608 | tf_op jit(solution)/shard_map/flash_fwd/pallas_call | solution.py:310
  186.9 24.8 %regroup_o.1 = bf16[512,2048]{1,0:T(8,128)(2,1)} custom-call(bf16[4096,256]{1,0:T(8,128)(2,1)} %get-tuple-element.49.refs_0_.o_ref), custom_call_target="tpu_custom_call" | custom-call | flops 2500000000 | bytes 1048576 | tf_op jit(solution)/shard_map/regroup_o/pallas_call | solution.py:600
  211.8 5.3 fusion.22
  217.1 1.3 fusion.16
  218.4 1.3 collective-permute-start
  220.6 4.1 copy.45
  225.1 8.8 %fusion.46 = f32[1024,1536]{1,0:T(8,128)} fusion(bf16[1024,1536]{1,0:T(8,128)(2,1)} %bitcast.193, bf16[512,1024]{1,0:T(8,128)(2,1)} %collective-permute-done, bf16[512,1024]{1,0:T(8,128)(2,1)} %fusion.16), kind=kOutput, calls=%fused_computation.114 | convolution fusion | flops 3225419776 | bytes 11534336 | tf_op jit(solution)/shard_map/dot_general | solution.py:648
  233.8 7.6 %fusion.47 = f32[1024,1536]{1,0:T(8,128)} fusion(bf16[1024,1536]{1,0:T(8,128)(2,1)S(1)} %bitcast.195, bf16[512,1024]{1,0:T(8,128)(2,1)} %collective-permute-done, bf16[512,1024]{1,0:T(8,128)(2,1)} %fusion.16), kind=kOutput, calls=%fused_computation.115 | convolution fusion | flops 3225419776 | bytes 11534336 | tf_op jit(solution)/shard_map/dot_general | solution.py:648
  241.4 9.1 %multiply_convert_fusion = (bf16[1024,1536]{1,0:T(8,128)(2,1)S(1)}, bf16[1024,1536]{1,0:T(8,128)(2,1)S(1)}, bf16[1024,1536]{1,0:T(8,128)(2,1)S(1)}) fusion(f32[1024,1536]{1,0:T(8,128)} %fusion.47, f32[1024,1536]{1,0:T(8,128)} %fusion.46, bf16[1536,1024]{1,0:T(8,128)(2,1)S(1)} %bitcast.197, bf16[512,1024]{1,0:T(8,128)(2,1)} %collective-permute-done.2, ...), kind=kOutput, calls=%fused_computation | convolution fusion | flops 3249012736 | bytes 27262976 | tf_op jit(solution)/shard_map/dot_general | solution.py:644
  250.4 3.4 fusion.53
  253.9 3.4 fusion.54
  257.3 3.5 convolution_add_fusion
  261.8 7.5 %fusion.24 = f32[1536,1024]{1,0:T(8,128)} fusion(bf16[1024,1536]{1,0:T(8,128)(2,1)S(1)} %get-tuple-element.81, bf16[512,1024]{1,0:T(8,128)(2,1)} %collective-permute-done.2, bf16[512,1024]{1,0:T(8,128)(2,1)} %bitcast.15), kind=kOutput, calls=%fused_computation.54 | convolution fusion | flops 3225419776 | bytes 11534336 | tf_op jit(solution)/shard_map/dot_general | solution.py:640
  269.3 7.2 %fusion.44 = f32[1024,1536]{1,0:T(8,128)} fusion(bf16[1024,1536]{1,0:T(8,128)(2,1)S(1)} %get-tuple-element.79, bf16[512,1024]{1,0:T(8,128)(2,1)} %collective-permute-done, bf16[512,1024]{1,0:T(8,128)(2,1)} %fusion.16), kind=kOutput, calls=%fused_computation.112 | convolution fusion | flops 3225419776 | bytes 11534336 | tf_op jit(solution)/shard_map/dot_general | solution.py:640
  276.5 7.1 %fusion.45 = f32[1024,1536]{1,0:T(8,128)} fusion(bf16[1024,1536]{1,0:T(8,128)(2,1)S(1)} %get-tuple-element.80, bf16[512,1024]{1,0:T(8,128)(2,1)} %collective-permute-done, bf16[512,1024]{1,0:T(8,128)(2,1)} %fusion.16), kind=kOutput, calls=%fused_computation.113 | convolution fusion | flops 3225419776 | bytes 11534336 | tf_op jit(solution)/shard_map/dot_general | solution.py:640
  285.0 6.0 fusion.48
  291.0 76.6 %gather_dh.1 = (bf16[8,512,1024]{2,1,0:T(8,128)(2,1)}, bf16[2,2,2,2,64,4096]{5,4,3,2,1,0:T(8,128)(2,1)}) custom-call(bf16[512,1024]{1,0:T(8,128)(2,1)} %get-tuple-element.77.src, bf16[64,4096]{1,0:T(8,128)(2,1)} %bitcast.180), custom_call_target="tpu_custom_call" | custom-call | flops 5000000000 | bytes 1048576 | tf_op jit(solution)/shard_map/gather_dh/pallas_call | solution.py:512
  367.6 6.5 fusion.56
  376.7 4.8 convolution_convert_fusion.d_ref
  381.5 77.9 %flash_bwd.1 = (bf16[4096,512]{1,0:T(8,128)(2,1)}, f32[2,2,128,1536]{3,2,1,0:T(8,128)}, f32[2,2,128,1536]{3,2,1,0:T(8,128)}, f32[2,2,192,1024]{3,2,1,0:T(8,128)}) custom-call(bf16[4096,256]{1,0:T(8,128)(2,1)} %get-tuple-element.46.q_ref, bf16[4096,256]{1,0:T(8,128)(2,1)} %get-tuple-element.49.refs_0_.o_ref, bf16[4096,256]{1,0:T(8,128)(2,1)} %convolution_convert_fusion.d_ref, ...), custom_call_target="tpu_custom_call" | custom-call | flops 21474836480 | bytes 16777216 | tf_op jit(solution)/shard_map/flash_bwd/pallas_call | solution.py:406
  459.5 8.3 %fusion.55 = f32[1024,512]{1,0:T(8,128)S(1)} fusion(bf16[4096,1024]{1,0:T(8,128)(2,1)} %get-tuple-element.64, bf16[4096,512]{1,0:T(8,128)(2,1)} %get-tuple-element.58.refs_0_), kind=kOutput, calls=%fused_computation.122 | convolution fusion | flops 4294967296 | bytes 14680064 | tf_op jit(solution)/shard_map/dot_general | solution.py:640
  469.7 5.3 bitcast_add_fusion.refs_3_
  475.1 4.3 bitcast_add_fusion.2.refs_1_
  479.4 2.3 bitcast_add_fusion.1.refs_2_
  481.6 81.9 %regroup_dqkv.1 = (bf16[512,4096]{1,0:T(8,128)(2,1)}, f32[2,128,1536]{2,1,0:T(8,128)}, f32[2,128,1536]{2,1,0:T(8,128)}, f32[2,192,1024]{2,1,0:T(8,128)}) custom-call(bf16[4096,512]{1,0:T(8,128)(2,1)} %get-tuple-element.58.refs_0_, f32[2,2,128,1536]{3,2,1,0:T(8,128)} %bitcast_add_fusion.2.refs_1_, f32[2,2,128,1536]{3,2,1,0:T(8,128)} %bitcast_add_fusion.1.refs_2_, ...), custom_call_target="tpu_custom_call" | custom-call | flops 7000000000 | bytes 1048576 | tf_op jit(solution)/shard_map/regroup_dqkv/pallas_call | solution.py:600
  563.6 3.5 bitcast_add_fusion.4.refs_3_
  567.1 1.3 bitcast_add_fusion.5.refs_2_
  568.5 10.7 %fusion.13 = (f32[1024]{0:T(1024)S(1)}, f32[512]{0:T(512)S(1)}, f32[512,1024]{1,0:T(8,128)}) fusion(f32[512]{0:T(512)S(1)} %add_rsqrt_fusion, bf16[1,512,1024]{2,1,0:T(8,128)(2,1)S(1)} %copy-done.13, f32[1024]{0:T(1024)S(1)} %convert_element_type.86, bf16[512,4096]{1,0:T(8,128)(2,1)} %get-tuple-element.62, bf16[1024,4096]{1,0:T(8,128)(2,1)} %bitcast.187), kind=kOutput, calls=%fused_computation.29 | convolution fusion | flops 4298635776 | bytes 15740928 | tf_op jit(solution)/shard_map/dot_general | solution.py:644
  579.3 1.5 collective-permute-start.5
  580.8 3.3 fusion.27
  584.1 1.3 bitcast_add_fusion.10
  586.1 1.5 bitcast_add_fusion.3.refs_4_
  587.7 2.6 bitcast_add_fusion.6
  590.9 42.1 %owner.1 = (f32[8,64,512]{2,1,0:T(8,128)}, f32[8,8,128]{2,1,0:T(8,128)}, f32[128,1536]{1,0:T(8,128)}, f32[128,1536]{1,0:T(8,128)}, f32[192,1024]{1,0:T(8,128)}) custom-call(f32[8,64,512]{2,1,0:T(8,128)} %bitcast.179, f32[8,8,128]{2,1,0:T(8,128)} %broadcast_in_dim.14.refs_1_, f32[2,128,1536]{2,1,0:T(8,128)} %bitcast_add_fusion.5.refs_2_, ...), custom_call_target="tpu_custom_call" | custom-call | flops 3000000000 | bytes 1048576 | tf_op jit(solution)/shard_map/owner/pallas_call | solution.py:630
  633.0 1.2 bitcast_add_fusion.8
  634.3 1.2 bitcast_add_fusion.9
  638.5 1.1 slice_bitcast_fusion.1
  640.3 1.5 collective-permute-start.8
  641.9 1.1 slice_bitcast_fusion
  649.0 1.9 reshape.270
  653.0 1.9 reshape.269
  (147 shorter events, 33.4 us)
Async XLA Ops:
  0.6 2.3 copy-start
  4.8 51.4 %copy-start.31 = (bf16[64,3072]{1,0:T(8,128)(2,1)S(1)}, bf16[64,3072]{1,0:T(8,128)(2,1)}, u32[]{:S(2)}) copy-start(bf16[64,3072]{1,0:T(8,128)(2,1)} %param.21) | copy-start | bytes 1179652
  54.6 3.6 copy-start.32
  54.6 5.6 copy-start.33
  69.6 2.0 copy-start.2
  87.3 1.0 copy-start.3
  88.3 1.0 copy-start.4
  89.3 1.0 copy-start.5
  90.3 1.0 copy-start.6
  186.9 24.9 %copy-start.12 = (bf16[1,512,1024]{2,1,0:T(8,128)(2,1)S(1)}, bf16[1,512,1024]{2,1,0:T(8,128)(2,1)}, u32[]{:S(2)}) copy-start(bf16[1,512,1024]{2,1,0:T(8,128)(2,1)} %param.12) | copy-start | bytes 3145732
  211.8 8.0 %copy-start.25 = (bf16[64,8,512]{2,0,1:T(8,128)(2,1)S(1)}, bf16[64,8,512]{2,0,1:T(8,128)(2,1)}, u32[]{:S(2)}) copy-start(bf16[64,8,512]{2,0,1:T(8,128)(2,1)} %copy-done.24) | copy-start | bytes 1572868
  218.4 6.6 %collective-permute-start = (bf16[512,1024]{1,0:T(8,128)(2,1)}, bf16[512,1024]{1,0:T(8,128)(2,1)}, u32[]{:S(2)}, u32[]{:S(2)}) collective-permute-start(bf16[512,1024]{1,0:T(8,128)(2,1)} %fusion.16), channel_id=1, source_target_pairs={{0,1},{1,0},{2,3},{3,2},{4,5},{5,4},{6,7},{7,6},{8,9},{9,8},{10,11... | collective-permute-start | bytes 3145736 | tf_op jit(solution)/shard_map/ppermute | solution.py:652
  219.8 21.6 %collective-permute-start.2 = (bf16[512,1024]{1,0:T(8,128)(2,1)}, bf16[512,1024]{1,0:T(8,128)(2,1)}, u32[]{:S(2)}, u32[]{:S(2)}) collective-permute-start(bf16[512,1024]{1,0:T(8,128)(2,1)} %bitcast.15), channel_id=1, source_target_pairs={{0,1},{1,0},{2,3},{3,2},{4,5},{5,4},{6,7},{7,6},{8,9},{9,8},{10,11... | collective-permute-start | bytes 3145736 | tf_op jit(solution)/shard_map/ppermute | solution.py:652
  225.0 8.8 %copy-start.36 = (bf16[2,2,2,2,64,1536]{5,4,3,2,1,0:T(8,128)(2,1)S(1)}, bf16[2,2,2,2,64,1536]{5,4,3,2,1,0:T(8,128)(2,1)}, u32[]{:S(2)}) copy-start(bf16[2,2,2,2,64,1536]{5,4,3,2,1,0:T(8,128)(2,1)} %get-tuple-element.51) | copy-start | bytes 9437188
  233.8 7.6 %copy-start.37 = (bf16[2,2,2,192,1024]{4,3,2,1,0:T(8,128)(2,1)S(1)}, bf16[2,2,2,192,1024]{4,3,2,1,0:T(8,128)(2,1)}, u32[]{:S(2)}) copy-start(bf16[2,2,2,192,1024]{4,3,2,1,0:T(8,128)(2,1)} %get-tuple-element.53) | copy-start | bytes 9437188
  253.9 7.2 %copy-start.11 = (f32[1024,1024]{1,0:T(8,128)}, f32[1024,1024]{1,0:T(8,128)S(1)}, u32[]{:S(2)}) copy-start(f32[1024,1024]{1,0:T(8,128)S(1)} %fusion.53) | copy-start | bytes 12582916
  253.9 3.5 copy-start.35
  260.9 22.7 %copy-start.7 = (f32[1024,1024]{1,0:T(8,128)}, f32[1024,1024]{1,0:T(8,128)S(1)}, u32[]{:S(2)}) copy-start(f32[1024,1024]{1,0:T(8,128)S(1)} %convolution_add_fusion) | copy-start | bytes 12582916
  261.2 23.8 %collective-permute-start.1 = (f32[512,1024]{1,0:T(8,128)S(1)}, f32[512,1024]{1,0:T(8,128)}, u32[]{:S(2)}, u32[]{:S(2)}) collective-permute-start(f32[512,1024]{1,0:T(8,128)S(1)} %slice.67), channel_id=1, source_target_pairs={{0,1},{1,0},{2,3},{3,2},{4,5},{5,4},{6,7},{7,6},{8,9},{9,8},{10,11... | collective-permute-start | bytes 6291464 | tf_op jit(solution)/shard_map/ppermute | solution.py:652
  261.7 21.8 %collective-permute-start.3 = (f32[512,1024]{1,0:T(8,128)S(1)}, f32[512,1024]{1,0:T(8,128)S(1)}, u32[]{:S(2)}, u32[]{:S(2)}) collective-permute-start(f32[512,1024]{1,0:T(8,128)S(1)} %slice.69), channel_id=1, source_target_pairs={{0,1},{1,0},{2,3},{3,2},{4,5},{5,4},{6,7},{7,6},{8,9},{9,8},{10,11... | collective-permute-start | bytes 6291464 | tf_op jit(solution)/shard_map/ppermute | solution.py:652
  283.6 1.4 copy-start.8
  367.6 9.1 %copy-start.34 = (bf16[8,512,1024]{2,1,0:T(8,128)(2,1)S(1)}, bf16[8,512,1024]{2,1,0:T(8,128)(2,1)}, u32[]{:S(2)}) copy-start(bf16[8,512,1024]{2,1,0:T(8,128)(2,1)} %get-tuple-element.54) | copy-start | bytes 25165828
  374.1 1.0 copy-start.26
  375.9 208.2 %collective-permute-start.6 = (f32[128,1024]{1,0:T(8,128)}, f32[128,1024]{1,0:T(8,128)}, u32[]{:S(2)}, u32[]{:S(2)}) collective-permute-start(f32[128,1024]{1,0:T(8,128)} %dynamic-slice_bitcast_fusion.1), channel_id=1, source_target_pairs={{0,8},{8,0},{1,9},{9,1},{2,10},{10,2},{3,11},{11,3},{4,12},{12,4},... | collective-permute-start | bytes 1572872 | tf_op jit(solution)/shard_map/ppermute | solution.py:656
  459.5 10.2 %copy-start.19 = (f32[2,2,192,1024]{3,2,1,0:T(8,128)S(1)}, f32[2,2,192,1024]{3,2,1,0:T(8,128)}, u32[]{:S(2)}) copy-start(f32[2,2,192,1024]{3,2,1,0:T(8,128)} %get-tuple-element.61) | copy-start | bytes 9437188
  467.8 1.9 copy-start.20
  467.8 11.5 %slice-start = ((s8[6291456]{0:T(1024)(128)(4,1)}), s8[4194304]{0:T(1024)(128)(4,1)S(1)}, s32[]{:S(2)}) async-start(s8[6291456]{0:T(1024)(128)(4,1)} %bitcast.168), calls=%async_computation | async-start | bytes 8388608
  468.9 118.7 %collective-permute-start.4 = (f32[512,512]{1,0:T(8,128)}, f32[512,512]{1,0:T(8,128)}, u32[]{:S(2)}, u32[]{:S(2)}) collective-permute-start(f32[512,512]{1,0:T(8,128)} %dynamic-slice_bitcast_fusion), channel_id=1, source_target_pairs={{0,8},{8,0},{1,9},{9,1},{2,10},{10,2},{3,11},{11,3},{4,12},{12,4},... | collective-permute-start | bytes 3145736 | tf_op jit(solution)/shard_map/ppermute | solution.py:656
  469.7 5.4 copy-start.18
  469.7 9.6 %slice-start.1 = ((s8[6291456]{0:T(1024)(128)(4,1)}), s8[2097152]{0:T(1024)(128)(4,1)S(1)}, s32[]{:S(2)}) async-start(s8[6291456]{0:T(1024)(128)(4,1)} %bitcast.168), calls=%async_computation.1 | async-start | bytes 4194304
  475.1 4.3 copy-start.17
  563.6 3.5 copy-start.10
  563.6 3.5 copy-start.23
  567.1 1.4 copy-start.13
  579.3 8.2 %collective-permute-start.5 = (f32[8,128]{1,0:T(8,128)S(1)}, f32[8,128]{1,0:T(8,128)S(1)}, u32[]{:S(2)}, u32[]{:S(2)}) collective-permute-start(f32[8,128]{1,0:T(8,128)S(1)} %fusion.37), channel_id=1, source_target_pairs={{0,8},{8,0},{1,9},{9,1},{2,10},{10,2},{3,11},{11,3},{4,12},{12,4},... | collective-permute-start | bytes 12296 | tf_op jit(solution)/shard_map/ppermute | solution.py:656
  580.8 3.3 copy-start.27
  580.8 5.3 copy-start.9
  580.8 5.3 copy-start.22
  584.1 3.6 copy-start.21
  585.4 2.3 collective-permute-start.7
  587.6 2.6 copy-start.29
  590.9 42.2 %copy-start.16 = (f32[2,128,1536]{2,1,0:T(8,128)S(1)}, f32[2,128,1536]{2,1,0:T(8,128)}, u32[]{:S(2)}) copy-start(f32[2,128,1536]{2,1,0:T(8,128)} %bitcast_add_fusion.4.refs_3_) | copy-start | bytes 4718596
  590.9 43.4 %copy-start.15 = (f32[2,128,1536]{2,1,0:T(8,128)S(1)}, f32[2,128,1536]{2,1,0:T(8,128)}, u32[]{:S(2)}) copy-start(f32[2,128,1536]{2,1,0:T(8,128)} %bitcast_add_fusion.5.refs_2_) | copy-start | bytes 4718596
  636.6 9.3 %copy-start.14 = (f32[2,192,1024]{2,1,0:T(8,128)S(1)}, f32[2,192,1024]{2,1,0:T(8,128)}, u32[]{:S(2)}) copy-start(f32[2,192,1024]{2,1,0:T(8,128)} %bitcast_add_fusion.3.refs_4_) | copy-start | bytes 4718596
  638.4 7.4 %copy-start.28 = (f32[192,1024]{1,0:T(8,128)S(1)}, f32[192,1024]{1,0:T(8,128)}, u32[]{:S(2)}) copy-start(f32[192,1024]{1,0:T(8,128)} %get-tuple-element.72) | copy-start | bytes 2359300
  640.3 6.5 collective-permute-start.8
  651.8 3.1 copy-start.30
  651.8 3.9 copy-start.1
  (1 other events, 0.8 us)

commit v4 on v3

--- a/solution.py
+++ b/solution.py
@@ -17,7 +17,7 @@
 
 def rope_tables(pos_ids):
     inv_freq = ROPE_BASE ** (-(jnp.arange(HEAD_DIM // 2, dtype=jnp.float32) * (2.0 / HEAD_DIM)))
-    angles = pos_ids.astype(jnp.float32)[..., None] * inv_freq
+    angles = pos_ids.astype(jnp.float32)[None, :] * inv_freq[:, None]
     return jnp.cos(angles), jnp.sin(angles)
 
 
@@ -36,6 +36,28 @@
 
 
 MESH = pl.DeviceIdType.MESH
+
+
+def by_rows(i):
+    return i, 0
+
+
+def by_cols(i):
+    return 0, i
+
+
+def whole(i):
+    return 0, 0
+
+
+def head(h):
+    return slice(h * HEAD_DIM, (h + 1) * HEAD_DIM)
+
+
+def pick(t, i):
+    return lax.dynamic_index_in_dim(t, i, 0, False)
+
+
 ORDERS = ('xyz', 'yzx', 'zxy')
 
 
@@ -83,22 +105,17 @@
 
 class CubeGather:
     def __init__(self, here, wires, jobs):
-        self.stages = [[], [], []]
-        self.need = [[], []]
-        self.rest = []
+        firsts, seconds, thirds = [], [], []
         for out, suffix, (a, b, e) in jobs:
             def mk(freed, flipped, d):
                 reg = here.region(freed, flipped) + suffix
                 return wires.copy(out.at[reg], out.at[reg], here.peer(d))
-            first = [mk('', '', d) for d in (a, b, e)]
-            second = [mk('', a, d) for d in (b, e)]
-            third = [mk(a, b, e)]
-            self.stages[0] += first
-            self.stages[1] += second
-            self.stages[2] += third
-            self.need[0].append(first[0])
-            self.need[1] += [first[1], second[0]]
-            self.rest += [first[2], second[1]] + third
+            firsts.append([mk('', '', d) for d in (a, b, e)])
+            seconds.append([mk('', a, d) for d in (b, e)])
+            thirds.append(mk(a, b, e))
+        self.stages = [[f[i] for i in range(3) for f in firsts], [t[i] for i in range(2) for t in seconds], thirds]
+        self.need = [[f[0] for f in firsts], [f[1] for f in firsts] + [t[0] for t in seconds]]
+        self.rest = [[f[2], t[1], e] for f, t, e in zip(firsts, seconds, thirds)]
 
     def start(self, i):
         for c in self.need[i - 1] if i else ():
@@ -106,9 +123,10 @@
         for c in self.stages[i]:
             c.start()
 
-    def arrive(self):
-        for c in self.rest:
-            c.wait_recv()
+    def arrive(self, lo=0, hi=None):
+        for job in self.rest[lo:hi]:
+            for c in job:
+                c.wait_recv()
 
     def drain(self):
         for st in self.stages:
@@ -151,9 +169,8 @@
                     pltpu.make_async_copy(w3.at[c], o3.at[zyx + (c,)], local_sem.at[1]),
                     pltpu.make_async_copy(w2, o2.at[zyx], local_sem.at[2]),
                     pltpu.make_async_copy(wo, oo.at[zyx + (c,)], local_sem.at[3])]
-        jobs = [(o1, (), ORDERS[0]), (o3, (), ORDERS[1]), (o2, (), ORDERS[2])]
-        for (off, n), order in zip(col_chunks(wo.shape[1], 3), ORDERS):
-            jobs.append((oo, (c, slice(None), slice(off, off + n)), order))
+        jobs = [(oo, (c, slice(None), slice(off, off + n)), order) for (off, n), order in zip(col_chunks(wo.shape[1], 3), ORDERS)]
+        jobs += [(o1, (), ORDERS[0]), (o3, (), ORDERS[1]), (o2, (), ORDERS[2])]
         self.cube = CubeGather(here, wires, jobs)
         self.post = wires.copy(oo.at[:, :, :, c], oo.at[:, :, :, c], nc)
 
@@ -167,8 +184,9 @@
         self.cube.start(0)
 
     def end(self):
-        self.cube.arrive()
+        self.cube.arrive(0, 3)
         self.post.start()
+        self.cube.arrive(3)
         self.post.wait()
         self.cube.drain()
 
@@ -191,15 +209,30 @@
     return [jax.ShapeDtypeStruct((*((2,) * (nd - 1)), *a.shape[nd:]), a.dtype) for a in arrs]
 
 
-def halve_add(arrs, got, nd):
-    here = Spot()
-    out = []
-    for i, (g, r) in enumerate(zip(arrs, got)):
-        order = ORDERS[i % 3]
-        live = [d for d in 'zyx' if d in order[:nd]]
-        d = order[nd - 1]
-        out.append(lax.dynamic_index_in_dim(g, here.bits[d], live.index(d), False) + r)
+def part_of(here, t, order, nd, flip):
+    live = [d for d in 'zyx' if d in order[:nd]]
+    d = order[nd - 1]
+    bit = here.bits[d]
+    return lax.dynamic_index_in_dim(t, 1 - bit if flip else bit, live.index(d), False)
+
+
+def total(terms):
+    out = terms[0]
+    for t in terms[1:]:
+        out = out + t
     return out
+
+
+def to_send(here, terms, nd):
+    return [total([part_of(here, t, ORDERS[i % 3], nd, True) for t in ts]) for i, ts in enumerate(terms)]
+
+
+def after(here, terms, got, nd):
+    return [[part_of(here, t, ORDERS[i % 3], nd, False) for t in ts] + [r] for i, (ts, r) in enumerate(zip(terms, got))]
+
+
+def wide_tables(cos_t, sin_t):
+    return jnp.concatenate([cos_t, cos_t], axis=0).T, jnp.concatenate([-sin_t, sin_t], axis=0).T
 
 
 def proj_kernel(nrot, x_ref, g_ref, w_ref, cos_ref, sin_ref, u_ref, q_ref, k_ref, v_ref, kt_ref, vt_ref):
@@ -207,37 +240,35 @@
     inv = lax.rsqrt(jnp.mean(x * x, axis=-1, keepdims=True) + NORM_EPS)
     u = (x * inv * g_ref[0:1, :].astype(jnp.float32)).astype(jnp.bfloat16)
     u_ref[...] = u
-    cos, sin = cos_ref[...], sin_ref[...]
+    cos, sin = wide_tables(cos_ref[...], sin_ref[...])
     for h in range(nrot + 2):
-        t = jnp.dot(u, w_ref[:, h * HEAD_DIM:(h + 1) * HEAD_DIM], preferred_element_type=jnp.float32)
+        t = jnp.dot(u, w_ref[:, head(h)], preferred_element_type=jnp.float32)
         if h <= nrot:
             t = t * cos + pltpu.roll(t, HEAD_DIM // 2, 1) * sin
         if h < nrot:
-            q_ref[:, h * HEAD_DIM:(h + 1) * HEAD_DIM] = t.astype(jnp.bfloat16)
+            q_ref[:, head(h)] = t.astype(jnp.bfloat16)
         else:
             n_ref, t_ref = (k_ref, kt_ref) if h == nrot else (v_ref, vt_ref)
             n_ref[...] = t.astype(jnp.bfloat16)
             t_ref[...] = t.T.astype(jnp.bfloat16)
 
 
-def project(x, gain, w, cosw, sinw, bt=512):
+def project(x, gain, w, cos_t, sin_t, bt=512):
     seq, dim = x.shape
     grp = w.shape[1]
     nq = grp // HEAD_DIM - 2
-    row = lambda i: (i, 0)
-    whole = lambda i: (0, 0)
     bf = jnp.bfloat16
     return pl.pallas_call(
         functools.partial(proj_kernel, nq), grid=(seq // bt,),
-        in_specs=[pl.BlockSpec((bt, dim), row), pl.BlockSpec((16, dim), whole), pl.BlockSpec((dim, grp), whole),
-                  pl.BlockSpec((bt, HEAD_DIM), row), pl.BlockSpec((bt, HEAD_DIM), row)],
-        out_specs=[pl.BlockSpec((bt, dim), row), pl.BlockSpec((bt, nq * HEAD_DIM), row), pl.BlockSpec((bt, HEAD_DIM), row), pl.BlockSpec((bt, HEAD_DIM), row),
-                   pl.BlockSpec((HEAD_DIM, bt), lambda i: (0, i)), pl.BlockSpec((HEAD_DIM, bt), lambda i: (0, i))],
+        in_specs=[pl.BlockSpec((bt, dim), by_rows), pl.BlockSpec((16, dim), whole), pl.BlockSpec((dim, grp), whole),
+                  pl.BlockSpec((cos_t.shape[0], bt), by_cols), pl.BlockSpec((cos_t.shape[0], bt), by_cols)],
+        out_specs=[pl.BlockSpec((bt, dim), by_rows), pl.BlockSpec((bt, nq * HEAD_DIM), by_rows), pl.BlockSpec((bt, HEAD_DIM), by_rows), pl.BlockSpec((bt, HEAD_DIM), by_rows),
+                   pl.BlockSpec((HEAD_DIM, bt), by_cols), pl.BlockSpec((HEAD_DIM, bt), by_cols)],
         out_shape=[jax.ShapeDtypeStruct((seq, dim), bf), jax.ShapeDtypeStruct((seq, nq * HEAD_DIM), bf), jax.ShapeDtypeStruct((seq, HEAD_DIM), bf),
                    jax.ShapeDtypeStruct((seq, HEAD_DIM), bf), jax.ShapeDtypeStruct((HEAD_DIM, seq), bf), jax.ShapeDtypeStruct((HEAD_DIM, seq), bf)],
         cost_estimate=pl.CostEstimate(flops=2 * seq * dim * grp, bytes_accessed=32 << 20, transcendentals=0),
         compiler_params=pltpu.CompilerParams(vmem_limit_bytes=48 << 20), name="project",
-    )(x, gain, w, cosw, sinw)
+    )(x, gain, w, cos_t, sin_t)
 
 
 LOG2E = math.log2(math.e)
@@ -247,7 +278,7 @@
 BIG = -1e30
 
 
-def fwd_kernel(bq, bk, q_ref, k_ref, vt_ref, w1, w3, w2, wo, o_ref, lse_ref, o1, o3, o2, oo, send_sem, recv_sem, local_sem):
+def fwd_kernel(bq, bk, q_ref, k_ref, vt_ref, w1, w3, w2, wo, o_ref, ot_ref, lse_ref, o1, o3, o2, oo, send_sem, recv_sem, local_sem):
     i = pl.program_id(0)
     last = pl.num_programs(0) - 1
     here = Spot()
@@ -263,7 +294,7 @@
         carry_over.cube.start(1)
 
     heads = q_ref.shape[1] // HEAD_DIM
-    qs = [q_ref[:, h * HEAD_DIM:(h + 1) * HEAD_DIM] for h in range(heads)]
+    qs = [q_ref[:, head(h)] for h in range(heads)]
 
     def block(j, carry, masked):
         rows = pl.ds(pl.multiple_of(j * bk, bk), bk)
@@ -293,7 +324,8 @@
     for h in range(heads):
         m, l, acc = carry[h]
         o = acc / l
-        o_ref[:, h * HEAD_DIM:(h + 1) * HEAD_DIM] = o.T.astype(jnp.bfloat16)
+        o_ref[:, head(h)] = o.T.astype(jnp.bfloat16)
+        ot_ref[head(h), :] = o.astype(jnp.bfloat16)
         lse_ref[h:h + 1, :] = m * SCALE2 + jnp.log2(l)
 
     @pl.when(i == last)
@@ -310,12 +342,12 @@
     return pl.pallas_call(
         functools.partial(fwd_kernel, bq, bk),
         grid=(seq // bq,),
-        in_specs=[pl.BlockSpec((bq, width), lambda i: (i, 0)),
-                  pl.BlockSpec((seq, HEAD_DIM), lambda i: (0, 0)),
-                  pl.BlockSpec((HEAD_DIM, seq), lambda i: (0, 0))] + [vm] * 4,
-        out_specs=[pl.BlockSpec((bq, width), lambda i: (i, 0)),
-                   pl.BlockSpec((heads, bq), lambda i: (0, i))] + [an] * 4,
-        out_shape=[jax.ShapeDtypeStruct((seq, width), jnp.bfloat16), jax.ShapeDtypeStruct((heads, seq), jnp.float32)] + gathered(ws),
+        in_specs=[pl.BlockSpec((bq, width), by_rows),
+                  pl.BlockSpec((seq, HEAD_DIM), whole),
+                  pl.BlockSpec((HEAD_DIM, seq), whole)] + [vm] * 4,
+        out_specs=[pl.BlockSpec((bq, width), by_rows), pl.BlockSpec((width, bq), by_cols),
+                   pl.BlockSpec((heads, bq), by_cols)] + [an] * 4,
+        out_shape=[jax.ShapeDtypeStruct((seq, width), jnp.bfloat16), jax.ShapeDtypeStruct((width, seq), jnp.bfloat16), jax.ShapeDtypeStruct((heads, seq), jnp.float32)] + gathered(ws),
         scratch_shapes=[pltpu.SemaphoreType.DMA((NW,)), pltpu.SemaphoreType.DMA((NW,)), pltpu.SemaphoreType.DMA((4,))],
         cost_estimate=pl.CostEstimate(flops=2 * seq * seq * width * 2, bytes_accessed=8 << 20, transcendentals=seq * seq),
         compiler_params=comm_params(cid, vmem_limit_bytes=56 << 20),
@@ -333,11 +365,10 @@
     v = v_ref[...]
     kt = kt_ref[...]
     here = Spot()
-    carry_over = halve_copies(here, Wires(send_sem, recv_sem), 3, (g1, g3, g2), (r1, r3, r2))
-
-    def turned(t, rows):
-        t = t.astype(jnp.bfloat16).astype(jnp.float32)
-        return (t * cos_ref[rows, :] - pltpu.roll(t, HEAD_DIM // 2, 1) * sin_ref[rows, :]).astype(jnp.bfloat16)
+    wires = Wires(send_sem, recv_sem)
+    carry_over = halve_copies(here, wires, 3, (g1, g3, g2), (r1, r3, r2))
+
+    half = HEAD_DIM // 2
 
     @pl.when(j == 0)
     def _():
@@ -349,7 +380,7 @@
         def prep(i, c):
             rows = pl.ds(pl.multiple_of(i * bq, bq), bq)
             for h in range(heads):
-                cols = slice(h * HEAD_DIM, (h + 1) * HEAD_DIM)
+                cols = head(h)
                 prod = o_ref[rows, cols].astype(jnp.float32) * d_ref[rows, cols].astype(jnp.float32)
                 rd[h:h + 1, rows] = jnp.sum(prod.T, axis=0, keepdims=True)
             return c
@@ -361,7 +392,7 @@
     def block(i, masked):
         rows = pl.ds(pl.multiple_of(i * bq, bq), bq)
         for h in range(heads):
-            cols = slice(h * HEAD_DIM, (h + 1) * HEAD_DIM)
+            cols = head(h)
             q = q_ref[rows, cols]
             d = d_ref[rows, cols]
             s = lax.dot_general(k, q, NT, preferred_element_type=jnp.float32)
@@ -382,34 +413,38 @@
         block(first + t, True)
     lax.fori_loop(first + ndiag, nq, lambda i, c: (block(i, False), c)[1], 0)
     own = pl.ds(pl.multiple_of(j * bk, bk), bk)
-    out_ref[own, width:width + HEAD_DIM] = turned(dka[...], own)
+    cosw, sinw = wide_tables(cos_ref[:, own], sin_ref[:, own])
+    dk = dka[...].astype(jnp.bfloat16).astype(jnp.float32)
+    out_ref[own, width:width + HEAD_DIM] = (dk * cosw - pltpu.roll(dk, half, 1) * sinw).astype(jnp.bfloat16)
     out_ref[own, width + HEAD_DIM:] = dva[...].astype(jnp.bfloat16)
 
     @pl.when(j == nk - 1)
     def _():
         def fin(i, c):
             rows = pl.ds(pl.multiple_of(i * bq, bq), bq)
+            cos, sin = cos_ref[:, rows], sin_ref[:, rows]
             for h in range(heads):
-                cols = slice(h * HEAD_DIM, (h + 1) * HEAD_DIM)
-                out_ref[rows, cols] = turned(dqt[cols, rows].T, rows)
+                cols = head(h)
+                t = dqt[cols, rows].astype(jnp.bfloat16).astype(jnp.float32)
+                lo, hi = t[:half], t[half:]
+                out_ref[rows, cols] = jnp.concatenate([lo * cos + hi * sin, hi * cos - lo * sin], axis=0).T.astype(jnp.bfloat16)
             return c
         lax.fori_loop(0, nq, fin, 0)
         for cp in carry_over:
             cp.wait()
 
 
-def flash_bwd(q, o, d, k, kt, v, lse, cosw, sinw, gs, cid, bq=512, bk=512):
+def flash_bwd(q, o, d, k, kt, v, lse, cos_t, sin_t, gs, cid, bq=512, bk=512):
     seq, width = q.shape
     heads = width // HEAD_DIM
-    whole = lambda j: (0, 0)
     an = pl.BlockSpec(memory_space=pl.ANY)
     return pl.pallas_call(
         functools.partial(bwd_kernel, bq, bk),
         grid=(seq // bk,),
         in_specs=[pl.BlockSpec((seq, width), whole), pl.BlockSpec((seq, width), whole), pl.BlockSpec((seq, width), whole),
-                  pl.BlockSpec((bk, HEAD_DIM), lambda j: (j, 0)), pl.BlockSpec((HEAD_DIM, bk), lambda j: (0, j)),
-                  pl.BlockSpec((bk, HEAD_DIM), lambda j: (j, 0)),
-                  pl.BlockSpec((heads, seq), whole), pl.BlockSpec((seq, HEAD_DIM), whole), pl.BlockSpec((seq, HEAD_DIM), whole)] + [an] * 3,
+                  pl.BlockSpec((bk, HEAD_DIM), by_rows), pl.BlockSpec((HEAD_DIM, bk), by_cols),
+                  pl.BlockSpec((bk, HEAD_DIM), by_rows),
+                  pl.BlockSpec((heads, seq), whole), pl.BlockSpec(cos_t.shape, whole), pl.BlockSpec(cos_t.shape, whole)] + [an] * 3,
         out_specs=[pl.BlockSpec((seq, width + 2 * HEAD_DIM), whole)] + [an] * 3,
         out_shape=[jax.ShapeDtypeStruct((seq, width + 2 * HEAD_DIM), jnp.bfloat16)] + halve_shapes(gs, 3),
         scratch_shapes=[pltpu.VMEM((width, seq), jnp.float32), pltpu.VMEM((bk, HEAD_DIM), jnp.float32), pltpu.VMEM((bk, HEAD_DIM), jnp.float32),
@@ -417,7 +452,7 @@
         cost_estimate=pl.CostEstimate(flops=5 * seq * seq * width * 2 // 2, bytes_accessed=16 << 20, transcendentals=seq * seq),
         compiler_params=comm_params(cid, vmem_limit_bytes=58 << 20),
         name="flash_bwd",
-    )(q, o, d, k, kt, v, lse, cosw, sinw, *gs)
+    )(q, o, d, k, kt, v, lse, cos_t, sin_t, *gs)
 
 
 class PlaneGather:
@@ -425,7 +460,7 @@
 
     def __init__(self, here, wires, src, out, local_sem):
         h = src.shape[0] // 2
-        A, B = slice(0, h), slice(h, 2 * h)
+        A, B = slice(h), slice(h, None)
         s = here.s
         sx, sy, sc = here.peer('x')[1], here.peer('y')[1], here.peer('c')[1]
         sd = here.s + 2 - 4 * here.x + 4 - 8 * here.y
@@ -477,44 +512,108 @@
         self.local.wait()
 
 
-NG = PlaneGather.N + 2 * 6 + 1
-
-
-def dh_kernel(src, wg, out, og, send_sem, recv_sem, local_sem):
+def dh_kernel(src, out, send_sem, recv_sem, local_sem):
     here = Spot()
-    greet(cube_targets(here))
+    greet([here.peer(d) for d in 'xyc'])
+    g = PlaneGather(here, Wires(send_sem, recv_sem), src, out, local_sem)
+    g.start_first()
+    g.start_second()
+    g.relay()
+    g.finish()
+
+
+def gather_dh(src, cid):
+    rows, cols = src.shape
+    n = PlaneGather.N
+    return pl.pallas_call(
+        dh_kernel, in_specs=[pl.BlockSpec(memory_space=pltpu.VMEM)], out_specs=pl.BlockSpec(memory_space=pl.ANY),
+        out_shape=jax.ShapeDtypeStruct((8, rows, cols), src.dtype),
+        scratch_shapes=[pltpu.SemaphoreType.DMA((n,)), pltpu.SemaphoreType.DMA((n,)), pltpu.SemaphoreType.DMA],
+        cost_estimate=busy(40), compiler_params=comm_params(cid), name="gather_dh",
+    )(src)
+
+
+def mlp_kernel(u_ref, d_ref, w1_ref, w3_ref, w2_ref, wg, y_ref, dx_ref, g1_ref, g3_ref, g2_ref, og, ut, send_sem, recv_sem, local_sem):
+    j = pl.program_id(0)
+    last = pl.num_programs(0) - 1
+    here = Spot()
+    c = here.c
     wires = Wires(send_sem, recv_sem)
-    c = here.c
-    loc = pltpu.make_async_copy(wg, og.at[here.region('') + (c,)], local_sem.at[1])
-    g = PlaneGather(here, wires, src, out, local_sem.at[0])
-    jobs = [(og, (c, slice(None), slice(off, off + n)), order) for (off, n), order in zip(col_chunks(wg.shape[1], 2), ('xyz', 'yxz'))]
+    loc = pltpu.make_async_copy(wg, og.at[here.region('') + (c,)], local_sem)
+    jobs = [(og, (c, slice(None), slice(off, off + n)), order) for (off, n), order in zip(col_chunks(wg.shape[1], 3), ORDERS)]
     cube = CubeGather(here, wires, jobs)
     post = wires.copy(og.at[:, :, :, c], og.at[:, :, :, c], here.peer('c'))
-    loc.start()
-    loc.wait()
-    cube.start(0)
-    g.start_first()
-    cube.start(1)
-    g.start_second()
-    g.relay()
-    cube.start(2)
-    g.finish()
-    cube.arrive()
-    post.start()
-    post.wait()
-    cube.drain()
-
-
-def gather_dh(src, wg, cid):
-    rows, cols = src.shape
+    toks = u_ref.shape[0]
+
+    @pl.when(j == 0)
+    def _():
+        greet(cube_targets(here))
+        loc.start()
+        loc.wait()
+        cube.start(0)
+        y_ref[...] = jnp.zeros_like(y_ref)
+        dx_ref[...] = jnp.zeros_like(dx_ref)
+
+        def flip(i, carry):
+            part = pl.ds(pl.multiple_of(i * 128, 128), 128)
+            ut[:, part] = u_ref[part, :].astype(jnp.float32).T.astype(jnp.bfloat16)
+            return carry
+        lax.fori_loop(0, toks // 128, flip, 0)
+
+    @pl.when(j == 1)
+    def _():
+        cube.start(1)
+
+    @pl.when(j == 3)
+    def _():
+        cube.start(2)
+
+    @pl.when(j == last)
+    def _():
+        cube.arrive()
+        post.start()
+
+    f32 = jnp.float32
+    u, d = u_ref[...], d_ref[...]
+    w1, w3, w2 = w1_ref[...], w3_ref[...], w2_ref[...]
+    gate = jnp.dot(u, w1, preferred_element_type=f32)
+    up = jnp.dot(u, w3, preferred_element_type=f32)
+    act = lax.dot_general(d, w2, NT, preferred_element_type=f32)
+    sig = jax.nn.sigmoid(gate)
+    silu = gate * sig
+    z = (silu * up).astype(jnp.bfloat16)
+    da = (act * up * sig * (1.0 + gate * (1.0 - sig))).astype(jnp.bfloat16)
+    dc = (act * silu).astype(jnp.bfloat16)
+    y_ref[...] += jnp.dot(z, w2, preferred_element_type=f32)
+    dx_ref[...] += lax.dot_general(da, w1, NT, preferred_element_type=f32) + lax.dot_general(dc, w3, NT, preferred_element_type=f32)
+    g1_ref[...] = jnp.dot(ut[...], da, preferred_element_type=f32)
+    g3_ref[...] = jnp.dot(ut[...], dc, preferred_element_type=f32)
+    g2_ref[...] = lax.dot_general(z, d, (((0,), (0,)), ((), ())), preferred_element_type=f32)
+
+    @pl.when(j == last)
+    def _():
+        post.wait()
+        cube.drain()
+
+
+def mlp(u, d, w1, w3, w2, wg, cid, bh=256):
+    toks, dim = u.shape
+    half = w1.shape[1]
+    f32 = jnp.float32
     vm = pl.BlockSpec(memory_space=pltpu.VMEM)
     an = pl.BlockSpec(memory_space=pl.ANY)
     return pl.pallas_call(
-        dh_kernel, in_specs=[vm] * 2, out_specs=[an] * 2,
-        out_shape=[jax.ShapeDtypeStruct((8, rows, cols), src.dtype), jax.ShapeDtypeStruct((2, 2, 2, 2, *wg.shape), wg.dtype)],
-        scratch_shapes=[pltpu.SemaphoreType.DMA((NG,)), pltpu.SemaphoreType.DMA((NG,)), pltpu.SemaphoreType.DMA((2,))],
-        cost_estimate=busy(50), compiler_params=comm_params(cid), name="gather_dh",
-    )(src, wg)
+        mlp_kernel, grid=(half // bh,),
+        in_specs=[vm, vm, pl.BlockSpec((dim, bh), by_cols), pl.BlockSpec((dim, bh), by_cols), pl.BlockSpec((bh, dim), by_rows), vm],
+        out_specs=[pl.BlockSpec((toks, dim), whole), pl.BlockSpec((toks, dim), whole), pl.BlockSpec((dim, bh), by_cols), pl.BlockSpec((dim, bh), by_cols),
+                   pl.BlockSpec((bh, dim), by_rows), an],
+        out_shape=[jax.ShapeDtypeStruct((toks, dim), f32), jax.ShapeDtypeStruct((toks, dim), f32), jax.ShapeDtypeStruct((dim, half), f32),
+                   jax.ShapeDtypeStruct((dim, half), f32), jax.ShapeDtypeStruct((half, dim), f32),
+                   jax.ShapeDtypeStruct((2, 2, 2, 2, *wg.shape), wg.dtype)],
+        scratch_shapes=[pltpu.VMEM((dim, toks), jnp.bfloat16), pltpu.SemaphoreType.DMA((19,)), pltpu.SemaphoreType.DMA((19,)), pltpu.SemaphoreType.DMA],
+        cost_estimate=pl.CostEstimate(flops=18 * toks * dim * half, bytes_accessed=48 << 20, transcendentals=toks * half),
+        compiler_params=comm_params(cid, vmem_limit_bytes=58 << 20), name="mlp",
+    )(u, d, w1, w3, w2, wg)
 
 
 def entry_kernel(x_ref, w_ref, meta_ref, pos_ref, xa, wa, ma, pa, send_sem, recv_sem, local_sem):
@@ -580,7 +679,8 @@
     piece = lambda i: pl.ds(pl.multiple_of(i * rows, rows), rows)
     mine = pl.ds(pl.multiple_of(s * width, width), width)
     cs = [wires.copy(src.at[piece(t[1])], out.at[:, mine], t) for t in peers]
-    cs += halve_copies(here, wires, 2, gs, rs)
+    cs += [wires.copy(g, r, here.peer(order[1])) for g, r, order in zip(gs[:3], rs, ORDERS)]
+    cs += [wires.copy(g.at[1 - here.z], r, here.peer('z')) for g, r in zip(gs[3:], rs[3:])]
     for c in cs:
         c.start()
     a = pltpu.make_async_copy(src.at[piece(s)], stage, local_sem.at[0])
@@ -597,43 +697,98 @@
     seq, width = src.shape
     rows, n = seq // 8, len(gs)
     an = pl.BlockSpec(memory_space=pl.ANY)
+    back = [jax.ShapeDtypeStruct(g.shape if i < 3 else g.shape[1:], g.dtype) for i, g in enumerate(gs)]
     out = pl.pallas_call(
         functools.partial(regroup_kernel, n), in_specs=[an] * (1 + n), out_specs=[an] * (1 + n),
-        out_shape=[jax.ShapeDtypeStruct((rows, 8 * width), src.dtype)] + halve_shapes(gs, 2),
+        out_shape=[jax.ShapeDtypeStruct((rows, 8 * width), src.dtype)] + back,
         scratch_shapes=[pltpu.SemaphoreType.DMA((7 + n,)), pltpu.SemaphoreType.DMA((7 + n,)), pltpu.SemaphoreType.DMA((2,)), pltpu.VMEM((rows, width), src.dtype)],
         cost_estimate=busy(70 if n else 25), compiler_params=comm_params(cid), name=name,
     )(src, *gs)
     return out[0], out[1:]
 
 
-def owner_kernel(n, *refs):
-    a, b, gs, oa, ob, rs = refs[0], refs[1], refs[2:2 + n], refs[2 + n], refs[3 + n], refs[4 + n:4 + 2 * n]
-    send_sem, recv_sem, local_sem = refs[4 + 2 * n:]
+def back_kernel(t_ref, w_ref, x_ref, gain_ref, res_ref, a, g1, g3, g2, dx_ref, gg_ref, oa, r1, r3, r2, acc, send_sem, recv_sem, local_sem):
+    j = pl.program_id(0)
+    bn = w_ref.shape[0]
     here = Spot()
     peers = here.others()
-    greet(peers + [here.peer('z')])
     wires = Wires(send_sem, recv_sem)
     s = here.s
-    cs = halve_copies(here, wires, 1, gs, rs)
-    cs += [wires.copy(r.at[t[1]], o.at[s], t) for t in peers for r, o in ((a, oa), (b, ob))]
-    loc = [pltpu.make_async_copy(a.at[s], oa.at[s], local_sem.at[0]), pltpu.make_async_copy(b.at[s], ob.at[s], local_sem.at[1])]
-    for c in cs + loc:
-        c.start()
-    for c in cs + loc:
-        c.wait()
-
-
-def owner(a, b, gs, cid):
-    n = len(gs)
+    cs = [wires.copy(g, r, here.peer(order[0])) for g, r, order in zip((g1, g3, g2), (r1, r3, r2), ORDERS)]
+    cs += [wires.copy(a.at[t[1]], oa.at[s], t) for t in peers]
+    loc = pltpu.make_async_copy(a.at[s], oa.at[s], local_sem)
+
+    @pl.when(j == 0)
+    def _():
+        greet(peers + [here.peer('z')])
+        for c in cs:
+            c.start()
+        loc.start()
+
+    acc[:, pl.ds(pl.multiple_of(j * bn, bn), bn)] = lax.dot_general(t_ref[...], w_ref[...], NT, preferred_element_type=jnp.float32)
+
+    @pl.when(j == pl.num_programs(0) - 1)
+    def _():
+        gg_ref[...] = jnp.zeros_like(gg_ref)
+        gain = gain_ref[0:1, :].astype(jnp.float32)
+
+        def rows_of(i, carry):
+            part = pl.ds(pl.multiple_of(i * HEAD_DIM, HEAD_DIM), HEAD_DIM)
+            x = x_ref[part, :].astype(jnp.float32)
+            inv = lax.rsqrt(jnp.mean(x * x, axis=-1, keepdims=True) + NORM_EPS)
+            normed = x * inv
+            d_out = acc[part, :]
+            d_normed = d_out * gain
+            gg_ref[...] += jnp.sum(d_out * normed, axis=0, keepdims=True)
+            grad_in = inv * (d_normed - normed * jnp.mean(d_normed * normed, axis=-1, keepdims=True))
+            dx_ref[part, :] = (res_ref[part, :] + grad_in).astype(jnp.bfloat16)
+            return carry
+        lax.fori_loop(0, x_ref.shape[0] // HEAD_DIM, rows_of, 0)
+        for c in cs:
+            c.wait()
+        loc.wait()
+
+
+def back_project(t, w, x, gain, res, a, gs, cid, bn=256):
+    toks, inner = t.shape
+    dim = w.shape[0]
     vm = pl.BlockSpec(memory_space=pltpu.VMEM)
     an = pl.BlockSpec(memory_space=pl.ANY)
     out = pl.pallas_call(
-        functools.partial(owner_kernel, n), in_specs=[vm] * 2 + [an] * n, out_specs=[vm] * 2 + [an] * n,
-        out_shape=[jax.ShapeDtypeStruct(t.shape, t.dtype) for t in (a, b)] + halve_shapes(gs, 1),
-        scratch_shapes=[pltpu.SemaphoreType.DMA((14 + n,)), pltpu.SemaphoreType.DMA((14 + n,)), pltpu.SemaphoreType.DMA((2,))],
-        cost_estimate=busy(30), compiler_params=comm_params(cid), name="owner",
-    )(a, b, *gs)
-    return out[0], out[1], out[2:]
+        back_kernel, grid=(dim // bn,),
+        in_specs=[vm, pl.BlockSpec((bn, inner), by_rows)] + [vm] * 4 + [an] * 3,
+        out_specs=[pl.BlockSpec((toks, dim), whole), pl.BlockSpec((1, dim), whole)] + [an] * 4,
+        out_shape=[jax.ShapeDtypeStruct((toks, dim), jnp.bfloat16), jax.ShapeDtypeStruct((1, dim), jnp.float32), jax.ShapeDtypeStruct(a.shape, a.dtype)]
+        + [jax.ShapeDtypeStruct(g.shape, g.dtype) for g in gs],
+        scratch_shapes=[pltpu.VMEM((toks, dim), jnp.float32), pltpu.SemaphoreType.DMA((10,)), pltpu.SemaphoreType.DMA((10,)), pltpu.SemaphoreType.DMA],
+        cost_estimate=busy(35), compiler_params=comm_params(cid, vmem_limit_bytes=48 << 20), name="back_project",
+    )(t, w, x, gain, res, a, *gs)
+    return out[0], out[1], out[2], out[3:]
+
+
+def last_kernel(b, p1, p3, ob, q1, q3, send_sem, recv_sem, local_sem):
+    here = Spot()
+    peers = here.others()
+    greet(peers)
+    wires = Wires(send_sem, recv_sem)
+    s, nc = here.s, here.peer('c')
+    cs = [wires.copy(p.at[1 - here.c], q, nc) for p, q in ((p1, q1), (p3, q3))]
+    cs += [wires.copy(b.at[t[1]], ob.at[s], t) for t in peers]
+    loc = pltpu.make_async_copy(b.at[s], ob.at[s], local_sem)
+    for c in cs + [loc]:
+        c.start()
+    for c in cs + [loc]:
+        c.wait()
+
+
+def last_exchange(b, p1, p3, cid):
+    vm = pl.BlockSpec(memory_space=pltpu.VMEM)
+    return pl.pallas_call(
+        last_kernel, in_specs=[vm] * 3, out_specs=[vm] * 3,
+        out_shape=[jax.ShapeDtypeStruct(b.shape, b.dtype)] + [jax.ShapeDtypeStruct(p.shape[1:], p.dtype) for p in (p1, p3)],
+        scratch_shapes=[pltpu.SemaphoreType.DMA((9,)), pltpu.SemaphoreType.DMA((9,)), pltpu.SemaphoreType.DMA],
+        cost_estimate=busy(5), compiler_params=comm_params(cid), name="last_exchange",
+    )(b, p1, p3)
 
 
 def dot_tokens(left_op, right_op):
@@ -690,12 +845,11 @@
     w_own = w_own.reshape(dim, grp)
     gain1 = meta_all[:, :, 0, :rows].reshape(dim)
     gain2 = meta_all[:, :, 1, :rows].reshape(dim)
-    cos_tab, sin_tab = rope_tables(pos_all.reshape(seq))
-
-    cosw = jnp.concatenate([cos_tab, cos_tab], axis=1)
-    sinw = jnp.concatenate([-sin_tab, sin_tab], axis=1)
-    u_all, q_own, k_own, v_own, k_t, v_t = project(x_all, jnp.broadcast_to(gain1[None], (16, dim)), w_own, cosw, sinw)
-    o_own, lse, w1, w3, w2, wo = flash_fwd(q_own, k_own, v_t, (split_cols(w_gate), split_cols(w_up), w_down, w_out), 2)
+    cos_t, sin_t = rope_tables(pos_all.reshape(seq))
+
+    gain1_rows = jnp.broadcast_to(gain1[None], (16, dim))
+    u_all, q_own, k_own, v_own, k_t, v_t = project(x_all, gain1_rows, w_own, cos_t, sin_t)
+    o_own, o_t, lse, w1, w3, w2, wo = flash_fwd(q_own, k_own, v_t, (split_cols(w_gate), split_cols(w_up), w_down, w_out), 2)
     ffn_half = w1.shape[-1]
     w1, w3 = w1.reshape(dim, ffn_half), w3.reshape(dim, ffn_half)
     w2 = w2.reshape(ffn_half, dim)
@@ -705,50 +859,37 @@
     u_mlp, normed2, inv_rms2 = rms_norm(residual, gain2)
     u_pair = jnp.concatenate([u_mlp, swap_core(u_mlp)], axis=0)
     d_pair = jnp.concatenate([d_layer, swap_core(d_layer)], axis=0)
-    gate_pre = dot_on(u_pair, w1)
-    up_pre = dot_on(u_pair, w3)
-    sig_gate = jax.nn.sigmoid(gate_pre)
-    silu_gate = gate_pre * sig_gate
-    mlp_act = (silu_gate * up_pre).astype(jnp.bfloat16)
-    y_part = dot_on(mlp_act, w2)
+    y_part, d_part, g1, g3, g2, wg = mlp(u_pair, d_pair, w1, w3, w2, w_flat, 7)
     layer_out = (residual.astype(jnp.float32) + (y_part[:tok] + swap_core(y_part[tok:]))).astype(jnp.bfloat16)
 
-    d_act = dot_back(d_pair, w2)
-    d_gate = (d_act * up_pre * sig_gate * (1.0 + gate_pre * (1.0 - sig_gate))).astype(jnp.bfloat16)
-    d_up = (d_act * silu_gate).astype(jnp.bfloat16)
-    d_part = dot_back(d_gate, w1) + dot_back(d_up, w3)
     d_umlp = d_part[:tok] + swap_core(d_part[tok:])
     d_res_norm, d_gain2 = rms_norm_grad(d_umlp, normed2, inv_rms2, gain2)
     d_resid = d_layer.astype(jnp.float32) + d_res_norm
     d_resid_bf = d_resid.astype(jnp.bfloat16)
-    g1 = dot_tokens(u_pair, d_gate).reshape(2, 2, 2, dim // 8, ffn_half)
-    g3 = dot_tokens(u_pair, d_up).reshape(2, 2, 2, dim // 8, ffn_half)
-    g2 = dot_tokens(mlp_act, d_pair).reshape(2, 2, 2, ffn_half // 8, dim)
-
-    dh_all, wg = gather_dh(d_resid_bf, w_flat, 4)
-    dh_all = dh_all.reshape(seq, dim)
+    g1 = g1.reshape(2, 2, 2, dim // 8, ffn_half)
+    g3 = g3.reshape(2, 2, 2, dim // 8, ffn_half)
+    g2 = g2.reshape(2, 2, 2, ffn_half // 8, dim)
+
+    dh_all = gather_dh(d_resid_bf, 4).reshape(seq, dim)
     wg = wg.reshape(dim, 8 * grp)
     wo_own = lax.dynamic_slice_in_dim(wo, s * grp_q, grp_q, 0)
     d_own = dot_back(dh_all, wo_own).astype(jnp.bfloat16)
-    go = dot_tokens(o_own, dh_all).reshape(2, grp_q // 2, dim)
-    dqkv_pre, *got = flash_bwd(q_own, o_own, d_own, k_own, k_t, v_own, lse, cosw, sinw, (g1, g3, g2), 6)
-    g_mlp = halve_add((g1, g3, g2), got, 3)
-
-    go_mine = lax.dynamic_index_in_dim(go, z, 0, False) + swap_z(lax.dynamic_index_in_dim(go, 1 - z, 0, False))
-    grad_w_out = lax.ppermute(go_mine, ALL_AXES, [(zz * 8 + ss, 2 * ss + zz) for zz in range(2) for ss in range(8)])
-    dqkv_tok, got = regroup(dqkv_pre, g_mlp, 5, 'regroup_dqkv')
-    g_mlp = halve_add(g_mlp, got, 2)
+    go = dot_on(o_t, dh_all).reshape(2, grp_q // 2, dim)
+    dqkv_pre, *got = flash_bwd(q_own, o_own, d_own, k_own, k_t, v_own, lse, cos_t, sin_t, (g1, g3, g2), 6)
     gq = dot_tokens(u_all, dqkv_pre).reshape(2, dim // 2, grp)
-    gq_mine = lax.dynamic_index_in_dim(gq, z, 0, False) + swap_z(lax.dynamic_index_in_dim(gq, 1 - z, 0, False))
-    d_uattn = dot_back(dqkv_tok, wg)
-    _, normed1, inv_rms1 = rms_norm(tokens, gain1)
-    d_tok_norm, d_gain1 = rms_norm_grad(d_uattn, normed1, inv_rms1, gain1)
-    grad_hidden = (d_resid + d_tok_norm).astype(jnp.bfloat16)
+    terms = after(here, [[g1], [g3], [g2]], got, 3)
+    dqkv_tok, (*got, gq_got, go_got) = regroup(dqkv_pre, (*to_send(here, terms, 2), gq, go), 5, 'regroup_dqkv')
+    grad_w_out = lax.ppermute(pick(go, z) + go_got, ALL_AXES, [(zz * 8 + ss, 2 * ss + zz) for zz in range(2) for ss in range(8)])
+    terms = after(here, terms, got, 2)
+    gq_mine = pick(gq, z) + gq_got
+    grad_hidden, d_gain1, got_q, got = back_project(dqkv_tok, wg, tokens, gain1_rows, d_resid, gq_mine.reshape(8, rows, grp), to_send(here, terms, 1), 8)
+    m1, m3, grad_w_down = [total(ts) for ts in after(here, terms, got, 1)]
 
     gains = jnp.concatenate([d_gain1.reshape(2, 8, rows), d_gain2.reshape(2, 8, rows)], axis=2)
-    gains_mine = lax.dynamic_index_in_dim(gains, z, 0, False) + swap_z(lax.dynamic_index_in_dim(gains, 1 - z, 0, False))
+    gains_mine = pick(gains, z) + swap_z(pick(gains, 1 - z))
     gains_mine = jnp.broadcast_to(gains_mine[:, None, :], (8, 8, 2 * rows))
-    got_q, got_g, got = owner(gq_mine.reshape(8, rows, grp), gains_mine, g_mlp, 10)
+    pair1, pair3 = m1.reshape(2, rows, ffn_half), m3.reshape(2, rows, ffn_half)
+    got_g, other1, other3 = last_exchange(gains_mine, pair1, pair3, 10)
     got_q = got_q.transpose(1, 0, 2)
     grad_w_query = got_q[:, :, :grp_q].reshape(rows, 8 * grp_q)
     grad_w_key = got_q[:, :, grp_q:grp_q + grp_k].reshape(rows, 8 * grp_k)
@@ -756,12 +897,8 @@
     grad_gains = jnp.sum(got_g[:, 0, :], axis=0)
     grad_gain_attn, grad_gain_mlp = grad_gains[:rows], grad_gains[rows:]
 
-    m1, m3, grad_w_down = halve_add(g_mlp, got, 1)
-    pair = jnp.stack([m1.reshape(2, rows, ffn_half), m3.reshape(2, rows, ffn_half)], axis=1)
-    keep = lax.dynamic_index_in_dim(pair, c, 0, False)
-    other = swap_core(lax.dynamic_index_in_dim(pair, 1 - c, 0, False))
-    grad_w_gate = join_cols(keep[0], other[0], c)
-    grad_w_up = join_cols(keep[1], other[1], c)
+    grad_w_gate = join_cols(pick(pair1, c), other1, c)
+    grad_w_up = join_cols(pick(pair3, c), other3, c)
     return (layer_out[None], grad_hidden[None], grad_gain_attn, grad_gain_mlp, grad_w_query, grad_w_key, grad_w_value, grad_w_out, grad_w_gate, grad_w_up, grad_w_down)
 
 

time: 664 us -> 590 us (0.89)
  matrix products: 93.2 us -> 27.4 us
  other arithmetic: 54.2 us -> 43.4 us
    dot_general x5 -> x1, matrix products: 31.5 us -> 4.71 us  [dot_back(): lax.dot_general(left_op, weight, (((1,), (1,)), ((), ())), preferred_elem...]
    dot_general x5 -> x1, matrix products: 36.6 us -> 10.5 us  [dot_tokens(): lax.dot_general(left_op, right_op, (((0,), (0,)), ((), ())), preferred_el...]
    pallas_call x1, Pallas kernels: 95.7 us -> 82.5 us  [flash_fwd(): pl.pallas_call(functools.partial(fwd_kernel, bq, bk), grid=(seq // bq,),...]
    dot_general x4 -> x2, matrix products: 25.1 us -> 12.1 us  [dot_on(): return jnp.dot(left_op, weight, preferred_element_type=jnp.float32)]
    pallas_call x2 -> x4, Pallas kernels: 119 us -> 128 us  [the longest x1 46 us: mlp(): pl.pallas_call(mlp_kernel, grid=(half // bh,), in_specs=[vm, vm, pl.Block...]
    neg x1 -> x0, other arithmetic: 7.48 us -> none  [layer_step(): sinw = jnp.concatenate([-sin_tab, sin_tab], axis=1)]
  transfers between devices with their start and end apart: 9 -> 6, of which waited for: 0 -> 3; matrix products, arithmetic and copies ran while one was open for 15% -> 4% of each run, Pallas kernels for 24% -> 1%
where the time goes in v4:
time: 590 us; the launch traced here: 585 us
  Pallas kernels  459 us (78%)
  other arithmetic  43.4 us (7%)
  local copies, waits for them, and re-layouts  41.8 us (7%)
  matrix products  27.4 us (5%)
  starting transfers between devices  8.56 us (1%)
    pallas_call x2, Pallas kernels, regroup(): pl.pallas_call(functools.partial(regroup_kernel, n), in_specs=[an] * (1 +...  107 us
    pallas_call x1, Pallas kernels, flash_fwd(): pl.pallas_call(functools.partial(fwd_kernel, bq, bk), grid=(seq // bq,),...  82.5 us
    pallas_call x1, Pallas kernels, flash_bwd(): pl.pallas_call(functools.partial(bwd_kernel, bq, bk), grid=(seq // bk,),...  76.5 us
    pallas_call x1, Pallas kernels, entry(): pl.pallas_call(entry_kernel, in_specs=[vm] * 4, out_specs=[an] * 4, out_s...  49.8 us
    pallas_call x1, Pallas kernels, mlp(): pl.pallas_call(mlp_kernel, grid=(half // bh,), in_specs=[vm, vm, pl.Block...  46 us
    pallas_call x1, Pallas kernels, gather_dh(): pl.pallas_call(dh_kernel, in_specs=[pl.BlockSpec(memory_space=pltpu.VMEM)...  40.5 us
    pallas_call x1, Pallas kernels, back_project(): pl.pallas_call(back_kernel, grid=(dim // bn,), in_specs=[vm, pl.BlockSpec...  34.4 us
    add x9, other arithmetic, total(): out = out + t  19.6 us
  transfers between devices with their start and end apart: 6, of which 3 were waited for; matrix products, arithmetic and copies ran while one was open for 4% of the time, Pallas kernels for 1%

profile of v4, /device:TPU:0, one launch (start us, length us, event | category | flops | bytes accessed | tf_op | source)
XLA Modules:
  0.0 585.3 jit_solution(10151305478684290425)
XLA Ops:
  0.7 1.0 bitcast_dynamic-update-slice_fusion
  4.8 49.8 %entry.1 = (bf16[8,512,1024]{2,1,0:T(8,128)(2,1)}, bf16[2,8,64,512]{3,2,1,0:T(8,128)(2,1)}, bf16[2,8,16,128]{3,2,1,0:T(8,128)(2,1)}, s32[8,4,128]{2,1,0:T(4,128)}) custom-call(bf16[512,1024]{1,0:T(8,128)(2,1)} %bitcast.181, bf16[8,64,512]{2,1,0:T(8,128)(2,1)} %bitcast.179, bf16[16,128]{1,0:T(8,128)(2,1)} %fusion.20.meta_ref, s32[4,128]{1,0:T(4,128)} %bitcast.193), custom_call_target="tpu_custom_call" | custom-call | flops 4499999744 | bytes 1048576 | tf_op jit(solution)/shard_map/entry/pallas_call | solution.py:659
  57.8 1.2 reshape.284.w1
  59.7 1.2 reshape.286.w3
  60.9 4.9 multiply_sine_fusion
  65.8 15.2 %project.1 = (bf16[4096,1024]{1,0:T(8,128)(2,1)}, bf16[4096,256]{1,0:T(8,128)(2,1)}, bf16[4096,128]{1,0:T(8,128)(2,1)S(1)}, bf16[4096,128]{1,0:T(8,128)(2,1)S(1)...) custom-call(bf16[4096,1024]{1,0:T(8,128)(2,1)} %bitcast.194, ...), custom_call_target="tpu_custom_call" | custom-call | flops 4294967296 | bytes 33554432 | tf_op jit(solution)/shard_map/project/pallas_call | solution.py:261
  82.9 1.0 copy-done.5
  84.9 82.5 %flash_fwd.1 = (bf16[4096,256]{1,0:T(8,128)(2,1)}, bf16[256,4096]{1,0:T(8,128)(2,1)}, f32[2,4096]{1,0:T(2,128)}, bf16[2,2,2,2,64,1536]{5,4,3,2,1,0:T(8,128)(2,1)...) custom-call(bf16[4096,256]{1,0:T(8,128)(2,1)} %get-tuple-element.57., ...), custom_call_target="tpu_custom_call" | custom-call | flops 17179869184 | bytes 8388608 | tf_op jit(solution)/shard_map/flash_fwd/pallas_call | solution.py:342
  167.4 24.8 %regroup_o.1 = bf16[512,2048]{1,0:T(8,128)(2,1)} custom-call(bf16[4096,256]{1,0:T(8,128)(2,1)} %get-tuple-element.60.refs_0_.o_ref), custom_call_target="tpu_custom_call" | custom-call | flops 2500000000 | bytes 1048576 | tf_op jit(solution)/shard_map/regroup_o/pallas_call | solution.py:701
  192.2 5.3 fusion.10
  201.2 1.5 pad_maximum_fusion.u_ref
  202.7 1.6 pad_maximum_fusion.1.d_ref
  204.3 46.0 %mlp.1 = (f32[1024,1024]{1,0:T(8,128)}, f32[1024,1024]{1,0:T(8,128)}, f32[1024,1536]{1,0:T(8,128)}, f32[1024,1536]{1,0:T(8,128)}, f32[1536,1024]{1,0:T(8,128)}, /*index=5*/bf16[2,2,2,2,64,4096]{5,4,3,2,1,0:T(8,128)(2,1)}) custom-call(bf16[1024,1024]{1,0:T(8,128)(2,1)} %pad_maximum_fusion.u_ref, bf16[1024,1024]{1,0:T(8,128)(2,1)} %pad_maximum_fusion.1.d_ref, ...), custom_call_target="tpu_custom_call" | custom-call | flops 28991029248 | bytes 50331648 | tf_op jit(solution)/shard_map/mlp/pallas_call | solution.py:605
  250.3 3.3 slice.41
  254.0 1.4 slice.39
  255.6 2.2 collective-permute-done.3
  257.8 2.3 fusion.9
  260.8 5.1 fusion.26
  265.9 40.5 %gather_dh.1 = bf16[8,512,1024]{2,1,0:T(8,128)(2,1)} custom-call(bf16[512,1024]{1,0:T(8,128)(2,1)} %get-tuple-element.97.src), custom_call_target="tpu_custom_call" | custom-call | flops 4000000000 | bytes 1048576 | tf_op jit(solution)/shard_map/gather_dh/pallas_call | solution.py:528
  306.4 6.8 %fusion.30.refs_5_ = f32[2,128,1024]{2,1,0:T(8,128)} fusion(bf16[2,128,4096]{2,1,0:T(8,128)(2,1)S(1)} %bitcast.202, bf16[4096,1024,1]{1,0,2:T(8,128)(2,1)} %bitcast.195), kind=kOutput, calls=%fused_computation.87 | convolution fusion | flops 2147483648 | bytes 11534336 | tf_op jit(solution)/shard_map/dot_general | solution.py:803
  313.3 4.7 convolution_convert_fusion.d_ref
  318.0 76.5 %flash_bwd.1 = (bf16[4096,512]{1,0:T(8,128)(2,1)}, f32[2,2,128,1536]{3,2,1,0:T(8,128)}, f32[2,2,128,1536]{3,2,1,0:T(8,128)}, f32[2,2,192,1024]{3,2,1,0:T(8,128)}) custom-call(bf16[4096,256]{1,0:T(8,128)(2,1)} %get-tuple-element.57.q_ref, bf16[4096,256]{1,0:T(8,128)(2,1)} %get-tuple-element.60.refs_0_.o_ref, bf16[4096,256]{1,0:T(8,128)(2,1)} %convolution_convert_fusion.d_ref, ...), custom_call_target="tpu_custom_call" | custom-call | flops 21474836480 | bytes 16777216 | tf_op jit(solution)/shard_map/flash_bwd/pallas_call | solution.py:441
  394.5 10.5 %fusion.29 = f32[1024,512]{1,0:T(8,128)} fusion(bf16[4096,1024]{1,0:T(8,128)(2,1)} %get-tuple-element.77, bf16[4096,512]{1,0:T(8,128)(2,1)} %get-tuple-element.73.refs_0_), kind=kOutput, calls=%fused_computation.86 | convolution fusion | flops 4294967296 | bytes 14680064 | tf_op jit(solution)/shard_map/dot_general | solution.py:795
  405.0 3.1 bitcast_add_fusion.refs_3_
  408.1 3.0 bitcast_add_fusion.1.refs_2_
  411.1 2.7 bitcast_add_fusion.2.refs_1_
  413.8 82.6 %regroup_dqkv.1 = (bf16[512,4096]{1,0:T(8,128)(2,1)}, f32[2,128,1536]{2,1,0:T(8,128)}, f32[2,128,1536]{2,1,0:T(8,128)}, f32[2,192,1024]{2,1,0:T(8,128)}, f32[512,512]{1,0:T(8,128)}, /*index=5*/f32[128,1024]{1,0:T(8,128)}) custom-call(bf16[4096,512]{1,0:T(8,128)(2,1)} %get-tuple-element.73.refs_0_, f32[2,128,1536]{2,1,0:T(8,128)} %bitcast_add_fusion.2.refs_1_, ...), custom_call_target="tpu_custom_call" | custom-call | flops 7000000000 | bytes 1048576 | tf_op jit(solution)/shard_map/regroup_dqkv/pallas_call | solution.py:701
  496.5 2.0 bitcast_add_fusion.10.g2
  499.1 1.5 bitcast_add_fusion.12.g3
  500.6 1.4 bitcast_add_fusion.14.g1
  502.8 1.2 bitcast_add_fusion.3
  503.9 34.4 %back_project.1 = (bf16[512,1024]{1,0:T(8,128)(2,1)S(1)}, f32[1,1024]{1,0:T(1,128)S(1)}, f32[8,64,512]{2,1,0:T(8,128)}, f32[128,1536]{1,0:T(8,128)S(1)}, f32[128...) custom-call(bf16[512,4096]{1,0:T(8,128)(2,1)} %get-tuple-element.79.t_ref, bf16[1024,4096]{1,0:T(8,128)(2,1)} %bitcast.157, ...), custom_call_target="tpu_custom_call" | custom-call | flops 3500000000 | bytes 1048576 | tf_op jit(solution)/shard_map/back_project/pallas_call | solution.py:757
  538.4 1.2 slice_bitcast_fusion
  539.6 1.8 slice_bitcast_fusion.1
  541.4 2.7 fusion.13
  544.0 1.3 fusion.14
  545.4 1.9 fusion.15
  549.5 2.1 bitcast_add_fusion.16
  553.1 1.1 reshape.309
  554.3 1.2 reshape.306
  555.4 5.5 collective-permute-start.5
  561.8 1.7 copy.55
  564.9 7.0 %last_exchange.1 = (f32[8,8,128]{2,1,0:T(8,128)}, f32[64,1536]{1,0:T(8,128)}, f32[64,1536]{1,0:T(8,128)}) custom-call(f32[8,8,128]{2,1,0:T(8,128)} %broadcast_in_dim.14.b, f32[2,64,1536]{2,1,0:T(8,128)} %bitcast.166, f32[2,64,1536]{2,1,0:T(8,128)} %bitcast.164), custom_call_target="tpu_custom_call" | custom-call | flops 500000000 | bytes 1048576 | tf_op jit(solution)/shard_map/last_exchange/pallas_call | solution.py:786
  571.9 1.1 reshape.310
  573.1 1.2 reshape.307
  576.1 1.9 reshape.311
  578.9 1.9 reshape.308
  583.2 1.9 copy.62
  (108 shorter events, 27.1 us)
Async XLA Ops:
  0.6 2.3 copy-start
  4.0 0.8 copy-start.21
  4.8 52.2 %copy-start.26 = (bf16[64,3072]{1,0:T(8,128)(2,1)S(1)}, bf16[64,3072]{1,0:T(8,128)(2,1)}, u32[]{:S(2)}) copy-start(bf16[64,3072]{1,0:T(8,128)(2,1)} %param.21) | copy-start | bytes 1179652
  54.6 4.4 copy-start.27
  59.6 6.2 %copy-start.2 = (bf16[2,8,64,512]{3,2,1,0:T(8,128)(2,1)S(1)}, bf16[2,8,64,512]{3,2,1,0:T(8,128)(2,1)}, u32[]{:S(2)}) copy-start(bf16[2,8,64,512]{3,2,1,0:T(8,128)(2,1)} %get-tuple-element.55) | copy-start | bytes 3145732
  81.0 1.0 copy-start.3
  81.9 1.0 copy-start.4
  82.9 1.0 copy-start.5
  83.9 1.0 copy-start.6
  167.4 24.8 %copy-start.23 = (bf16[1,512,1024]{2,1,0:T(8,128)(2,1)S(1)}, bf16[1,512,1024]{2,1,0:T(8,128)(2,1)}, u32[]{:S(2)}) copy-start(bf16[1,512,1024]{2,1,0:T(8,128)(2,1)} %param.12) | copy-start | bytes 3145732
  197.5 1.4 copy-start.9
  197.5 2.1 copy-start.22
  197.9 3.2 collective-permute-start
  198.9 3.8 collective-permute-start.1
  250.3 3.7 copy-start.8
  253.6 4.2 collective-permute-start.3
  255.4 5.3 collective-permute-start.2
  255.6 5.2 copy-start.7
  255.6 5.2 copy-start.10
  265.9 40.5 %copy-start.29 = (bf16[256,4096]{1,0:T(8,128)(2,1)S(1)}, bf16[256,4096]{1,0:T(8,128)(2,1)}, u32[]{:S(2)}) copy-start(bf16[256,4096]{1,0:T(8,128)(2,1)} %get-tuple-element.78) | copy-start | bytes 6291460
  306.4 6.9 %copy-start.28 = (bf16[8,512,1024]{2,1,0:T(8,128)(2,1)S(1)}, bf16[8,512,1024]{2,1,0:T(8,128)(2,1)}, u32[]{:S(2)}) copy-start(bf16[8,512,1024]{2,1,0:T(8,128)(2,1)} %gather_dh.1) | copy-start | bytes 25165828
  394.5 10.5 %copy-start.14 = (f32[2,2,192,1024]{3,2,1,0:T(8,128)S(1)}, f32[2,2,192,1024]{3,2,1,0:T(8,128)}, u32[]{:S(2)}) copy-start(f32[2,2,192,1024]{3,2,1,0:T(8,128)} %get-tuple-element.76) | copy-start | bytes 9437188
  405.0 3.1 copy-start.12
  408.1 3.0 copy-start.11
  496.5 2.6 copy-start.13
  498.5 2.1 copy-start.18
  500.6 1.5 copy-start.24
  500.6 2.1 copy-start.25
  538.3 3.0 copy-start.20
  541.3 2.7 copy-start.19
  545.4 6.2 %copy-start.16 = (f32[128,1536]{1,0:T(8,128)}, f32[128,1536]{1,0:T(8,128)S(1)}, u32[]{:S(2)}) copy-start(f32[128,1536]{1,0:T(8,128)S(1)} %fusion.14) | copy-start | bytes 2359300
  547.3 5.1 copy-start.17
  548.7 15.5 %collective-permute-start.4 = (f32[8,128]{1,0:T(8,128)S(1)}, f32[8,128]{1,0:T(8,128)S(1)}, u32[]{:S(2)}, u32[]{:S(2)}) collective-permute-start(f32[8,128]{1,0:T(8,128)S(1)} %fusion.25), channel_id=1, source_target_pairs={{0,8},{8,0},{1,9},{9,1},{2,10},{10,2},{3,11},{11,3},{4,12},{12,4},... | collective-permute-start | bytes 12296 | tf_op jit(solution)/shard_map/ppermute | solution.py:811
  555.4 26.8 %collective-permute-start.5 = (f32[128,1024]{1,0:T(8,128)}, f32[128,1024]{1,0:T(8,128)}, u32[]{:S(2)}, u32[]{:S(2)}) collective-permute-start(f32[128,1024]{1,0:T(8,128)} %bitcast_add_fusion.16), channel_id=1, source_target_pairs={{0,0},{1,2},{2,4},{3,6},{4,8},{5,10},{6,12},{7,14},{8,1},{9,3},{10... | collective-permute-start | bytes 1572872 | tf_op jit(solution)/shard_map/ppermute | solution.py:882
  575.3 2.8 copy-start.15
  578.1 7.0 %copy-start.1 = (bf16[64,1024]{1,0:T(8,128)(2,1)S(1)}, bf16[64,1024]{1,0:T(8,128)(2,1)}, u32[]{:S(2)}) copy-start(bf16[64,1024]{1,0:T(8,128)(2,1)} %param.18) | copy-start | bytes 393220

commit v5 on v4

--- a/solution.py
+++ b/solution.py
@@ -241,8 +241,9 @@
     u = (x * inv * g_ref[0:1, :].astype(jnp.float32)).astype(jnp.bfloat16)
     u_ref[...] = u
     cos, sin = wide_tables(cos_ref[...], sin_ref[...])
+    full = jnp.dot(u, w_ref[...], preferred_element_type=jnp.float32)
     for h in range(nrot + 2):
-        t = jnp.dot(u, w_ref[:, head(h)], preferred_element_type=jnp.float32)
+        t = full[:, head(h)]
         if h <= nrot:
             t = t * cos + pltpu.roll(t, HEAD_DIM // 2, 1) * sin
         if h < nrot:
@@ -267,7 +268,7 @@
         out_shape=[jax.ShapeDtypeStruct((seq, dim), bf), jax.ShapeDtypeStruct((seq, nq * HEAD_DIM), bf), jax.ShapeDtypeStruct((seq, HEAD_DIM), bf),
                    jax.ShapeDtypeStruct((seq, HEAD_DIM), bf), jax.ShapeDtypeStruct((HEAD_DIM, seq), bf), jax.ShapeDtypeStruct((HEAD_DIM, seq), bf)],
         cost_estimate=pl.CostEstimate(flops=2 * seq * dim * grp, bytes_accessed=32 << 20, transcendentals=0),
-        compiler_params=pltpu.CompilerParams(vmem_limit_bytes=48 << 20), name="project",
+        compiler_params=pltpu.CompilerParams(vmem_limit_bytes=62 << 20), name="project",
     )(x, gain, w, cos_t, sin_t)
 
 
@@ -533,7 +534,7 @@
     )(src)
 
 
-def mlp_kernel(u_ref, d_ref, w1_ref, w3_ref, w2_ref, wg, y_ref, dx_ref, g1_ref, g3_ref, g2_ref, og, ut, send_sem, recv_sem, local_sem):
+def mlp_kernel(u_ref, d_ref, w1_ref, w3_ref, w2_ref, wg, y_ref, yp_ref, dx_ref, dxp_ref, g1_ref, g3_ref, g2_ref, og, ut, send_sem, recv_sem, local_sem):
     j = pl.program_id(0)
     last = pl.num_programs(0) - 1
     here = Spot()
@@ -551,8 +552,8 @@
         loc.start()
         loc.wait()
         cube.start(0)
-        y_ref[...] = jnp.zeros_like(y_ref)
-        dx_ref[...] = jnp.zeros_like(dx_ref)
+        for r in (y_ref, yp_ref, dx_ref, dxp_ref):
+            r[...] = jnp.zeros_like(r)
 
         def flip(i, carry):
             part = pl.ds(pl.multiple_of(i * 128, 128), 128)
@@ -584,8 +585,13 @@
     z = (silu * up).astype(jnp.bfloat16)
     da = (act * up * sig * (1.0 + gate * (1.0 - sig))).astype(jnp.bfloat16)
     dc = (act * silu).astype(jnp.bfloat16)
-    y_ref[...] += jnp.dot(z, w2, preferred_element_type=f32)
-    dx_ref[...] += lax.dot_general(da, w1, NT, preferred_element_type=f32) + lax.dot_general(dc, w3, NT, preferred_element_type=f32)
+    y = jnp.dot(z, w2, preferred_element_type=f32)
+    dx = lax.dot_general(da, w1, NT, preferred_element_type=f32) + lax.dot_general(dc, w3, NT, preferred_element_type=f32)
+    mine = y_ref.shape[0]
+    y_ref[...] += y[:mine]
+    yp_ref[...] += y[mine:]
+    dx_ref[...] += dx[:mine]
+    dxp_ref[...] += dx[mine:]
     g1_ref[...] = jnp.dot(ut[...], da, preferred_element_type=f32)
     g3_ref[...] = jnp.dot(ut[...], dc, preferred_element_type=f32)
     g2_ref[...] = lax.dot_general(z, d, (((0,), (0,)), ((), ())), preferred_element_type=f32)
@@ -605,9 +611,9 @@
     return pl.pallas_call(
         mlp_kernel, grid=(half // bh,),
         in_specs=[vm, vm, pl.BlockSpec((dim, bh), by_cols), pl.BlockSpec((dim, bh), by_cols), pl.BlockSpec((bh, dim), by_rows), vm],
-        out_specs=[pl.BlockSpec((toks, dim), whole), pl.BlockSpec((toks, dim), whole), pl.BlockSpec((dim, bh), by_cols), pl.BlockSpec((dim, bh), by_cols),
+        out_specs=[pl.BlockSpec((toks // 2, dim), whole)] * 4 + [pl.BlockSpec((dim, bh), by_cols), pl.BlockSpec((dim, bh), by_cols),
                    pl.BlockSpec((bh, dim), by_rows), an],
-        out_shape=[jax.ShapeDtypeStruct((toks, dim), f32), jax.ShapeDtypeStruct((toks, dim), f32), jax.ShapeDtypeStruct((dim, half), f32),
+        out_shape=[jax.ShapeDtypeStruct((toks // 2, dim), f32)] * 4 + [jax.ShapeDtypeStruct((dim, half), f32),
                    jax.ShapeDtypeStruct((dim, half), f32), jax.ShapeDtypeStruct((half, dim), f32),
                    jax.ShapeDtypeStruct((2, 2, 2, 2, *wg.shape), wg.dtype)],
         scratch_shapes=[pltpu.VMEM((dim, toks), jnp.bfloat16), pltpu.SemaphoreType.DMA((19,)), pltpu.SemaphoreType.DMA((19,)), pltpu.SemaphoreType.DMA],
@@ -761,7 +767,7 @@
         out_shape=[jax.ShapeDtypeStruct((toks, dim), jnp.bfloat16), jax.ShapeDtypeStruct((1, dim), jnp.float32), jax.ShapeDtypeStruct(a.shape, a.dtype)]
         + [jax.ShapeDtypeStruct(g.shape, g.dtype) for g in gs],
         scratch_shapes=[pltpu.VMEM((toks, dim), jnp.float32), pltpu.SemaphoreType.DMA((10,)), pltpu.SemaphoreType.DMA((10,)), pltpu.SemaphoreType.DMA],
-        cost_estimate=busy(35), compiler_params=comm_params(cid, vmem_limit_bytes=48 << 20), name="back_project",
+        cost_estimate=busy(35), compiler_params=comm_params(cid, vmem_limit_bytes=62 << 20), name="back_project",
     )(t, w, x, gain, res, a, *gs)
     return out[0], out[1], out[2], out[3:]
 
@@ -839,7 +845,7 @@
     w_grp = jnp.concatenate([w_query.reshape(rows, 8, grp_q), w_key.reshape(rows, 8, grp_k), w_value.reshape(rows, 8, grp_k)], axis=2)
     w_flat = w_grp.reshape(rows, 8 * grp)
     pad = HEAD_DIM - gain_attn.shape[0]
-    meta = jnp.pad(jnp.stack([jnp.pad(gain_attn, (0, pad)), jnp.pad(gain_mlp, (0, pad))]), ((0, 14), (0, 0)))
+    meta = jnp.pad(jnp.stack([gain_attn, gain_mlp]), ((0, 14), (0, pad)))
     x_all, w_own, meta_all, pos_all = entry(tokens, w_grp.transpose(1, 0, 2), meta, positions[0].reshape(-1, 128), 1)
     x_all = x_all.reshape(seq, dim)
     w_own = w_own.reshape(dim, grp)
@@ -859,10 +865,10 @@
     u_mlp, normed2, inv_rms2 = rms_norm(residual, gain2)
     u_pair = jnp.concatenate([u_mlp, swap_core(u_mlp)], axis=0)
     d_pair = jnp.concatenate([d_layer, swap_core(d_layer)], axis=0)
-    y_part, d_part, g1, g3, g2, wg = mlp(u_pair, d_pair, w1, w3, w2, w_flat, 7)
-    layer_out = (residual.astype(jnp.float32) + (y_part[:tok] + swap_core(y_part[tok:]))).astype(jnp.bfloat16)
-
-    d_umlp = d_part[:tok] + swap_core(d_part[tok:])
+    y_part, y_peer, d_part, d_peer, g1, g3, g2, wg = mlp(u_pair, d_pair, w1, w3, w2, w_flat, 7)
+    layer_out = (residual.astype(jnp.float32) + (y_part + swap_core(y_peer))).astype(jnp.bfloat16)
+
+    d_umlp = d_part + swap_core(d_peer)
     d_res_norm, d_gain2 = rms_norm_grad(d_umlp, normed2, inv_rms2, gain2)
     d_resid = d_layer.astype(jnp.float32) + d_res_norm
     d_resid_bf = d_resid.astype(jnp.bfloat16)
@@ -879,7 +885,10 @@
     gq = dot_tokens(u_all, dqkv_pre).reshape(2, dim // 2, grp)
     terms = after(here, [[g1], [g3], [g2]], got, 3)
     dqkv_tok, (*got, gq_got, go_got) = regroup(dqkv_pre, (*to_send(here, terms, 2), gq, go), 5, 'regroup_dqkv')
-    grad_w_out = lax.ppermute(pick(go, z) + go_got, ALL_AXES, [(zz * 8 + ss, 2 * ss + zz) for zz in range(2) for ss in range(8)])
+    go_mine = pick(go, z) + go_got
+    stay = dim // HEAD_DIM - 1
+    moved = lax.ppermute(go_mine, ALL_AXES, [(zz * 8 + ss, 2 * ss + zz) for zz in range(2) for ss in range(8) if ss != zz * stay])
+    grad_w_out = jnp.where(s == z * stay, go_mine, moved)
     terms = after(here, terms, got, 2)
     gq_mine = pick(gq, z) + gq_got
     grad_hidden, d_gain1, got_q, got = back_project(dqkv_tok, wg, tokens, gain1_rows, d_resid, gq_mine.reshape(8, rows, grp), to_send(here, terms, 1), 8)

time: 590 us -> 575 us (0.975)
  local copies, waits for them, and re-layouts: 41.8 us -> 26.2 us
    unnamed x66 -> x67, local copies, waits for them, and re-layouts: 13 us -> 5.7 us
    add x9 -> x8, other arithmetic: 19.6 us -> 21.2 us  [total(): out = out + t]
  transfers between devices with their start and end apart: 6 -> 6, of which waited for: 3 -> 3; matrix products, arithmetic and copies ran while one was open for 4% -> 3% of each run, Pallas kernels for 1% -> 2%
where the time goes in v5:
time: 575 us; the launch traced here: 570 us
  Pallas kernels  462 us (80%)
  other arithmetic  44.4 us (8%)
  matrix products  27.5 us (5%)
  local copies, waits for them, and re-layouts  26.2 us (5%)
    pallas_call x2, Pallas kernels, regroup(): pl.pallas_call(functools.partial(regroup_kernel, n), in_specs=[an] * (1 +...  107 us
    pallas_call x1, Pallas kernels, flash_fwd(): pl.pallas_call(functools.partial(fwd_kernel, bq, bk), grid=(seq // bq,),...  82.5 us
    pallas_call x1, Pallas kernels, flash_bwd(): pl.pallas_call(functools.partial(bwd_kernel, bq, bk), grid=(seq // bk,),...  76.5 us
    pallas_call x1, Pallas kernels, entry(): pl.pallas_call(entry_kernel, in_specs=[vm] * 4, out_specs=[an] * 4, out_s...  49.8 us
    pallas_call x1, Pallas kernels, mlp(): pl.pallas_call(mlp_kernel, grid=(half // bh,), in_specs=[vm, vm, pl.Block...  46.1 us
    pallas_call x1, Pallas kernels, gather_dh(): pl.pallas_call(dh_kernel, in_specs=[pl.BlockSpec(memory_space=pltpu.VMEM)...  40.5 us
    pallas_call x1, Pallas kernels, back_project(): pl.pallas_call(back_kernel, grid=(dim // bn,), in_specs=[vm, pl.BlockSpec...  35.6 us
    add x8, other arithmetic, total(): out = out + t  21.2 us
  transfers between devices with their start and end apart: 6, of which 3 were waited for; matrix products, arithmetic and copies ran while one was open for 3% of the time, Pallas kernels for 2%

profile of v5, /device:TPU:0, one launch (start us, length us, event | category | flops | bytes accessed | tf_op | source)
XLA Modules:
  0.0 570.4 jit_solution(16582500243787795258)
XLA Ops:
  0.7 1.0 bitcast_dynamic-update-slice_fusion
  1.8 1.0 bitcast_dynamic-update-slice_fusion.1
  2.7 1.3 fusion.23.meta_ref
  4.1 49.8 %entry.1 = (bf16[8,512,1024]{2,1,0:T(8,128)(2,1)}, bf16[2,8,64,512]{3,2,1,0:T(8,128)(2,1)}, bf16[2,8,16,128]{3,2,1,0:T(8,128)(2,1)}, s32[8,4,128]{2,1,0:T(4,128)}) custom-call(bf16[512,1024]{1,0:T(8,128)(2,1)} %bitcast.177, bf16[8,64,512]{2,1,0:T(8,128)(2,1)} %bitcast.175, bf16[16,128]{1,0:T(8,128)(2,1)} %fusion.23.meta_ref, s32[4,128]{1,0:T(4,128)} %bitcast.192), custom_call_target="tpu_custom_call" | custom-call | flops 4499999744 | bytes 1048576 | tf_op jit(solution)/shard_map/entry/pallas_call | solution.py:665
  57.1 1.2 reshape.284.w1
  59.0 1.2 reshape.286.w3
  60.1 4.9 multiply_sine_fusion
  65.7 14.4 %project.1 = (bf16[4096,1024]{1,0:T(8,128)(2,1)}, bf16[4096,256]{1,0:T(8,128)(2,1)}, bf16[4096,128]{1,0:T(8,128)(2,1)}, bf16[4096,128]{1,0:T(8,128)(2,1)}, bf16[...) custom-call(bf16[4096,1024]{1,0:T(8,128)(2,1)} %bitcast.193, bf16[16,1024]{1,0:T(8,128)(2,1)} %broadcast_in_dim.11.g_ref.gain_ref, ...), custom_call_target="tpu_custom_call" | custom-call | flops 4294967296 | bytes 33554432 | tf_op jit(solution)/shard_map/project/pallas_call | solution.py:262
  80.1 82.5 %flash_fwd.1 = (bf16[4096,256]{1,0:T(8,128)(2,1)}, bf16[256,4096]{1,0:T(8,128)(2,1)}, f32[2,4096]{1,0:T(2,128)}, bf16[2,2,2,2,64,1536]{5,4,3,2,1,0:T(8,128)(2,1)...) custom-call(bf16[4096,256]{1,0:T(8,128)(2,1)} %get-tuple-element.59., ...), custom_call_target="tpu_custom_call" | custom-call | flops 17179869184 | bytes 8388608 | tf_op jit(solution)/shard_map/flash_fwd/pallas_call | solution.py:343
  162.6 24.8 %regroup_o.1 = bf16[512,2048]{1,0:T(8,128)(2,1)} custom-call(bf16[4096,256]{1,0:T(8,128)(2,1)} %get-tuple-element.62.refs_0_.o_ref), custom_call_target="tpu_custom_call" | custom-call | flops 2500000000 | bytes 1048576 | tf_op jit(solution)/shard_map/regroup_o/pallas_call | solution.py:707
  187.5 5.3 fusion.10
  193.2 0.9 collective-permute-start
  194.9 0.8 copy.42
  196.4 1.5 pad_maximum_fusion.u_ref
  197.9 1.6 pad_maximum_fusion.1.d_ref
  199.5 46.1 %mlp.1 = (f32[512,1024]{1,0:T(8,128)}, f32[512,1024]{1,0:T(8,128)}, f32[512,1024]{1,0:T(8,128)}, f32[512,1024]{1,0:T(8,128)}, f32[1024,1536]{1,0:T(8,128)}, /*in...) custom-call(bf16[1024,1024]{1,0:T(8,128)(2,1)} %pad_maximum_fusion.u_ref, ...), custom_call_target="tpu_custom_call" | custom-call | flops 28991029248 | bytes 50331648 | tf_op jit(solution)/shard_map/mlp/pallas_call | solution.py:611
  246.2 3.6 collective-permute-done.3
  249.9 2.5 fusion.9
  253.0 4.5 fusion.29
  257.5 40.5 %gather_dh.1 = bf16[8,512,1024]{2,1,0:T(8,128)(2,1)} custom-call(bf16[512,1024]{1,0:T(8,128)(2,1)} %get-tuple-element.101.src), custom_call_target="tpu_custom_call" | custom-call | flops 4000000000 | bytes 1048576 | tf_op jit(solution)/shard_map/gather_dh/pallas_call | solution.py:529
  298.1 6.8 %fusion.33.refs_5_ = f32[2,128,1024]{2,1,0:T(8,128)} fusion(bf16[2,128,4096]{2,1,0:T(8,128)(2,1)S(1)} %bitcast.201, bf16[4096,1024,1]{1,0,2:T(8,128)(2,1)} %bitcast.194), kind=kOutput, calls=%fused_computation.89 | convolution fusion | flops 2147483648 | bytes 11534336 | tf_op jit(solution)/shard_map/dot_general | solution.py:809
  304.9 4.8 convolution_convert_fusion.d_ref
  309.8 76.5 %flash_bwd.1 = (bf16[4096,512]{1,0:T(8,128)(2,1)}, f32[2,2,128,1536]{3,2,1,0:T(8,128)}, f32[2,2,128,1536]{3,2,1,0:T(8,128)}, f32[2,2,192,1024]{3,2,1,0:T(8,128)}) custom-call(bf16[4096,256]{1,0:T(8,128)(2,1)} %get-tuple-element.59.q_ref, bf16[4096,256]{1,0:T(8,128)(2,1)} %get-tuple-element.62.refs_0_.o_ref, bf16[4096,256]{1,0:T(8,128)(2,1)} %convolution_convert_fusion.d_ref, ...), custom_call_target="tpu_custom_call" | custom-call | flops 21474836480 | bytes 16777216 | tf_op jit(solution)/shard_map/flash_bwd/pallas_call | solution.py:442
  386.3 10.6 %fusion.32 = f32[1024,512]{1,0:T(8,128)} fusion(bf16[4096,1024]{1,0:T(8,128)(2,1)} %get-tuple-element.81, bf16[4096,512]{1,0:T(8,128)(2,1)} %get-tuple-element.77.refs_0_), kind=kOutput, calls=%fused_computation.88 | convolution fusion | flops 4294967296 | bytes 14680064 | tf_op jit(solution)/shard_map/dot_general | solution.py:801
  396.8 3.0 bitcast_add_fusion.refs_3_
  399.8 4.1 bitcast_add_fusion.1
  403.9 82.6 %regroup_dqkv.1 = (bf16[512,4096]{1,0:T(8,128)(2,1)}, f32[2,128,1536]{2,1,0:T(8,128)}, f32[2,128,1536]{2,1,0:T(8,128)}, f32[2,192,1024]{2,1,0:T(8,128)}, f32[512,512]{1,0:T(8,128)}, /*index=5*/f32[128,1024]{1,0:T(8,128)}) custom-call(bf16[4096,512]{1,0:T(8,128)(2,1)} %get-tuple-element.77.refs_0_, f32[2,128,1536]{2,1,0:T(8,128)} %get-tuple-element.117.refs_1_, ...), custom_call_target="tpu_custom_call" | custom-call | flops 7000000000 | bytes 1048576 | tf_op jit(solution)/shard_map/regroup_dqkv/pallas_call | solution.py:707
  486.6 2.5 bitcast_add_fusion.10.g2
  489.1 2.5 bitcast_add_fusion.12.g3
  491.6 2.5 bitcast_add_fusion.14.g1
  494.2 1.2 bitcast_add_fusion.3
  495.3 35.6 %back_project.1 = (bf16[512,1024]{1,0:T(8,128)(2,1)}, f32[1,1024]{1,0:T(1,128)}, f32[8,64,512]{2,1,0:T(8,128)}, f32[128,1536]{1,0:T(8,128)}, f32[128,1536]{1,0:T(8,128)}, /*index=5*/f32[192,1024]{1,0:T(8,128)}) custom-call(bf16[512,4096]{1,0:T(8,128)(2,1)} %get-tuple-element.83.t_ref, bf16[1024,4096]{1,0:T(8,128)(2,1)} %bitcast.153, ...), custom_call_target="tpu_custom_call" | custom-call | flops 3500000000 | bytes 1048576 | tf_op jit(solution)/shard_map/back_project/pallas_call | solution.py:763
  530.9 1.2 slice_bitcast_fusion
  532.2 1.9 slice_bitcast_fusion.1
  534.0 2.9 fusion.13
  537.0 1.8 fusion.14
  539.1 1.8 fusion.15
  543.1 1.1 bitcast_add_fusion.16
  544.7 1.5 collective-permute-start.5
  546.1 0.8 copy.43
  547.0 1.7 copy.55
  550.1 8.8 %last_exchange.1 = (f32[8,8,128]{2,1,0:T(8,128)}, f32[64,1536]{1,0:T(8,128)}, f32[64,1536]{1,0:T(8,128)}) custom-call(f32[8,8,128]{2,1,0:T(8,128)} %broadcast_in_dim.14.b, f32[2,64,1536]{2,1,0:T(8,128)} %bitcast.162, f32[2,64,1536]{2,1,0:T(8,128)} %bitcast.160), custom_call_target="tpu_custom_call" | custom-call | flops 500000000 | bytes 1048576 | tf_op jit(solution)/shard_map/last_exchange/pallas_call | solution.py:792
  558.9 1.1 reshape.310
  560.0 1.2 reshape.307
  562.2 1.9 reshape.311
  565.1 1.9 reshape.308
  568.4 0.9 broadcast_select_fusion.4
  569.2 1.0 copy.60
  (106 shorter events, 15.3 us)
Async XLA Ops:
  0.6 1.0 copy-start
  2.7 1.4 copy-start.16
  4.1 52.2 %copy-start.26 = (bf16[64,3072]{1,0:T(8,128)(2,1)S(1)}, bf16[64,3072]{1,0:T(8,128)(2,1)}, u32[]{:S(2)}) copy-start(bf16[64,3072]{1,0:T(8,128)(2,1)} %param.21) | copy-start | bytes 1179652
  53.9 4.4 copy-start.27
  162.6 24.8 %copy-start.18 = (bf16[1,512,1024]{2,1,0:T(8,128)(2,1)S(1)}, bf16[1,512,1024]{2,1,0:T(8,128)(2,1)}, u32[]{:S(2)}) copy-start(bf16[1,512,1024]{2,1,0:T(8,128)(2,1)} %param.12) | copy-start | bytes 3145732
  192.8 1.4 copy-start.3
  192.8 2.1 copy-start.17
  193.2 3.2 collective-permute-start
  194.1 3.8 collective-permute-start.1
  245.7 4.2 collective-permute-start.3
  246.0 6.8 %collective-permute-start.2 = (f32[512,1024]{1,0:T(8,128)}, f32[512,1024]{1,0:T(8,128)}, u32[]{:S(2)}, u32[]{:S(2)}) collective-permute-start(f32[512,1024]{1,0:T(8,128)} %get-tuple-element.68), channel_id=1, source_target_pairs={{0,1},{1,0},{2,3},{3,2},{4,5},{5,4},{6,7},{7,6},{8,9},{9,8},{10,11... | collective-permute-start | bytes 6291464 | tf_op jit(solution)/shard_map/ppermute | solution.py:813
  249.9 2.9 copy-start.2
  249.9 2.9 copy-start.4
  249.9 3.2 copy-start.8
  257.5 40.5 %copy-start.30 = (bf16[256,4096]{1,0:T(8,128)(2,1)S(1)}, bf16[256,4096]{1,0:T(8,128)(2,1)}, u32[]{:S(2)}) copy-start(bf16[256,4096]{1,0:T(8,128)(2,1)} %get-tuple-element.82) | copy-start | bytes 6291460
  298.1 6.9 %copy-start.29 = (bf16[8,512,1024]{2,1,0:T(8,128)(2,1)S(1)}, bf16[8,512,1024]{2,1,0:T(8,128)(2,1)}, u32[]{:S(2)}) copy-start(bf16[8,512,1024]{2,1,0:T(8,128)(2,1)} %gather_dh.1) | copy-start | bytes 25165828
  386.2 10.6 %copy-start.5 = (f32[2,2,192,1024]{3,2,1,0:T(8,128)S(1)}, f32[2,2,192,1024]{3,2,1,0:T(8,128)}, u32[]{:S(2)}) copy-start(f32[2,2,192,1024]{3,2,1,0:T(8,128)} %get-tuple-element.80) | copy-start | bytes 9437188
  386.2 13.6 %copy-start.7 = (f32[2,2,128,1536]{3,2,1,0:T(8,128)S(1)}, f32[2,2,128,1536]{3,2,1,0:T(8,128)}, u32[]{:S(2)}) copy-start(f32[2,2,128,1536]{3,2,1,0:T(8,128)} %get-tuple-element.79) | copy-start | bytes 9437188
  396.8 3.0 copy-start.6
  486.6 2.6 copy-start.13
  489.1 2.5 copy-start.11
  491.6 2.5 copy-start.20
  491.6 2.5 copy-start.24
  530.9 3.1 copy-start.15
  534.0 3.0 copy-start.14
  534.0 3.0 copy-start.23
  537.0 1.9 copy-start.12
  537.0 2.1 copy-start.22
  538.8 5.4 copy-start.9
  538.8 2.7 copy-start.28
  538.8 4.3 copy-start.25
  540.9 3.4 copy-start.10
  542.3 7.0 %collective-permute-start.4 = (f32[8,128]{1,0:T(8,128)S(1)}, f32[8,128]{1,0:T(8,128)S(1)}, u32[]{:S(2)}, u32[]{:S(2)}) collective-permute-start(f32[8,128]{1,0:T(8,128)S(1)} %fusion.28), channel_id=1, source_target_pairs={{0,8},{8,0},{1,9},{9,1},{2,10},{10,2},{3,11},{11,3},{4,12},{12,4},... | collective-permute-start | bytes 12296 | tf_op jit(solution)/shard_map/ppermute | solution.py:817
  544.3 4.3 copy-start.21
  544.7 23.7 %collective-permute-start.5 = (f32[128,1024]{1,0:T(8,128)S(1)}, f32[128,1024]{1,0:T(8,128)}, u32[]{:S(2)}, u32[]{:S(2)}) collective-permute-start(f32[128,1024]{1,0:T(8,128)S(1)} %bitcast_add_fusion.16), channel_id=1, source_target_pairs={{1,2},{2,4},{3,6},{4,8},{5,10},{6,12},{7,14},{8,1},{9,3},{10,5},{1... | collective-permute-start | bytes 1572872 | tf_op jit(solution)/shard_map/ppermute | solution.py:890
  565.1 4.2 copy-start.19
  565.1 5.1 copy-start.1

commit v6 on v5

--- a/solution.py
+++ b/solution.py
@@ -320,8 +320,7 @@
     init = tuple((jnp.full((1, bq), BIG, jnp.float32), jnp.zeros((1, bq), jnp.float32), jnp.zeros((HEAD_DIM, bq), jnp.float32)) for _ in range(heads))
     full = i * bq // bk
     carry = lax.fori_loop(0, full, lambda j, c: block(j, c, False), init)
-    for d in range(max(1, bq // bk)):
-        carry = block(full + d, carry, True)
+    carry = lax.fori_loop(full, full + bq // bk, lambda j, c: block(j, c, True), carry)
     for h in range(heads):
         m, l, acc = carry[h]
         o = acc / l
@@ -534,7 +533,7 @@
     )(src)
 
 
-def mlp_kernel(u_ref, d_ref, w1_ref, w3_ref, w2_ref, wg, y_ref, yp_ref, dx_ref, dxp_ref, g1_ref, g3_ref, g2_ref, og, ut, send_sem, recv_sem, local_sem):
+def mlp_kernel(own_u, peer_u, own_d, peer_d, w1_ref, w3_ref, w2_ref, wg, y_ref, yp_ref, dx_ref, dxp_ref, g1_ref, g3_ref, g2_ref, og, u_ref, d_ref, ut, send_sem, recv_sem, local_sem):
     j = pl.program_id(0)
     last = pl.num_programs(0) - 1
     here = Spot()
@@ -544,7 +543,7 @@
     jobs = [(og, (c, slice(None), slice(off, off + n)), order) for (off, n), order in zip(col_chunks(wg.shape[1], 3), ORDERS)]
     cube = CubeGather(here, wires, jobs)
     post = wires.copy(og.at[:, :, :, c], og.at[:, :, :, c], here.peer('c'))
-    toks = u_ref.shape[0]
+    toks, mine = u_ref.shape[0], y_ref.shape[0]
 
     @pl.when(j == 0)
     def _():
@@ -554,6 +553,9 @@
         cube.start(0)
         for r in (y_ref, yp_ref, dx_ref, dxp_ref):
             r[...] = jnp.zeros_like(r)
+        for pair, own, peer in ((u_ref, own_u, peer_u), (d_ref, own_d, peer_d)):
+            pair[:mine] = own[...]
+            pair[mine:] = peer[...]
 
         def flip(i, carry):
             part = pl.ds(pl.multiple_of(i * 128, 128), 128)
@@ -587,7 +589,6 @@
     dc = (act * silu).astype(jnp.bfloat16)
     y = jnp.dot(z, w2, preferred_element_type=f32)
     dx = lax.dot_general(da, w1, NT, preferred_element_type=f32) + lax.dot_general(dc, w3, NT, preferred_element_type=f32)
-    mine = y_ref.shape[0]
     y_ref[...] += y[:mine]
     yp_ref[...] += y[mine:]
     dx_ref[...] += dx[:mine]
@@ -602,24 +603,25 @@
         cube.drain()
 
 
-def mlp(u, d, w1, w3, w2, wg, cid, bh=256):
-    toks, dim = u.shape
+def mlp(us, ds, w1, w3, w2, wg, cid, bh=256):
+    mine, dim = us[0].shape
+    toks = mine + mine
     half = w1.shape[1]
     f32 = jnp.float32
     vm = pl.BlockSpec(memory_space=pltpu.VMEM)
     an = pl.BlockSpec(memory_space=pl.ANY)
     return pl.pallas_call(
         mlp_kernel, grid=(half // bh,),
-        in_specs=[vm, vm, pl.BlockSpec((dim, bh), by_cols), pl.BlockSpec((dim, bh), by_cols), pl.BlockSpec((bh, dim), by_rows), vm],
-        out_specs=[pl.BlockSpec((toks // 2, dim), whole)] * 4 + [pl.BlockSpec((dim, bh), by_cols), pl.BlockSpec((dim, bh), by_cols),
+        in_specs=[vm] * 4 + [pl.BlockSpec((dim, bh), by_cols), pl.BlockSpec((dim, bh), by_cols), pl.BlockSpec((bh, dim), by_rows), vm],
+        out_specs=[pl.BlockSpec((mine, dim), whole)] * 4 + [pl.BlockSpec((dim, bh), by_cols), pl.BlockSpec((dim, bh), by_cols),
                    pl.BlockSpec((bh, dim), by_rows), an],
-        out_shape=[jax.ShapeDtypeStruct((toks // 2, dim), f32)] * 4 + [jax.ShapeDtypeStruct((dim, half), f32),
+        out_shape=[jax.ShapeDtypeStruct((mine, dim), f32)] * 4 + [jax.ShapeDtypeStruct((dim, half), f32),
                    jax.ShapeDtypeStruct((dim, half), f32), jax.ShapeDtypeStruct((half, dim), f32),
                    jax.ShapeDtypeStruct((2, 2, 2, 2, *wg.shape), wg.dtype)],
-        scratch_shapes=[pltpu.VMEM((dim, toks), jnp.bfloat16), pltpu.SemaphoreType.DMA((19,)), pltpu.SemaphoreType.DMA((19,)), pltpu.SemaphoreType.DMA],
+        scratch_shapes=[pltpu.VMEM((toks, dim), jnp.bfloat16)] * 2 + [pltpu.VMEM((dim, toks), jnp.bfloat16), pltpu.SemaphoreType.DMA((19,)), pltpu.SemaphoreType.DMA((19,)), pltpu.SemaphoreType.DMA],
         cost_estimate=pl.CostEstimate(flops=18 * toks * dim * half, bytes_accessed=48 << 20, transcendentals=toks * half),
         compiler_params=comm_params(cid, vmem_limit_bytes=58 << 20), name="mlp",
-    )(u, d, w1, w3, w2, wg)
+    )(*us, *ds, w1, w3, w2, wg)
 
 
 def entry_kernel(x_ref, w_ref, meta_ref, pos_ref, xa, wa, ma, pa, send_sem, recv_sem, local_sem):
@@ -863,9 +865,7 @@
     attn_out, _ = regroup(o_own, (), 3, 'regroup_o')
     residual = (tokens.astype(jnp.float32) + dot_on(attn_out, wo)).astype(jnp.bfloat16)
     u_mlp, normed2, inv_rms2 = rms_norm(residual, gain2)
-    u_pair = jnp.concatenate([u_mlp, swap_core(u_mlp)], axis=0)
-    d_pair = jnp.concatenate([d_layer, swap_core(d_layer)], axis=0)
-    y_part, y_peer, d_part, d_peer, g1, g3, g2, wg = mlp(u_pair, d_pair, w1, w3, w2, w_flat, 7)
+    y_part, y_peer, d_part, d_peer, g1, g3, g2, wg = mlp((u_mlp, swap_core(u_mlp)), (d_layer, swap_core(d_layer)), w1, w3, w2, w_flat, 7)
     layer_out = (residual.astype(jnp.float32) + (y_part + swap_core(y_peer))).astype(jnp.bfloat16)
 
     d_umlp = d_part + swap_core(d_peer)

time: 575 us -> 575 us (level)
  transfers between devices with their start and end apart: 6 -> 6, of which waited for: 3 -> 4; matrix products, arithmetic and copies ran while one was open for 3% -> 3% of each run, Pallas kernels for 2% -> 2%
where the time goes in v6:
time: 575 us; the launch traced here: 570 us
  Pallas kernels  462 us (80%)
  other arithmetic  41.6 us (7%)
  matrix products  27.5 us (5%)
  local copies, waits for them, and re-layouts  27.1 us (5%)
  waiting for transfers between devices  6.28 us (1%)
    pallas_call x2, Pallas kernels, regroup(): pl.pallas_call(functools.partial(regroup_kernel, n), in_specs=[an] * (1 +...  107 us
    pallas_call x1, Pallas kernels, flash_fwd(): pl.pallas_call(functools.partial(fwd_kernel, bq, bk), grid=(seq // bq,),...  82.5 us
    pallas_call x1, Pallas kernels, flash_bwd(): pl.pallas_call(functools.partial(bwd_kernel, bq, bk), grid=(seq // bk,),...  76.3 us
    pallas_call x1, Pallas kernels, entry(): pl.pallas_call(entry_kernel, in_specs=[vm] * 4, out_specs=[an] * 4, out_s...  49.8 us
    pallas_call x1, Pallas kernels, mlp(): pl.pallas_call(mlp_kernel, grid=(half // bh,), in_specs=[vm] * 4 + [pl.Bl...  46.5 us
    pallas_call x1, Pallas kernels, gather_dh(): pl.pallas_call(dh_kernel, in_specs=[pl.BlockSpec(memory_space=pltpu.VMEM)...  40.5 us
    pallas_call x1, Pallas kernels, back_project(): pl.pallas_call(back_kernel, grid=(dim // bn,), in_specs=[vm, pl.BlockSpec...  35.7 us
    add x8, other arithmetic, total(): out = out + t  21.2 us
  transfers between devices with their start and end apart: 6, of which 4 were waited for; matrix products, arithmetic and copies ran while one was open for 3% of the time, Pallas kernels for 2%

profile of v6, /device:TPU:0, one launch (start us, length us, event | category | flops | bytes accessed | tf_op | source)
XLA Modules:
  0.0 570.3 jit_solution(622933785766668426)
XLA Ops:
  0.7 1.0 bitcast_dynamic-update-slice_fusion
  1.8 1.0 bitcast_dynamic-update-slice_fusion.1
  2.7 1.3 fusion.23.meta_ref
  4.1 49.8 %entry.1 = (bf16[8,512,1024]{2,1,0:T(8,128)(2,1)}, bf16[2,8,64,512]{3,2,1,0:T(8,128)(2,1)}, bf16[2,8,16,128]{3,2,1,0:T(8,128)(2,1)}, s32[8,4,128]{2,1,0:T(4,128)}) custom-call(bf16[512,1024]{1,0:T(8,128)(2,1)} %bitcast.177, bf16[8,64,512]{2,1,0:T(8,128)(2,1)} %bitcast.173, bf16[16,128]{1,0:T(8,128)(2,1)} %fusion.23.meta_ref, s32[4,128]{1,0:T(4,128)} %bitcast.192), custom_call_target="tpu_custom_call" | custom-call | flops 4499999744 | bytes 1048576 | tf_op jit(solution)/shard_map/entry/pallas_call | solution.py:667
  57.1 1.2 reshape.284.w1
  59.0 1.2 reshape.286.w3
  60.1 5.3 multiply_sine_fusion
  66.1 14.4 %project.1 = (bf16[4096,1024]{1,0:T(8,128)(2,1)}, bf16[4096,256]{1,0:T(8,128)(2,1)}, bf16[4096,128]{1,0:T(8,128)(2,1)}, bf16[4096,128]{1,0:T(8,128)(2,1)}, bf16[...) custom-call(bf16[4096,1024]{1,0:T(8,128)(2,1)} %bitcast.193, bf16[16,1024]{1,0:T(8,128)(2,1)} %broadcast_in_dim.11.g_ref.gain_ref, ...), custom_call_target="tpu_custom_call" | custom-call | flops 4294967296 | bytes 33554432 | tf_op jit(solution)/shard_map/project/pallas_call | solution.py:262
  80.4 82.5 %flash_fwd.1 = (bf16[4096,256]{1,0:T(8,128)(2,1)}, bf16[256,4096]{1,0:T(8,128)(2,1)}, f32[2,4096]{1,0:T(2,128)}, bf16[2,2,2,2,64,1536]{5,4,3,2,1,0:T(8,128)(2,1)...) custom-call(bf16[4096,256]{1,0:T(8,128)(2,1)} %get-tuple-element.59., ...), custom_call_target="tpu_custom_call" | custom-call | flops 17179869184 | bytes 8388608 | tf_op jit(solution)/shard_map/flash_fwd/pallas_call | solution.py:342
  162.9 24.8 %regroup_o.1 = bf16[512,2048]{1,0:T(8,128)(2,1)} custom-call(bf16[4096,256]{1,0:T(8,128)(2,1)} %get-tuple-element.62.refs_0_.o_ref), custom_call_target="tpu_custom_call" | custom-call | flops 2500000000 | bytes 1048576 | tf_op jit(solution)/shard_map/regroup_o/pallas_call | solution.py:709
  187.8 5.3 fusion.10
  193.5 0.9 collective-permute-start
  195.2 0.8 copy.42
  196.7 1.5 collective-permute-done.1.peer_d
  198.2 1.0 copy-done.31
  199.2 46.5 %mlp.1 = (f32[512,1024]{1,0:T(8,128)}, f32[512,1024]{1,0:T(8,128)}, f32[512,1024]{1,0:T(8,128)}, f32[512,1024]{1,0:T(8,128)}, f32[1024,1536]{1,0:T(8,128)}, /*in...) custom-call(bf16[512,1024]{1,0:T(8,128)(2,1)} %copy-done.19, ...), custom_call_target="tpu_custom_call" | custom-call | flops 28991029248 | bytes 50331648 | tf_op jit(solution)/shard_map/mlp/pallas_call | solution.py:613
  246.3 3.6 collective-permute-done.3
  249.9 2.5 fusion.9
  253.1 4.5 fusion.29
  257.5 40.5 %gather_dh.1 = bf16[8,512,1024]{2,1,0:T(8,128)(2,1)} custom-call(bf16[512,1024]{1,0:T(8,128)(2,1)} %get-tuple-element.101.src), custom_call_target="tpu_custom_call" | custom-call | flops 4000000000 | bytes 1048576 | tf_op jit(solution)/shard_map/gather_dh/pallas_call | solution.py:528
  298.1 6.8 %fusion.33.refs_5_ = f32[2,128,1024]{2,1,0:T(8,128)} fusion(bf16[2,128,4096]{2,1,0:T(8,128)(2,1)S(1)} %bitcast.201, bf16[4096,1024,1]{1,0,2:T(8,128)(2,1)} %bitcast.194), kind=kOutput, calls=%fused_computation.87 | convolution fusion | flops 2147483648 | bytes 11534336 | tf_op jit(solution)/shard_map/dot_general | solution.py:811
  304.9 4.8 convolution_convert_fusion.d_ref
  309.7 76.3 %flash_bwd.1 = (bf16[4096,512]{1,0:T(8,128)(2,1)}, f32[2,2,128,1536]{3,2,1,0:T(8,128)}, f32[2,2,128,1536]{3,2,1,0:T(8,128)}, f32[2,2,192,1024]{3,2,1,0:T(8,128)}) custom-call(bf16[4096,256]{1,0:T(8,128)(2,1)} %get-tuple-element.59.q_ref, bf16[4096,256]{1,0:T(8,128)(2,1)} %get-tuple-element.62.refs_0_.o_ref, bf16[4096,256]{1,0:T(8,128)(2,1)} %convolution_convert_fusion.d_ref, ...), custom_call_target="tpu_custom_call" | custom-call | flops 21474836480 | bytes 16777216 | tf_op jit(solution)/shard_map/flash_bwd/pallas_call | solution.py:441
  386.1 10.5 %fusion.32 = f32[1024,512]{1,0:T(8,128)} fusion(bf16[4096,1024]{1,0:T(8,128)(2,1)} %get-tuple-element.81, bf16[4096,512]{1,0:T(8,128)(2,1)} %get-tuple-element.77.refs_0_), kind=kOutput, calls=%fused_computation.86 | convolution fusion | flops 4294967296 | bytes 14680064 | tf_op jit(solution)/shard_map/dot_general | solution.py:803
  396.6 3.0 bitcast_add_fusion.refs_3_
  399.6 4.1 bitcast_add_fusion.1
  403.7 82.7 %regroup_dqkv.1 = (bf16[512,4096]{1,0:T(8,128)(2,1)}, f32[2,128,1536]{2,1,0:T(8,128)}, f32[2,128,1536]{2,1,0:T(8,128)}, f32[2,192,1024]{2,1,0:T(8,128)}, f32[512,512]{1,0:T(8,128)}, /*index=5*/f32[128,1024]{1,0:T(8,128)}) custom-call(bf16[4096,512]{1,0:T(8,128)(2,1)} %get-tuple-element.77.refs_0_, f32[2,128,1536]{2,1,0:T(8,128)} %get-tuple-element.117.refs_1_, ...), custom_call_target="tpu_custom_call" | custom-call | flops 7000000000 | bytes 1048576 | tf_op jit(solution)/shard_map/regroup_dqkv/pallas_call | solution.py:709
  486.4 2.5 bitcast_add_fusion.10.g2
  488.9 2.5 bitcast_add_fusion.12.g3
  491.4 2.5 bitcast_add_fusion.14.g1
  493.9 1.2 bitcast_add_fusion.3
  495.1 35.7 %back_project.1 = (bf16[512,1024]{1,0:T(8,128)(2,1)}, f32[1,1024]{1,0:T(1,128)}, f32[8,64,512]{2,1,0:T(8,128)}, f32[128,1536]{1,0:T(8,128)}, f32[128,1536]{1,0:T(8,128)}, /*index=5*/f32[192,1024]{1,0:T(8,128)}) custom-call(bf16[512,4096]{1,0:T(8,128)(2,1)} %get-tuple-element.83.t_ref, bf16[1024,4096]{1,0:T(8,128)(2,1)} %bitcast.153, ...), custom_call_target="tpu_custom_call" | custom-call | flops 3500000000 | bytes 1048576 | tf_op jit(solution)/shard_map/back_project/pallas_call | solution.py:765
  530.8 1.2 slice_bitcast_fusion
  532.0 1.9 slice_bitcast_fusion.1
  533.9 2.9 fusion.13
  536.9 1.8 fusion.14
  538.9 1.8 fusion.15
  543.0 1.1 bitcast_add_fusion.16
  544.5 1.5 collective-permute-start.5
  546.0 0.8 copy.43
  546.8 1.7 copy.55
  549.9 8.8 %last_exchange.1 = (f32[8,8,128]{2,1,0:T(8,128)}, f32[64,1536]{1,0:T(8,128)}, f32[64,1536]{1,0:T(8,128)}) custom-call(f32[8,8,128]{2,1,0:T(8,128)} %broadcast_in_dim.14.b, f32[2,64,1536]{2,1,0:T(8,128)} %bitcast.160, f32[2,64,1536]{2,1,0:T(8,128)} %bitcast.158), custom_call_target="tpu_custom_call" | custom-call | flops 500000000 | bytes 1048576 | tf_op jit(solution)/shard_map/last_exchange/pallas_call | solution.py:794
  558.7 1.1 reshape.310
  559.9 1.2 reshape.307
  562.1 1.9 reshape.311
  565.0 1.9 reshape.308
  568.3 0.9 broadcast_select_fusion.4
  569.1 1.0 copy.60
  (110 shorter events, 15.2 us)
Async XLA Ops:
  0.6 1.0 copy-start
  2.7 1.4 copy-start.14
  4.1 52.2 %copy-start.27 = (bf16[64,3072]{1,0:T(8,128)(2,1)S(1)}, bf16[64,3072]{1,0:T(8,128)(2,1)}, u32[]{:S(2)}) copy-start(bf16[64,3072]{1,0:T(8,128)(2,1)} %param.21) | copy-start | bytes 1179652
  53.9 4.4 copy-start.28
  162.9 24.8 %copy-start.18 = (bf16[1,512,1024]{2,1,0:T(8,128)(2,1)S(1)}, bf16[1,512,1024]{2,1,0:T(8,128)(2,1)}, u32[]{:S(2)}) copy-start(bf16[1,512,1024]{2,1,0:T(8,128)(2,1)} %param.12) | copy-start | bytes 3145732
  193.1 1.4 copy-start.16
  193.1 2.1 copy-start.15
  193.5 5.7 %copy-start.19 = (bf16[512,1024]{1,0:T(8,128)(2,1)}, bf16[512,1024]{1,0:T(8,128)(2,1)S(1)}, u32[]{:S(2)}) copy-start(bf16[512,1024]{1,0:T(8,128)(2,1)S(1)} %fusion.4.own_u) | copy-start | bytes 3145732
  193.5 3.2 collective-permute-start
  194.5 3.8 collective-permute-start.1
  196.7 2.5 copy-start.30
  198.2 1.0 copy-start.31
  245.7 4.2 collective-permute-start.3
  246.1 6.8 %collective-permute-start.2 = (f32[512,1024]{1,0:T(8,128)}, f32[512,1024]{1,0:T(8,128)}, u32[]{:S(2)}, u32[]{:S(2)}) collective-permute-start(f32[512,1024]{1,0:T(8,128)} %get-tuple-element.68), channel_id=1, source_target_pairs={{0,1},{1,0},{2,3},{3,2},{4,5},{5,4},{6,7},{7,6},{8,9},{9,8},{10,11... | collective-permute-start | bytes 6291464 | tf_op jit(solution)/shard_map/ppermute | solution.py:815
  249.9 2.9 copy-start.2
  249.9 2.9 copy-start.6
  249.9 3.1 copy-start.17
  257.5 40.5 %copy-start.33 = (bf16[256,4096]{1,0:T(8,128)(2,1)S(1)}, bf16[256,4096]{1,0:T(8,128)(2,1)}, u32[]{:S(2)}) copy-start(bf16[256,4096]{1,0:T(8,128)(2,1)} %get-tuple-element.82) | copy-start | bytes 6291460
  298.1 6.8 %copy-start.32 = (bf16[8,512,1024]{2,1,0:T(8,128)(2,1)S(1)}, bf16[8,512,1024]{2,1,0:T(8,128)(2,1)}, u32[]{:S(2)}) copy-start(bf16[8,512,1024]{2,1,0:T(8,128)(2,1)} %gather_dh.1) | copy-start | bytes 25165828
  386.0 10.6 %copy-start.3 = (f32[2,2,192,1024]{3,2,1,0:T(8,128)S(1)}, f32[2,2,192,1024]{3,2,1,0:T(8,128)}, u32[]{:S(2)}) copy-start(f32[2,2,192,1024]{3,2,1,0:T(8,128)} %get-tuple-element.80) | copy-start | bytes 9437188
  386.0 13.5 %copy-start.5 = (f32[2,2,128,1536]{3,2,1,0:T(8,128)S(1)}, f32[2,2,128,1536]{3,2,1,0:T(8,128)}, u32[]{:S(2)}) copy-start(f32[2,2,128,1536]{3,2,1,0:T(8,128)} %get-tuple-element.79) | copy-start | bytes 9437188
  396.6 3.0 copy-start.4
  486.3 2.6 copy-start.11
  488.9 2.5 copy-start.9
  491.4 2.5 copy-start.21
  491.4 2.5 copy-start.25
  530.8 3.1 copy-start.13
  533.9 3.0 copy-start.12
  533.9 3.0 copy-start.24
  536.9 1.9 copy-start.10
  536.9 2.1 copy-start.23
  538.7 5.4 copy-start.7
  538.7 2.7 copy-start.29
  538.7 4.3 copy-start.26
  540.8 3.4 copy-start.8
  542.2 7.0 %collective-permute-start.4 = (f32[8,128]{1,0:T(8,128)S(1)}, f32[8,128]{1,0:T(8,128)S(1)}, u32[]{:S(2)}, u32[]{:S(2)}) collective-permute-start(f32[8,128]{1,0:T(8,128)S(1)} %fusion.28), channel_id=1, source_target_pairs={{0,8},{8,0},{1,9},{9,1},{2,10},{10,2},{3,11},{11,3},{4,12},{12,4},... | collective-permute-start | bytes 12296 | tf_op jit(solution)/shard_map/ppermute | solution.py:819
  544.2 4.3 copy-start.22
  544.5 23.7 %collective-permute-start.5 = (f32[128,1024]{1,0:T(8,128)S(1)}, f32[128,1024]{1,0:T(8,128)}, u32[]{:S(2)}, u32[]{:S(2)}) collective-permute-start(f32[128,1024]{1,0:T(8,128)S(1)} %bitcast_add_fusion.16), channel_id=1, source_target_pairs={{1,2},{2,4},{3,6},{4,8},{5,10},{6,12},{7,14},{8,1},{9,3},{10,5},{1... | collective-permute-start | bytes 1572872 | tf_op jit(solution)/shard_map/ppermute | solution.py:890
  564.9 4.2 copy-start.20
  564.9 5.1 copy-start.1
